TPU v7x, 32 devices: a whole 2x2x4 slice. The times are simulated.
32 devices in a mesh: dp: 8 (over z, x), tensor: 4 (over y, core).
Axes of the slice: x: 2, y: 2, z: 4, core: 2. Of those that a mesh axis runs over, the one named last changes fastest.
Arguments:
- block_input: bfloat16 [24576, 1024], P('dp'), may hold values from -6 to 6
- pre_gain: float32 [1024], replicated, may hold values from 0.25 to 1.75
- w_zx: bfloat16 [1024, 2, 2048], P(None, None, 'tensor'), may hold values from -0.1875 to 0.1875
- w_bc: bfloat16 [1024, 256], replicated, may hold values from -0.1875 to 0.1875
- w_dt: bfloat16 [1024, 32], P(None, 'tensor'), may hold values from -0.1875 to 0.1875
- conv_x_w: float32 [4, 2048], P(None, 'tensor'), may hold values from -3 to 3
- conv_x_b: float32 [2048], P('tensor'), may hold values from -3 to 3
- conv_bc_w: float32 [4, 256], replicated, may hold values from -3 to 3
- conv_bc_b: float32 [256], replicated, may hold values from -3 to 3
- dt_bias: float32 [32], P('tensor'), may hold values from -5 to -1
- a_log: float32 [32], P('tensor'), may hold values from -1.5 to 2.5
- d_skip: float32 [32], P('tensor'), may hold values from 0.5 to 2
- gate_gain: float32 [2048], P('tensor'), may hold values from 0.25 to 1.75
- w_out: bfloat16 [2048, 1024], P('tensor'), may hold values from -0.125 to 0.125
- out_grad: bfloat16 [24576, 1024], P('dp'), may hold values from -6 to 6
Outputs:
- block_output: bfloat16 [24576, 1024], P('dp')
- grad_input: float32 [24576, 1024], P('dp')
- grad_pre_gain: float32 [1024], replicated
- grad_w_zx: float32 [1024, 2, 2048], P(None, None, 'tensor')
- grad_w_bc: float32 [1024, 256], replicated
- grad_w_dt: float32 [1024, 32], P(None, 'tensor')
- grad_conv_x_w: float32 [4, 2048], P(None, 'tensor')
- grad_conv_x_b: float32 [2048], P('tensor')
- grad_conv_bc_w: float32 [4, 256], replicated
- grad_conv_bc_b: float32 [256], replicated
- grad_dt_bias: float32 [32], P('tensor')
- grad_a_log: float32 [32], P('tensor')
- grad_d_skip: float32 [32], P('tensor')
- grad_gate_gain: float32 [2048], P('tensor')
- grad_w_out: float32 [2048, 1024], P('tensor')
All inputs are finite; a program needn't handle non-finite values.
Results may differ from a plain program's by a relative error of at most 0.023.
Values may be sent and summed in bfloat16 or wider, within the bound.
A program may use at most 320 MiB of HBM per device.

v0:
```python
from functools import partial

import jax
import jax.numpy as jnp
from jax import lax
from jax.sharding import PartitionSpec as P

INNER = 2048
SPAN = 256
SEQ_LEN = 512


epsilon = 1e-05
precise = lax.Precision.HIGHEST


def causal_conv(sequence, kernel_w, kernel_b):
    tap_count = kernel_w.shape[0]
    length = sequence.shape[1]
    padded = jnp.pad(sequence, ((0, 0), (tap_count - 1, 0), (0, 0)))
    summed = jnp.zeros(sequence.shape, jnp.float32) + kernel_b
    for offset in range(tap_count):
        summed = summed + padded[:, offset : offset + length, :] * kernel_w[offset]
    return summed


def bc_convolve(bc_linear, kernel_w, kernel_b):
    return jax.nn.silu(causal_conv(bc_linear, kernel_w, kernel_b))


def ssd_scan(values, dt_values, a_rates, b_proj, c_proj, block_len):
    seq_count, length, head_count, head_width = values.shape
    span_count = length // block_len
    state_width = b_proj.shape[-1]
    weighted = (values * dt_values[..., None]).reshape(
        seq_count, span_count, block_len, head_count, head_width
    )
    cumulative = jnp.cumsum(
        jnp.transpose(
            (dt_values * a_rates).reshape(seq_count, span_count, block_len, head_count),
            (0, 1, 3, 2),
        ),
        axis=-1,
    )
    b_blocks = b_proj.reshape(seq_count, span_count, block_len, state_width)
    c_blocks = c_proj.reshape(seq_count, span_count, block_len, state_width)
    intersection = jnp.einsum("scin,scjn->scij", c_blocks, b_blocks, precision=precise)
    differences = cumulative[..., :, None] - cumulative[..., None, :]
    lower_mask = jnp.tril(jnp.ones((block_len, block_len), bool))
    decays = jnp.exp(jnp.where(lower_mask, differences, -jnp.inf))
    kernel_mat = decays * intersection[:, :, None]
    y_within = jnp.einsum("schij,scjhp->scihp", kernel_mat, weighted, precision=precise)
    final_cum = cumulative[..., -1:]
    state_decay = jnp.exp(final_cum - cumulative)
    block_states = jnp.einsum(
        "scjn,schj,scjhp->schpn", b_blocks, state_decay, weighted, precision=precise
    )
    block_decay = jnp.exp(cumulative[..., -1])
    running = jnp.zeros((seq_count, head_count, head_width, state_width), jnp.float32)
    entering = []
    for number in range(span_count):
        entering.append(running)
        running = running * block_decay[:, number, :, None, None] + block_states[:, number]
    prior_states = jnp.stack(entering, axis=1)
    y_across = jnp.einsum(
        "scin,schpn,schi->scihp", c_blocks, prior_states, jnp.exp(cumulative), precision=precise
    )
    return (y_within + y_across).reshape(seq_count, length, head_count, head_width)


def mixer(
    block_len,
    z_linear,
    x_linear,
    dt_linear,
    bc_active,
    conv_weight,
    conv_bias,
    dt_bias,
    a_log,
    d_skip,
):
    seq_count, length, channels = x_linear.shape
    x_active = jax.nn.silu(causal_conv(x_linear, conv_weight, conv_bias))
    dt_values = jax.nn.softplus(dt_linear + dt_bias)
    a_rates = -jnp.exp(a_log)
    head_count = dt_values.shape[-1]
    state_width = bc_active.shape[-1] // 2
    values = x_active.reshape(seq_count, length, head_count, channels // head_count)
    scanned = ssd_scan(
        values,
        dt_values,
        a_rates,
        bc_active[..., :state_width],
        bc_active[..., state_width:],
        block_len,
    )
    scanned = scanned + values * d_skip[:, None]
    return scanned.reshape(seq_count, length, channels) * jax.nn.silu(z_linear)


def cross_rows(left, right):
    return lax.dot_general(
        left, right, (((0,), (0,)), ((), ())), preferred_element_type=jnp.float32
    )


def cross_cols(left, right):
    return lax.dot_general(
        left, right, (((1,), (1,)), ((), ())), preferred_element_type=jnp.float32
    )


def body(
    block_input,
    pre_gain,
    w_zx,
    w_bc,
    w_dt,
    conv_x_w,
    conv_x_b,
    conv_bc_w,
    conv_bc_b,
    dt_bias,
    a_log,
    d_skip,
    gate_gain,
    w_out,
    out_grad,
):
    tok_rows = block_input.shape[0]
    model_width = block_input.shape[1]
    local_width = w_zx.shape[2]
    seq_count = tok_rows // SEQ_LEN
    input_f32 = block_input.astype(jnp.float32)
    rms_input = lax.rsqrt(jnp.mean(input_f32 * input_f32, axis=1, keepdims=True) + epsilon)
    normed = input_f32 * rms_input
    hidden = (normed * pre_gain).astype(jnp.bfloat16)
    w_zx_flat = w_zx.reshape(model_width, 2 * local_width)
    zx_linear = jnp.dot(hidden, w_zx_flat, preferred_element_type=jnp.float32)
    bc_linear = jnp.dot(hidden, w_bc, preferred_element_type=jnp.float32)
    dt_linear = jnp.dot(hidden, w_dt, preferred_element_type=jnp.float32)

    def to_seqs(matrix):
        return matrix.reshape(seq_count, SEQ_LEN, matrix.shape[-1])

    bc_active, bc_back = jax.vjp(bc_convolve, to_seqs(bc_linear), conv_bc_w, conv_bc_b)
    gated_seq, mixer_back = jax.vjp(
        partial(mixer, SPAN),
        to_seqs(zx_linear[:, :local_width]),
        to_seqs(zx_linear[:, local_width:]),
        to_seqs(dt_linear),
        bc_active,
        conv_x_w,
        conv_x_b,
        dt_bias,
        a_log,
        d_skip,
    )
    gated = gated_seq.reshape(tok_rows, local_width)
    squares_sum = lax.psum(jnp.sum(gated * gated, axis=1, keepdims=True), "tensor")
    rms_gate = lax.rsqrt(squares_sum / INNER + epsilon)
    quantized = (gated * gate_gain).astype(jnp.bfloat16)
    partial_out = jnp.dot(quantized, w_out, preferred_element_type=jnp.float32)
    projected = lax.psum(partial_out.astype(jnp.bfloat16), "tensor").astype(jnp.float32)
    block_output = (input_f32 + rms_gate * projected).astype(jnp.bfloat16)
    grad_f32 = out_grad.astype(jnp.float32)
    scaled = (rms_gate * grad_f32).astype(jnp.bfloat16)
    grad_w_out = cross_rows(quantized, scaled)
    d_quant = cross_cols(scaled, w_out)
    grad_gate_gain = jnp.sum(d_quant * gated, axis=0)
    row_dots = lax.psum(jnp.sum(d_quant * gated * gate_gain, axis=1, keepdims=True), "tensor")
    d_gated = d_quant * gate_gain - rms_gate * rms_gate * gated * (row_dots / INNER)
    (
        d_z,
        d_x,
        d_dt,
        d_bc_active,
        grad_conv_x_w,
        grad_conv_x_b,
        grad_dt_bias,
        grad_a_log,
        grad_d_skip,
    ) = mixer_back(d_gated.reshape(gated_seq.shape))
    d_bc_linear, grad_conv_bc_w, grad_conv_bc_b = bc_back(d_bc_active)
    d_zx = jnp.concatenate(
        [d_z.reshape(tok_rows, local_width), d_x.reshape(tok_rows, local_width)], axis=1
    ).astype(jnp.bfloat16)
    d_dt_low = d_dt.reshape(tok_rows, -1).astype(jnp.bfloat16)
    grad_w_zx = cross_rows(hidden, d_zx).reshape(w_zx.shape)
    grad_w_dt = cross_rows(hidden, d_dt_low)
    dh_part = cross_cols(d_zx, w_zx_flat) + cross_cols(d_dt_low, w_dt)
    bc_part = d_bc_linear.reshape(tok_rows, -1)
    share = tok_rows // lax.axis_size("tensor")
    start = lax.axis_index("tensor") * share
    hidden_share = lax.dynamic_slice_in_dim(hidden, start, share, 0)
    normed_share = lax.dynamic_slice_in_dim(normed, start, share, 0)
    dh_sum, bc_sum = (
        lax.psum(dh_part.astype(jnp.bfloat16), "tensor").astype(jnp.float32),
        lax.psum(bc_part.astype(jnp.bfloat16), "tensor").astype(jnp.float32),
    )
    bc_low = bc_sum.astype(jnp.bfloat16)
    d_hidden = dh_sum + cross_cols(bc_low, w_bc)
    d_normed = d_hidden * pre_gain
    grad_input = grad_f32 + rms_input * (
        d_normed - normed * jnp.mean(d_normed * normed, axis=1, keepdims=True)
    )
    bc_share = lax.dynamic_slice_in_dim(bc_low, start, share, 0)
    dh_share = lax.dynamic_slice_in_dim(d_hidden, start, share, 0)
    grad_w_bc_part = cross_rows(hidden_share, bc_share)
    grad_pre_part = jnp.sum(dh_share * normed_share, axis=0)
    head_sums = (
        lax.psum(grad_w_zx.astype(jnp.bfloat16), "dp").astype(jnp.float32),
        lax.psum(grad_w_dt.astype(jnp.bfloat16), "dp").astype(jnp.float32),
        lax.psum(grad_conv_x_w.astype(jnp.bfloat16), "dp").astype(jnp.float32),
        lax.psum(grad_conv_x_b.astype(jnp.bfloat16), "dp").astype(jnp.float32),
        lax.psum(grad_dt_bias.astype(jnp.bfloat16), "dp").astype(jnp.float32),
        lax.psum(grad_a_log.astype(jnp.bfloat16), "dp").astype(jnp.float32),
        lax.psum(grad_d_skip.astype(jnp.bfloat16), "dp").astype(jnp.float32),
        lax.psum(grad_gate_gain.astype(jnp.bfloat16), "dp").astype(jnp.float32),
        lax.psum(grad_w_out.astype(jnp.bfloat16), "dp").astype(jnp.float32),
    )
    shared_sums = lax.psum(
        (grad_pre_part, grad_w_bc_part, grad_conv_bc_w, grad_conv_bc_b), ("dp", "tensor")
    )
    return (
        block_output,
        grad_input,
        shared_sums[0],
        head_sums[0],
        shared_sums[1],
        head_sums[1],
        head_sums[2],
        head_sums[3],
        shared_sums[2],
        shared_sums[3],
        head_sums[4],
        head_sums[5],
        head_sums[6],
        head_sums[7],
        head_sums[8],
    )


def solution(mesh):
    placed = (
        P("dp", None),
        P(),
        P(None, None, "tensor"),
        P(),
        P(None, "tensor"),
        P(None, "tensor"),
        P("tensor"),
        P(),
        P(),
        P("tensor"),
        P("tensor"),
        P("tensor"),
        P("tensor"),
        P("tensor", None),
        P("dp", None),
    )
    return jax.shard_map(
        body,
        mesh=mesh,
        in_specs=placed,
        out_specs=(
            P("dp", None),
            P("dp", None),
            P(),
            P(None, None, "tensor"),
            P(),
            P(None, "tensor"),
            P(None, "tensor"),
            P("tensor"),
            P(),
            P(),
            P("tensor"),
            P("tensor"),
            P("tensor"),
            P("tensor"),
            P("tensor", None),
        ),
        check_vma=False,
    )
```

profile of v0, /device:TPU:0, one launch (start us, length us, event | category | flops | bytes accessed | tf_op | source)
XLA Modules:
  0.0 941.3 jit_solution(8227289039185275452)
XLA Ops:
  11.9 5.1 convert_multiply_fusion
  22.4 6.8 reduce-window.14
  33.0 12.4 %fusion.119 = f32[3072,1024]{1,0:T(8,128)} fusion(bf16[3072,1024]{1,0:T(8,128)(2,1)} %copy-done.2, bf16[1024,1024]{1,0:T(8,128)(2,1)S(1)} %bitcast.215), kind=kOutput, calls=%fused_computation.197 | convolution fusion | flops 6442450944 | bytes 20971520 | tf_op jit(solution)/shard_map/dot_general | solution.py:140
  45.4 10.6 %fusion.115 = (f32[3072,512]{1,0:T(8,128)}, f32[3072,512]{1,0:T(8,128)}) fusion(f32[3072,1024]{1,0:T(8,128)} %fusion.119), kind=kLoop, calls=%fused_computation.193 | loop fusion | bytes 25165824 | tf_op jit(solution)/shard_map/slice | solution.py:151
  55.9 6.6 copy.114
  62.6 14.4 %fusion.39 = (f32[6,512,512]{1,2,0:T(8,128)}, f32[6,512,512]{1,2,0:T(8,128)}) fusion(f32[6,512,512]{1,2,0:T(8,128)} %copy.114, f32[512]{0:T(512)S(1)} %bitcast.233, f32[512]{0:T(512)S(1)} %bitcast.235, f32[512]{0:T(512)S(1)} %bitcast.231, f32[512]{0:T(512)S(1)} %bitcast.229, f32[512]{0:T(512)S(1)} %copy-done.77), kind=kLoop, calls=%fused_computation.79 | loop fusion | flops 18874368 | bytes 18884608 | tf_op jit(solution)/shard_map/jvp(jit(silu))/mul | solution.py:84
  77.1 8.7 reshape.292
  99.9 5.3 fusion.124
  109.6 29.2 %fusion.37 = f32[6,2,256,8,64]{2,4,3,1,0:T(8,128)} fusion(f32[6,2,8,64,256]{4,3,2,1,0:T(8,128)S(1)} %fusion.124, f32[6,2,256,8]{2,3,1,0:T(8,128)S(1)} %get-tuple-element.54, f32[6,2,256,256]{3,2,1,0:T(8,128)S(1)} %fusion.122, f32[6,2,8,256]{3,2,1,0:T(8,128)S(1)} %get-tuple-element.55, pred[256,256]{1,0:T(8,128)(4,1)S(1)} %copy-done.43, ...), kind=kOutput, calls=%fused_computation.62 | convolution fusion | flops 4855431168 | bytes 22380544 | tf_op jit(solution)/shard_map/jvp(schij,scjhp->scihp)/dot_general | solution.py:52
  138.9 11.0 %copy.117 = f32[6,2,256,8,64]{2,1,4,3,0:T(2,128)} copy(f32[6,2,256,8,64]{2,4,3,1,0:T(8,128)} %fusion.37) | data formatting | bytes 12582912 | tf_op jit(solution)/shard_map/jvp()/add | solution.py:68
  149.9 9.0 reshape.299
  158.8 10.3 %reshape.328 = f32[6,2,256,8,64]{4,3,2,1,0:T(8,128)} reshape(f32[3072,512]{1,0:T(8,128)} %get-tuple-element.63) | data formatting | bytes 12582912 | tf_op jit(solution)/shard_map/reshape | solution.py:145
  169.1 6.6 copy.119
  175.8 10.1 %multiply_reduce_fusion.11 = (f32[6,512]{1,0:T(8,128)S(1)}, f32[6,512,512]{1,2,0:T(8,128)}) fusion(f32[6,512,512]{1,2,0:T(8,128)} %copy.119, f32[6,512,512]{1,2,0:T(8,128)} %reshape.299, f32[512]{0:T(512)S(1)} %mul.499, f32[6,512,512]{1,2,0:T(8,128)} %get-tuple-element.57), kind=kLoop, calls=%fused_computation.74 | loop fusion | flops 20444160 | bytes 25180160 | tf_op jit(solution)/shard_map/reduce_sum | solution.py:161
  185.9 6.6 copy.120
  192.5 12.7 %psum.126 = f32[3072,1]{0,1:T(1,128)S(1)} all-reduce(f32[3072,1]{0,1:T(1,128)S(1)} %bitcast.227), channel_id=1, replica_groups=mesh['dp'=8,'tensor'=4] {'tensor'}, use_global_device_ids=true, to_apply=%region_4.5 | all-reduce | flops 3072 | bytes 24576 | tf_op jit(solution)/shard_map/psum | solution.py:161
  205.2 11.7 %fusion.64 = (bf16[512]{0:T(512)(128)(2,1)}, f32[3072]{0:T(1024)S(1)}, f32[3072,512]{1,0:T(8,128)}) fusion(f32[6,512,512]{2,1,0:T(8,128)} %copy.120, f32[512]{0:T(512)S(1)} %copy-done.78, bf16[512,1024]{1,0:T(8,128)(2,1)S(1)} %copy-done, bf16[3072,1024]{1,0:T(8,128)(2,1)} %param.29, f32[3072]{0:T(1024)S(1)} %bitcast.223), kind=kOutput, calls=%fused_computation.123 | convolution fusion | flops 3236950528 | bytes 19950592 | tf_op jit(solution)/shard_map/dot_general | solution.py:109
  216.9 10.1 %psum.128 = f32[3072,1]{0,1:T(1,128)S(1)} all-reduce(f32[3072,1]{0,1:T(1,128)S(1)} %bitcast.239), channel_id=1, replica_groups=mesh['dp'=8,'tensor'=4] {'tensor'}, use_global_device_ids=true, to_apply=%region_7.8 | all-reduce | flops 3072 | bytes 24576 | tf_op jit(solution)/shard_map/psum | solution.py:172
  227.1 7.6 fusion.36
  234.7 10.2 %reshape.327 = f32[6,2,256,8,64]{4,3,2,1,0:T(8,128)} reshape(f32[3072,512]{1,0:T(8,128)} %get-tuple-element.66) | data formatting | bytes 12582912 | tf_op jit(solution)/shard_map/reshape | solution.py:184
  244.9 9.8 %copy.129 = f32[6,2,256,8,64]{2,4,3,1,0:T(8,128)} copy(f32[6,2,256,8,64]{4,3,2,1,0:T(8,128)} %reshape.327) | data formatting | bytes 12582912 | tf_op jit(solution)/shard_map/reshape | solution.py:184
  254.7 9.9 %copy.128 = f32[6,2,256,8,64]{2,4,3,1,0:T(8,128)} copy(f32[6,2,256,8,64]{4,3,2,1,0:T(8,128)} %reshape.328) | data formatting | bytes 12582912 | tf_op jit(solution)/shard_map/reshape | solution.py:145
  264.5 8.9 multiply_reduce_fusion.3
  277.2 5.9 multiply_reduce_fusion.2
  283.2 22.3 %bitcast_add_fusion = f32[6,2,256,8,64]{2,4,3,1,0:T(8,128)} fusion(f32[6,2,256,8,64]{2,4,3,1,0:T(8,128)S(1)} %get-tuple-element.94, f32[6,2,256,8]{2,3,1,0:T(8,128)S(1)} %copy-done.36, f32[6,2,256,256]{3,2,1,0:T(8,128)S(1)} %copy-done.21, f32[6,2,8,256]{3,2,1,0:T(8,128)S(1)} %get-tuple-element.55, pred[256,256]{1,0:T(8,128)(4,1)S(1)} %copy-done.44, ...), kind=kOutput, calls=%fused_computation.47 | convolution fusion | flops 4853858304 | bytes 22282240 | tf_op jit(solution)/shard_map/transpose(jvp(schij,scjhp->scihp))/dot_general | solution.py:52
  305.6 11.0 %copy.130 = f32[6,2,256,8,64]{2,1,4,3,0:T(2,128)} copy(f32[6,2,256,8,64]{2,4,3,1,0:T(8,128)} %bitcast_add_fusion) | data formatting | bytes 12582912 | tf_op jit(solution)/shard_map/transpose(jvp(schij,scjhp->scihp))/add_any | solution.py:52
  316.6 9.0 reshape.306
  325.5 6.6 copy.121
  332.3 24.4 %multiply_reduce_fusion.8 = (f32[512]{0:T(512)}, f32[512]{0:T(512)}, f32[512]{0:T(512)}, f32[512]{0:T(512)}, bf16[512]{0:T(512)(128)(2,1)}, /*index=5*/f32[6,512...) fusion(f32[6,512,512]{1,2,0:T(8,128)} %copy.114, f32[6,512,512]{1,2,0:T(8,128)} %get-tuple-element.57, ...), kind=kLoop, calls=%fused_computation.70 | loop fusion | flops 61338624 | bytes 47297536 | tf_op jit(solution)/shard_map/transpose(jvp())/reduce_sum | solution.py:23
  356.7 6.8 broadcast_multiply_fusion
  363.5 8.4 fusion.25
  381.2 11.7 %fusion.75 = bf16[1024,1024]{0,1:T(8,128)(2,1)} fusion(bf16[3072,1024]{1,0:T(8,128)(2,1)} %copy-done.2, bf16[3072,512]{1,0:T(8,128)(2,1)} %bitcast.207, bf16[3072,512]{1,0:T(8,128)(2,1)} %bitcast.209), kind=kOutput, calls=%fused_computation.126 | convolution fusion | flops 6456082432 | bytes 14680064 | tf_op jit(solution)/shard_map/dot_general | solution.py:103
  392.9 6.5 copy.137
  399.5 8.3 fusion.78
  407.9 37.6 %fusion.6 = (f32[6,2,8,256]{3,2,1,0:T(8,128)S(1)}, f32[6,2,8,256]{3,2,1,0:T(8,128)S(1)}, f32[6,2,256,256]{3,2,1,0:T(8,128)}) fusion(f32[6,2,256,256]{3,2,1,0:T(8,128)} %copy-done.20, f32[6,2,8,256]{3,2,1,0:T(8,128)S(1)} %get-tuple-element.55, pred[256,256]{1,0:T(8,128)(4,1)S(1)} %copy-done.45, f32[6,2,256,8,64]{2,1,4,3,0:T(2,128)} %reshape.292, ...), kind=kOutput, calls=%fused_computation.10 | convolution fusion | flops 4889198592 | bytes 19333120 | tf_op jit(solution)/shard_map/transpose(jvp(schij,scjhp->scihp))/dot_general | solution.py:52
  445.5 13.8 %fusion.42 = f32[6,2,256,128,1]{3,2,4,1,0:T(8,128)} fusion(f32[6,1,8,64,128]{4,3,2,1,0:T(8,128)S(1)} %copy-done.18, f32[6,2,256,8,64]{2,1,4,3,0:T(2,128)} %reshape.292, f32[6,2,256,8]{2,3,1,0:T(8,128)S(1)} %copy-done.37, f32[6,2,256,8]{2,3,1,0:T(8,128)S(1)} %get-tuple-element.80), kind=kOutput, calls=%fused_computation.83 | convolution fusion | flops 2419064832 | bytes 9633792 | tf_op jit(solution)/shard_map/transpose(jvp(scjn,schj,scjhp->schpn))/dot_general | solution.py:55
  459.9 29.7 %reduce-window.16 = f32[6,2,8,2,128]{4,2,3,1,0:T(8,128)S(1)} reduce-window(f32[6,2,8,2,128]{4,2,3,1,0:T(8,128)S(1)} %add_bitcast_fusion, f32[]{:T(128)} %constant.25.clone.1), window={size=1x1x1x1x128 pad=0_0x0_0x0_0x0_0x0_127}, to_apply=%region_12.13 | reduce-window | flops 3121152 | bytes 196612 | tf_op jit(solution)/shard_map/reduce-window.2
  501.7 10.4 %bitcast_add_fusion.2 = f32[6,2,256,128]{3,2,1,0:T(8,128)S(1)} fusion(f32[6,2,256,128]{3,2,1,0:T(8,128)S(1)} %fusion.123, f32[6,1,8,64,128]{4,3,2,1,0:T(8,128)S(1)} %copy-done.12, f32[6,2,256,8,64]{2,4,3,1,0:T(8,128)S(1)} %bitcast.190, f32[6,2,256,8]{2,3,1,0:T(8,128)S(1)} %get-tuple-element.54), kind=kOutput, calls=%fused_computation.128 | convolution fusion | flops 2417885184 | bytes 11108352 | tf_op jit(solution)/shard_map/transpose(jvp(scin,schpn,schi->scihp))/dot_general | solution.py:65
  512.2 5.2 bitcast_add_fusion.1
  524.5 5.4 convolution_convert_fusion
  529.9 7.3 fusion.47
  546.2 37.9 %all-reduce.26 = (bf16[1024,8]{0,1:T(8,128)(2,1)S(1)}, bf16[4,512]{1,0:T(4,128)(2,1)S(1)}, bf16[512]{0:T(512)(128)(2,1)S(1)}, bf16[8]{0:T(256)(128)(2,1)S(1)}, b...) all-reduce(bf16[1024,8]{0,1:T(8,128)(2,1)S(1)} %convolution_convert, ...), channel_id=1, replica_groups=mesh['dp'=8,'tensor'=4] {'dp'}, use_global_device_ids=true, to_apply=%region_23.24 | all-reduce | flops 11288 | bytes 45152 | tf_op jit(solution)/shard_map/psum | solution.py:214
  588.1 5.1 convert_element_type.115
  594.8 193.5 %all-reduce.37.cloned.1.call-done = (bf16[3072,1024]{1,0:T(8,128)(2,1)}, bf16[3072,1024]{1,0:T(8,128)(2,1)}, bf16[3072,256]{1,0:T(8,128)(2,1)}) async-done(((bf16[3072,1024]{1,0:T(8,128)(2,1)}, bf16[3072,1024]{1,0:T(8,128)(2,1)}, bf16[3072,256]{1,0:T(8,128)(2,1)}), (bf16[3072,1024]{1,0:T(8,128)(2,1)}, bf16[3072,1024]{1,0:T(8,128)(2,1)}, bf16[3072,256]{1,0:T(8,128)(2,1)})) %all-reduce.37.cloned.1.call-update) | async-done | bytes 14155792 | tf_op jit(solution)/shard_map/psum | solution.py:165
  788.3 9.9 %multiply_reduce_fusion.1 = (f32[3072]{0:T(1024)S(1)}, f32[3072,1024]{1,0:T(8,128)}) fusion(bf16[3072,1024]{1,0:T(8,128)(2,1)} %param.15, f32[1024]{0:T(1024)S(1)} %copy-done.47, f32[3072]{0:T(1024)S(1)} %copy-done.34, bf16[3072,256]{1,0:T(8,128)(2,1)} %get-tuple-element.46, bf16[1024,256]{1,0:T(8,128)(2,1)S(1)} %copy-done.32, ...), kind=kOutput, calls=%fused_computation.16 | convolution fusion | flops 1632629760 | bytes 27291648 | tf_op jit(solution)/shard_map/dot_general | solution.py:109
  801.3 19.2 %convert_add_fusion.1 = (f32[3072,1024]{1,0:T(8,128)}, bf16[3072,1024]{1,0:T(8,128)(2,1)}) fusion(bf16[3072,1024]{1,0:T(8,128)(2,1)} %param.29, f32[3072,1024]{1,0:T(8,128)} %get-tuple-element.98, bf16[3072,1024]{1,0:T(8,128)(2,1)} %param.15, f32[3072]{0:T(1024)S(1)} %broadcast_multiply_fusion.9, f32[1024]{0:T(1024)S(1)} %copy-done.47, ...), kind=kLoop, calls=%fused_computation.11 | loop fusion | flops 37748736 | bytes 50372608 | tf_op jit(solution)/shard_map/add | solution.py:205
  823.7 39.6 %all-reduce.25 = (f32[1024]{0:T(1024)}, f32[4,256]{1,0:T(4,128)}, f32[256]{0:T(256)}) all-reduce(f32[1024]{0:T(1024)S(1)} %multiply_reduce_fusion.16, f32[4,256]{1,0:T(4,128)S(1)} %pad_add_fusion.6, f32[256]{0:T(256)S(1)} %get-tuple-element.29), channel_id=1, replica_groups=mesh['dp'=8,'tensor'=4] {'dp','tensor'}, use_global_device_ids=true, to_apply=%region_20.21 | all-reduce | flops 2304 | bytes 18432 | tf_op jit(solution)/shard_map/psum | solution.py:223
  863.3 69.0 %all-reduce.33.cloned.1.call-done = f32[1024,256]{1,0:T(8,128)} async-done(((f32[1024,256]{1,0:T(8,128)}), f32[1024,256]{1,0:T(8,128)}) %all-reduce.33.cloned.1.call-update) | async-done | bytes 1048592 | tf_op jit(solution)/shard_map/psum | solution.py:223
  (258 shorter events, 88.1 us)
Async XLA Ops:
  7.2 198.0 %copy-start = (bf16[512,1024]{1,0:T(8,128)(2,1)S(1)}, bf16[512,1024]{1,0:T(8,128)(2,1)}, u32[]{:S(2)}) copy-start(bf16[512,1024]{1,0:T(8,128)(2,1)} %param.28) | copy-start | bytes 3145732
  7.2 580.9 %all-reduce.35.cloned.1.call-start = ((), (), s32[]{:S(2)}) async-start(), calls=%async_computation.1 | async-start | bytes 6291456 | tf_op jit(solution)/shard_map/psum | solution.py:213
  11.9 9.7 %copy-start.73 = (f32[8]{0:T(128)}, f32[8]{0:T(128)S(1)}, u32[]{:S(2)}) copy-start(f32[8]{0:T(128)S(1)} %exponential_negate_fusion) | copy-start | bytes 100
  11.9 7.9 copy-start.41
  17.0 14.1 %copy-start.26 = (bf16[1024,2,512]{2,1,0:T(2,128)(2,1)S(1)}, bf16[1024,2,512]{2,1,0:T(2,128)(2,1)}, u32[]{:S(2)}) copy-start(bf16[1024,2,512]{2,1,0:T(2,128)(2,1)} %param.17) | copy-start | bytes 6291460
  29.8 64.3 %copy-start.35 = (f32[6,2,256,8]{2,3,1,0:T(8,128)}, f32[6,2,256,8]{2,3,1,0:T(8,128)S(1)}, u32[]{:S(2)}) copy-start(f32[6,2,256,8]{2,3,1,0:T(8,128)S(1)} %fusion.101) | copy-start | bytes 294916
  55.9 6.6 copy-start.68
  55.9 6.7 copy-start.77
  62.6 14.5 %copy-start.48 = (f32[1,512]{1,0:T(1,128)}, f32[1,512]{1,0:T(1,128)S(1)}, u32[]{:S(2)}) copy-start(f32[1,512]{1,0:T(1,128)S(1)} %get-tuple-element.85) | copy-start | bytes 6148
  62.6 14.5 %copy-start.50 = (f32[1,512]{1,0:T(1,128)}, f32[1,512]{1,0:T(1,128)S(1)}, u32[]{:S(2)}) copy-start(f32[1,512]{1,0:T(1,128)S(1)} %get-tuple-element.86) | copy-start | bytes 6148
  62.6 14.5 %copy-start.52 = (f32[1,512]{1,0:T(1,128)}, f32[1,512]{1,0:T(1,128)S(1)}, u32[]{:S(2)}) copy-start(f32[1,512]{1,0:T(1,128)S(1)} %get-tuple-element.87) | copy-start | bytes 6148
  77.0 8.7 copy-start.31
  90.6 6.2 slice-start.1
  90.6 6.2 copy-start.57
  94.1 11.2 %copy-start.4 = (f32[6,512,128]{2,1,0:T(8,128)}, f32[6,512,128]{2,1,0:T(8,128)S(1)}, u32[]{:S(2)}) copy-start(f32[6,512,128]{2,1,0:T(8,128)S(1)} %get-tuple-element.78) | copy-start | bytes 4718596
  94.1 11.2 %copy-start.8 = (f32[6,512,128]{2,1,0:T(8,128)}, f32[6,512,128]{2,1,0:T(8,128)S(1)}, u32[]{:S(2)}) copy-start(f32[6,512,128]{2,1,0:T(8,128)S(1)} %get-tuple-element.79) | copy-start | bytes 4718596
  169.1 6.6 copy-start.81
  175.8 10.1 %copy-start.54 = (f32[512]{0:T(512)}, f32[512]{0:T(512)S(1)}, u32[]{:S(2)}) copy-start(f32[512]{0:T(512)S(1)} %mul.499) | copy-start | bytes 6148
  185.9 19.3 %copy-start.78 = (f32[512]{0:T(512)S(1)}, f32[512]{0:T(512)}, u32[]{:S(2)}) copy-start(f32[512]{0:T(512)} %param.27) | copy-start | bytes 6148
  254.7 22.5 %slice-start.2 = ((s8[6291456]{0:T(1024)(128)(4,1)}), s8[2097152]{0:T(1024)(128)(4,1)S(1)}, s32[]{:S(2)}) async-start(s8[6291456]{0:T(1024)(128)(4,1)} %bitcast.185), calls=%async_computation.5 | async-start | bytes 4194304
  264.5 8.9 copy-start.5
  264.5 12.7 %slice-start.3 = ((s8[6291456]{0:T(1024)(128)(4,1)}), s8[4194304]{0:T(1024)(128)(4,1)S(1)}, s32[]{:S(2)}) async-start(s8[6291456]{0:T(1024)(128)(4,1)} %bitcast.185), calls=%async_computation.6 | async-start | bytes 8388608
  273.5 9.7 %copy-start.3 = (f32[6,2,256,8,64]{2,4,3,1,0:T(8,128)}, f32[6,2,256,8,64]{2,4,3,1,0:T(8,128)S(1)}, u32[]{:S(2)}) copy-start(f32[6,2,256,8,64]{2,4,3,1,0:T(8,128)S(1)} %get-tuple-element.51) | copy-start | bytes 18874372
  277.2 6.0 copy-start.17
  277.2 6.0 copy-start.21
  277.2 6.0 copy-start.36
  325.5 6.6 copy-start.25
  325.5 6.6 copy-start.67
  325.5 6.8 copy-start.55
  332.3 24.4 %copy-start.49 = (f32[1,512]{1,0:T(1,128)S(1)}, f32[1,512]{1,0:T(1,128)}, u32[]{:S(2)}) copy-start(f32[1,512]{1,0:T(1,128)} %copy-done.48) | copy-start | bytes 6148
  332.3 24.4 %copy-start.51 = (f32[1,512]{1,0:T(1,128)S(1)}, f32[1,512]{1,0:T(1,128)}, u32[]{:S(2)}) copy-start(f32[1,512]{1,0:T(1,128)} %copy-done.50) | copy-start | bytes 6148
  332.3 24.4 %copy-start.53 = (f32[1,512]{1,0:T(1,128)S(1)}, f32[1,512]{1,0:T(1,128)}, u32[]{:S(2)}) copy-start(f32[1,512]{1,0:T(1,128)} %copy-done.52) | copy-start | bytes 6148
  399.5 8.4 copy-start.45
  407.8 37.7 %copy-start.18 = (f32[6,1,8,64,128]{4,3,2,1,0:T(8,128)S(1)}, f32[6,1,8,64,128]{4,3,2,1,0:T(8,128)}, u32[]{:S(2)}) copy-start(f32[6,1,8,64,128]{4,3,2,1,0:T(8,128)} %copy-done.17) | copy-start | bytes 4718596
  407.8 37.7 %copy-start.37 = (f32[6,2,256,8]{2,3,1,0:T(8,128)S(1)}, f32[6,2,256,8]{2,3,1,0:T(8,128)}, u32[]{:S(2)}) copy-start(f32[6,2,256,8]{2,3,1,0:T(8,128)} %copy-done.35) | copy-start | bytes 294916
  407.8 380.5 %all-reduce.37.cloned.1.call-start = ((), (), s32[]{:S(2)}) async-start(), calls=%async_computation.2 | async-start | bytes 28311552 | tf_op jit(solution)/shard_map/psum | solution.py:165
  445.5 13.8 %copy-start.40 = (f32[6,2,8]{2,1,0:T(2,128)S(1)}, f32[6,2,8]{2,1,0:T(2,128)}, u32[]{:S(2)}) copy-start(f32[6,2,8]{2,1,0:T(2,128)} %copy-done.39) | copy-start | bytes 1156
  445.5 14.1 %copy-start.56 = (f32[6,8]{1,0:T(8,128)S(1)}, f32[6,8]{1,0:T(8,128)}, u32[]{:S(2)}) copy-start(f32[6,8]{1,0:T(8,128)} %get-tuple-element.95) | copy-start | bytes 580
  445.5 14.3 %copy-start.38 = (f32[6,2,8,256]{3,2,1,0:T(8,128)S(1)}, f32[6,2,8,256]{3,2,1,0:T(8,128)}, u32[]{:S(2)}) copy-start(f32[6,2,8,256]{3,2,1,0:T(8,128)} %get-tuple-element.50) | copy-start | bytes 294916
  489.8 11.9 %slice-start.4 = ((s8[6291456]{0:T(1024)(128)(4,1)}), s8[2097152]{0:T(1024)(128)(4,1)S(1)}, s32[]{:S(2)}) async-start(s8[6291456]{0:T(1024)(128)(4,1)} %bitcast.189), calls=%async_computation.7 | async-start | bytes 4194304
  493.6 8.1 slice-start.5
  501.7 10.5 %copy-start.6 = (f32[6,512,128]{2,1,0:T(8,128)S(1)}, f32[6,512,128]{2,1,0:T(8,128)}, u32[]{:S(2)}) copy-start(f32[6,512,128]{2,1,0:T(8,128)} %copy-done.4) | copy-start | bytes 4718596
  501.7 10.5 %copy-start.29 = (f32[6,2,256,128,1]{3,2,4,1,0:T(8,128)S(1)}, f32[6,2,256,128,1]{3,2,4,1,0:T(8,128)}, u32[]{:S(2)}) copy-start(f32[6,2,256,128,1]{3,2,4,1,0:T(8,128)} %fusion.42) | copy-start | bytes 4718596
  529.9 7.3 copy-start.42
  541.8 390.5 %all-reduce.33.cloned.1.call-start = ((), (), s32[]{:S(2)}) async-start(), calls=%async_computation | async-start | bytes 2097152 | tf_op jit(solution)/shard_map/psum | solution.py:223
  546.2 242.2 %copy-start.32 = (bf16[1024,256]{1,0:T(8,128)(2,1)S(1)}, bf16[1024,256]{1,0:T(8,128)(2,1)}, u32[]{:S(2)}) copy-start(bf16[1024,256]{1,0:T(8,128)(2,1)} %param.18) | copy-start | bytes 1572868
  546.2 242.2 %copy-start.34 = (f32[3072]{0:T(1024)S(1)}, f32[3072]{0:T(1024)}, u32[]{:S(2)}) copy-start(f32[3072]{0:T(1024)} %copy-done.33) | copy-start | bytes 36868
  546.2 242.2 %copy-start.47 = (f32[1024]{0:T(1024)S(1)}, f32[1024]{0:T(1024)}, u32[]{:S(2)}) copy-start(f32[1024]{0:T(1024)} %param.16) | copy-start | bytes 12292
  (45 other events, 157.7 us)
Sparse Core Ops, SparseCore 0:
  407.9 129.0 all-reduce.34
  541.9 246.4 all-reduce.36
  801.4 130.8 all-reduce.32
where the time goes:
time: 952 us; the launch traced here: 941 us
  waiting for transfers between devices  263 us (28%)
  matrix products  227 us (24%)
  other arithmetic  176 us (18%)
  local copies, waits for them, and re-layouts  160 us (17%)
  blocking collectives  100 us (11%)
  between operations  15.2 us (2%)
    psum x1, waiting for transfers between devices, body(): lax.psum(partial_out.astype(jnp.bfloat16), 'tensor').astype(jnp.float32)  194 us
    dot_general x3, matrix products, ssd_scan(): jnp.einsum('schij,scjhp->scihp', kernel_mat, weighted, precision=precise)  89.2 us
    psum x1, waiting for transfers between devices, body(): lax.psum((grad_pre_part, grad_w_bc_part, grad_conv_bc_w, grad_conv_bc_b),...  69 us
    another operation x7, other arithmetic  47.2 us
    psum x1, blocking collectives, body(): lax.psum((grad_pre_part, grad_w_bc_part, grad_conv_bc_w, grad_conv_bc_b),...  39.6 us
    psum x1, blocking collectives, body(): lax.psum(grad_w_dt.astype(jnp.bfloat16), 'dp').astype(jnp.float32)  37.9 us
    dot_general x4, matrix products, cross_cols(): lax.dot_general(left, right, (((1,), (1,)), ((), ())), preferred_element_...  33.3 us
    reshape x4, local copies, waits for them, and re-layouts, to_seqs(): return matrix.reshape(seq_count, SEQ_LEN, matrix.shape[-1])  33.3 us
  transfers between devices with their start and end apart: 3, of which 2 were waited for; matrix products, arithmetic and copies ran while one was open for 18% of the time, Pallas kernels for 0%

commit v1 on v0

v1 whole, which is shorter than its diff:
```python
from functools import partial

import jax
import jax.numpy as jnp
from jax import lax
from jax.experimental import pallas as pl
from jax.experimental.pallas import tpu as pltpu
from jax.sharding import PartitionSpec as P

SEQ_LEN = 512
L = 128
HEAD = 64
PAD = 8
epsilon = 1e-05
f32 = jnp.float32
bf16 = jnp.bfloat16
HI = lax.Precision.HIGHEST
MESH = pl.DeviceIdType.MESH


def nn(a, b):
    return lax.dot_general(a, b, (((1,), (0,)), ((), ())), preferred_element_type=f32)


def nt(a, b):
    return lax.dot_general(a, b, (((1,), (1,)), ((), ())), preferred_element_type=f32)


def tn(a, b):
    return lax.dot_general(a, b, (((0,), (0,)), ((), ())), preferred_element_type=f32)


def exact(a, b):
    return lax.dot_general(
        a, b, (((1,), (0,)), ((), ())), precision=HI, preferred_element_type=f32
    )


def sigmoid(v):
    return 0.5 + 0.5 * jnp.tanh(0.5 * v)


def softplus(v):
    u = jnp.exp(-jnp.abs(v))
    return jnp.maximum(v, 0.0) + jnp.where(u < 1e-3, u - 0.5 * u * u, jnp.log(1.0 + u))


def fold_rows(v):
    return jnp.sum(v.reshape(v.shape[0] // 8, 8, v.shape[1]), axis=0)


def lane_iota(shape):
    return lax.broadcasted_iota(jnp.int32, shape, 1)


def row_iota(shape):
    return lax.broadcasted_iota(jnp.int32, shape, 0)


def conv(window, taps, bias):
    total = bias
    for k in range(4):
        total = total + window[PAD - 3 + k : PAD - 3 + k + L] * taps[k : k + 1]
    return total


def spread(cols, head):
    return jnp.broadcast_to(cols[:, head : head + 1], (L, L))


def span_decay(dtl, hp):
    pre = dtl + hp[0:1]
    dt = softplus(pre)
    ltri = (row_iota((L, L)) >= lane_iota((L, L))).astype(f32)
    cum = exact(ltri, dt * hp[1:2])
    return pre, dt, cum, cum.T


def remote(src, dst, send, recv, where):
    return pltpu.make_async_remote_copy(
        src_ref=src,
        dst_ref=dst,
        send_sem=send,
        recv_sem=recv,
        device_id=where,
        device_id_type=MESH,
    )


def greet(peers):
    barrier = pltpu.get_barrier_semaphore()
    for peer in peers:
        pl.semaphore_signal(barrier, inc=1, device_id=peer, device_id_type=MESH)
    pl.semaphore_wait(barrier, len(peers))


def bit_peers(axis, base, first, count):
    me = lax.axis_index(axis)
    peers, bits = [], []
    for k in range(count):
        step = base * 2**k
        bit = lax.rem(me // step, 2)
        peers.append({axis: me + step * (1 - 2 * bit)})
        bits.append(bit)
    return peers, bits


class Halving:
    def __init__(self, links, rows, src, work, recvs, full, sems):
        self.links, self.rows = links, rows
        self.src, self.work, self.recvs, self.full, self.sems = src, work, recvs, full, sems
        self.n = len(links)
        offs, size = [0], rows
        for _, bit in links:
            size //= 2
            offs.append(offs[-1] + bit * size)
        self.offs = offs

    def size(self, k):
        return self.rows >> k

    def at(self, off, size):
        return pl.ds(pl.multiple_of(off, size), size)

    def scatter(self, k):
        peer, bit = self.links[k]
        half = self.size(k + 1)
        off = self.offs[k] + (1 - bit) * half
        if k == 0:
            src = self.src.at[self.at(off, half)]
        else:
            src = self.work.at[self.at(off - self.offs[1], half)]
        return remote(src, self.recvs[k], self.sems.at[0, k], self.sems.at[1, k], peer)

    def fold(self, k):
        self.scatter(k).wait()
        half = self.size(k + 1)
        step = min(half, 64)
        keep = self.offs[k + 1]

        @pl.loop(0, half // step)
        def _(i):
            off = i * step
            rows = pl.ds(pl.multiple_of(off, step), step)
            near = pl.ds(pl.multiple_of(keep - self.offs[1] + off, step), step)
            if k == 0:
                mine = self.src[pl.ds(pl.multiple_of(keep + off, step), step), :]
            else:
                mine = self.work[near, :]
            total = mine.astype(f32) + self.recvs[k][rows, :].astype(f32)
            self.work[near, :] = total.astype(self.work.dtype)

    def own_copy(self):
        last = self.size(self.n)
        return pltpu.make_async_copy(
            self.work.at[self.at(self.offs[self.n] - self.offs[1], last)],
            self.full.at[self.at(self.offs[self.n], last)],
            self.sems.at[0, 2 * self.n],
        )

    def gather(self, k):
        peer, _ = self.links[k]
        rows = self.at(self.offs[k + 1], self.size(k + 1))
        sems = self.sems
        return remote(
            self.full.at[rows],
            self.full.at[rows],
            sems.at[0, self.n + k],
            sems.at[1, self.n + k],
            peer,
        )

    def close(self, j):
        n = self.n
        if 1 <= j <= n:
            self.fold(j - 1)
        elif j > n:
            self.gather(2 * n - j).wait()

    def begin(self, j):
        n = self.n
        if j < n:
            self.scatter(j).start()
            return
        if j == n:
            self.own_copy().start()
            self.own_copy().wait()
        if j < 2 * n:
            self.gather(2 * n - 1 - j).start()

    @staticmethod
    def scratch(rows, cols, n, dtype):
        recvs = [pltpu.VMEM((rows >> (k + 1), cols), dtype) for k in range(n)]
        return [pltpu.VMEM((rows // 2, cols), dtype)] + recvs + [
            pltpu.SemaphoreType.DMA((2, 2 * n + 1))
        ]


class Doubling:
    def __init__(self, peers, acc, recv, sems):
        self.peers, self.acc, self.recv, self.sems = peers, acc, recv, sems

    def copy(self, k):
        return remote(
            self.acc.at[k],
            self.recv.at[k],
            self.sems.at[0, k],
            self.sems.at[1, k],
            self.peers[k],
        )

    def close(self, j):
        if j > 0:
            self.copy(j - 1).wait()
            self.acc[j] = self.acc[j - 1] + self.recv[j - 1]

    def begin(self, j):
        if j < len(self.peers):
            self.copy(j).start()

    @staticmethod
    def scratch(n, rows, cols):
        return [
            pltpu.VMEM((n + 1, rows, cols), f32),
            pltpu.VMEM((n, rows, cols), f32),
            pltpu.SemaphoreType.DMA((2, n)),
        ]


def correction(x, dh, gain):
    v = x.astype(f32)
    r = lax.rsqrt(jnp.mean(v * v, axis=1, keepdims=True) + epsilon)
    normed = v * r
    dn = dh * gain
    return r * (dn - normed * jnp.mean(dn * normed, axis=1, keepdims=True))


def log2(n):
    return n.bit_length() - 1


def forward_kernel(
    width,
    _seq,
    x_ref,
    g_ref,
    gain_ref,
    w_ref,
    wo_ref,
    prm_ref,
    bcp_ref,
    hp_ref,
    hid_ref,
    z_ref,
    xl_ref,
    bcl_ref,
    dtl_ref,
    u_ref,
    y_ref,
    sin_ref,
    st_ref,
    po_ref,
    q_scr,
    bca_scr,
    s_scr,
    cs_scr,
    xs_scr,
):
    rows_all = x_ref.shape[0]
    model = x_ref.shape[1]
    pairs = width // L

    @pl.loop(0, rows_all // 32)
    def _(i):
        rows = pl.ds(pl.multiple_of(i * 32, 32), 32)
        v = x_ref[rows, :].astype(f32)
        r = lax.rsqrt(jnp.mean(v * v, axis=1, keepdims=True) + epsilon)
        hid_ref[rows, :] = (v * r * gain_ref[...]).astype(bf16)

    xl_ref[0:PAD, :] = jnp.zeros((PAD, width), f32)
    bcl_ref[0:PAD, :] = jnp.zeros((PAD, 256), f32)

    @pl.loop(0, width // 256)
    def _(j):
        cols = pl.ds(pl.multiple_of(j * 256, 256), 256)
        z_ref[:, cols] = nn(hid_ref[...], w_ref[:, cols])

    @pl.loop(0, width // 256)
    def _(j):
        cols = pl.ds(pl.multiple_of(j * 256, 256), 256)
        wcols = pl.ds(pl.multiple_of(width + j * 256, 256), 256)
        xl_ref[PAD : PAD + rows_all, cols] = nn(hid_ref[...], w_ref[:, wcols])

    bcl_ref[PAD : PAD + rows_all, :] = nn(hid_ref[...], w_ref[:, 2 * width : 2 * width + 256])
    dtl_ref[...] = nn(hid_ref[...], w_ref[:, 2 * width + 256 : 2 * width + 384])

    @pl.loop(0, width // 256)
    def _(j):
        cols = pl.ds(pl.multiple_of(j * 256, 256), 256)
        u_ref[:, cols] = nt(g_ref[...], wo_ref[cols, :])

    @pl.loop(0, rows_all // L)
    def _(c):
        t0 = pl.multiple_of(c * L, L)
        for half in range(2):
            lanes = slice(half * L, half * L + L)
            v = conv(bcl_ref[pl.ds(t0, L + PAD), lanes], bcp_ref[0:4, lanes], bcp_ref[4:5, lanes])
            bca_scr[pl.ds(t0, L), lanes] = (v * sigmoid(v)).astype(bf16)

    s_scr[...] = jnp.zeros_like(s_scr)
    hp = hp_ref[...]

    @pl.loop(0, rows_all // L)
    def _(c):
        t0 = pl.multiple_of(c * L, L)
        rows = pl.ds(t0, L)
        lo = lane_iota((L, L)) < HEAD
        mlo = (lane_iota((1, L)) < HEAD).astype(bf16)
        mhi = (lane_iota((1, L)) >= HEAD).astype(bf16)
        tri = row_iota((L, L)) >= lane_iota((L, L))
        _, dt, cum, cum_t = span_decay(dtl_ref[rows, :], hp)
        bm = bca_scr[rows, 0:L]
        cm = bca_scr[rows, L : 2 * L]
        both = nt(cm, bm)
        sb = s_scr[...].astype(bf16)
        sin_ref[c] = sb
        cs_scr[...] = nn(cm, sb)
        squares = jnp.zeros((L, L), f32)
        inner = jnp.zeros((L, L), f32)
        for p in range(pairs):
            lanes = slice(p * L, p * L + L)
            xc = conv(xl_ref[pl.ds(t0, L + PAD), lanes], prm_ref[0:4, lanes], prm_ref[4:5, lanes])
            x = xc * sigmoid(xc)
            h0, h1 = 2 * p, 2 * p + 1
            a0, a1 = spread(cum, h0), spread(cum, h1)
            ap = jnp.where(lo, a0, a1)
            k0 = both * jnp.exp(jnp.where(tri, a0 - cum_t[h0 : h0 + 1], -jnp.inf))
            k1 = both * jnp.exp(jnp.where(tri, a1 - cum_t[h1 : h1 + 1], -jnp.inf))
            xdt = x * jnp.where(lo, spread(dt, h0), spread(dt, h1))
            xb = xdt.astype(bf16)
            fin = ap[L - 1 : L]
            within = nn(
                jnp.concatenate([k0.astype(bf16), k1.astype(bf16)], axis=1),
                jnp.concatenate([xb * mlo, xb * mhi], axis=0),
            )
            y = within + jnp.exp(ap) * cs_scr[:, lanes] + prm_ref[5:6, lanes] * x
            xs_scr[:, lanes] = (xdt * jnp.exp(fin - ap)).astype(bf16)
            s_scr[:, lanes] = s_scr[:, lanes] * jnp.exp(fin)
            y_ref[rows, lanes] = y
            z = z_ref[rows, lanes]
            gated = y * (z * sigmoid(z))
            q = gated * prm_ref[6:7, lanes]
            q_scr[rows, lanes] = q.astype(bf16)
            squares = squares + gated * gated
            inner = inner + u_ref[rows, lanes] * q
        s_scr[...] += nn(bm.T, xs_scr[...])
        s0 = jnp.sum(squares, axis=1, keepdims=True)
        s1 = jnp.sum(inner, axis=1, keepdims=True)
        lane = lane_iota((L, L))
        stat = jnp.where(lane == 0, s0, jnp.where(lane == 1, s1, 0.0))
        st_ref[:, rows] = stat.T[0:2]

    @pl.loop(0, model // 256)
    def _(j):
        cols = pl.ds(pl.multiple_of(j * 256, 256), 256)
        po_ref[:, cols] = nn(q_scr[...], wo_ref[:, cols]).astype(bf16)


def gate_kernel(
    width,
    own,
    inner_total,
    ncore,
    ny,
    _seq,
    st_ref,
    g_ref,
    hid_ref,
    z_ref,
    y_ref,
    u_ref,
    prm_ref,
    po_ref,
    x_ref,
    dz_ref,
    dy_ref,
    gz_ref,
    go_ref,
    ggg_ref,
    bo_ref,
    stot_ref,
    q_scr,
    sc_scr,
    acc_scr,
    st_in,
    send_scr,
    recv_scr,
    po_in,
    po_own,
    x_own,
    st_send,
    st_recv,
    core_send,
    core_recv,
    po_send,
    po_recv,
    local,
):
    rows_all = z_ref.shape[0]
    here = pl.program_id(0)
    spot = lax.axis_index("tensor")
    core, yy = lax.rem(spot, ncore), spot // ncore
    ys = [lax.rem(yy + d, ny) for d in range(1, ny)]
    peers = [{"tensor": v * ncore + core} for v in ys]
    twin = {"tensor": spot + 1 - 2 * core}
    nloc, _, Ry, _ = po_ref.shape

    def po_copies():
        return [
            remote(po_ref.at[:, ys[d]], po_in.at[d], po_send.at[d], po_recv.at[d], peers[d])
            for d in range(ny - 1)
        ]

    def own_copies():
        return [
            pltpu.make_async_copy(po_ref.at[:, yy], po_own, local.at[0]),
            pltpu.make_async_copy(x_ref.at[pl.ds(core * nloc, nloc), yy], x_own, local.at[1]),
        ]

    @pl.when(here == 0)
    def _():
        greet(peers + ([twin] if ncore == 2 else []))
        copies = [
            remote(st_ref, st_in.at[d], st_send.at[d], st_recv.at[d], peers[d])
            for d in range(ny - 1)
        ]
        for copy in copies:
            copy.start()
        for copy in copies:
            copy.wait()
        total = st_ref[...]
        for d in range(ny - 1):
            total = total + st_in[d]
        stot_ref[...] = total
        for copy in po_copies() + own_copies():
            copy.start()

    model = g_ref.shape[1]
    pairs = width // L

    @pl.when(pl.program_id(0) == 0)
    def _():
        acc_scr[...] = jnp.zeros_like(acc_scr)
        ggg_ref[...] = jnp.zeros_like(ggg_ref)

    @pl.loop(0, rows_all // L)
    def _(c):
        rows = pl.ds(pl.multiple_of(c * L, L), L)
        st = stot_ref[here, :, rows]
        r_row = lax.rsqrt(st[0:1] / inner_total + epsilon)
        c_row = r_row * r_row * r_row * (st[1:2] / inner_total)
        cols8 = jnp.concatenate([r_row, c_row, jnp.zeros((6, L), f32)], axis=0).T
        r = jnp.broadcast_to(cols8[:, 0:1], (L, L))
        c2 = jnp.broadcast_to(cols8[:, 1:2], (L, L))
        for m in range(model // L):
            lanes = slice(m * L, m * L + L)
            sc_scr[rows, lanes] = (g_ref[rows, lanes].astype(f32) * r).astype(bf16)
        for p in range(pairs):
            lanes = slice(p * L, p * L + L)
            gg = prm_ref[6:7, lanes]
            z = z_ref[rows, lanes]
            y = y_ref[rows, lanes]
            sg = sigmoid(z)
            silz = z * sg
            gated = y * silz
            q_scr[rows, lanes] = (gated * gg).astype(bf16)
            dq = r * u_ref[rows, lanes]
            ggg_ref[:, lanes] += fold_rows(dq * gated)
            dgated = dq * gg - c2 * gated
            dy_ref[rows, lanes] = (dgated * silz).astype(bf16)
            dz_ref[rows, lanes] = (dgated * y * (sg + silz * (1.0 - sg))).astype(bf16)

    @pl.loop(0, model // 256)
    def _(j):
        cols = pl.ds(pl.multiple_of(j * 256, 256), 256)
        acc_scr[cols, 0:width] += tn(hid_ref[:, cols], dz_ref[...])
        acc_scr[cols, width : 2 * width] += tn(sc_scr[:, cols], q_scr[...])

    @pl.when(here == pl.num_programs(0) - 1)
    def _():
        if ncore == 2:
            send_scr[:, 0:own] = acc_scr[:, own:width].astype(bf16)
            send_scr[:, own : 2 * own] = acc_scr[:, width + own : 2 * width].astype(bf16)
            copy = remote(send_scr, recv_scr, core_send, core_recv, twin)
            copy.start()
            copy.wait()
            theirs = recv_scr[...].astype(f32)
        else:
            theirs = jnp.zeros((model, 2 * own), f32)
        gz_ref[...] = (acc_scr[:, 0:own] + theirs[:, 0:own]).astype(bf16)
        mine = acc_scr[:, width : width + own] + theirs[:, own : 2 * own]
        go_ref[...] = mine.astype(bf16)
        for copy in po_copies() + own_copies():
            copy.wait()
        for i in range(nloc):
            for h in range(Ry // L):
                lanes = pl.ds(pl.multiple_of(yy * Ry + h * L, L), L)
                r_row = lax.rsqrt(stot_ref[i, 0:1, lanes] / inner_total + epsilon)
                r = jnp.broadcast_to(r_row, (8, L)).T[:, 0:1]

                @pl.loop(0, model // L)
                def _(m, i=i, h=h, r=r):
                    cols = pl.ds(pl.multiple_of(m * L, L), L)
                    rows = slice(h * L, h * L + L)
                    total = po_own[i, rows, cols].astype(f32)
                    for d in range(ny - 1):
                        total = total + po_in[d, i, rows, cols].astype(f32)
                    bo_ref[i, rows, cols] = (x_own[i, rows, cols].astype(f32) + r * total).astype(bf16)


def scan_kernel(
    width,
    own,
    heads,
    ncore,
    ny,
    ndp,
    nloc_static,
    _seq,
    hid_ref,
    dz_ref,
    dy_ref,
    xl_ref,
    bcl_ref,
    dtl_ref,
    sin_ref,
    w_ref,
    prm_ref,
    bcp_ref,
    hp_ref,
    ggg_ref,
    gain_ref,
    gz_ref,
    go_ref,
    bo_ref,
    x_ref,
    dh_ref,
    gw_ref,
    gbcw_ref,
    small_ref,
    other_ref,
    shared_ref,
    corr_ref,
    fz_ref,
    fo_ref,
    boy_ref,
    bot_ref,
    boty_ref,
    d_scr,
    bcc_scr,
    bca_scr,
    ds_scr,
    dsb_scr,
    cs_scr,
    bds_scr,
    xs_scr,
    dye_scr,
    nx_scr,
    nbc_scr,
    gx_ref,
    gbc_ref,
    gdt_ref,
    gpre_ref,
    acc_scr,
    send_scr,
    recv_scr,
    dh_scr,
    dh_in,
    x_own,
    core_send,
    core_recv,
    y_sems,
    bo_sems,
    local,
    *machine,
):
    rows_all = dz_ref.shape[0]
    model = hid_ref.shape[1]
    pairs = width // L
    spans = rows_all // L
    Ry = rows_all // ny
    seq, back = pl.program_id(0), pl.program_id(1)
    step = seq * spans + back
    spot = lax.axis_index("tensor")
    core, yy = lax.rem(spot, ncore), spot // ncore
    twin = {"tensor": spot + 1 - 2 * core}
    ys = [lax.rem(yy + d, ny) for d in range(1, ny)]
    peers = [{"tensor": v * ncore + core} for v in ys]
    nbits = log2(ndp)
    dp_peers, dp_bits = bit_peers("dp", 1, 0, nbits)
    links = list(zip(dp_peers, dp_bits))
    swapped = [links[1], links[0]] + links[2:] if nbits > 1 else links
    half = len(machine) // 2
    mz, mo = machine[:half], machine[half:]
    jobs = [
        Halving(links, model, gz_ref, mz[0], mz[1:-1], fz_ref, mz[-1]),
        Halving(swapped, model, go_ref, mo[0], mo[1:-1], fo_ref, mo[-1]),
    ]
    last_step = nloc_static * spans - 1

    def bo_first():
        out = [
            remote(bo_ref, boy_ref.at[d], bo_sems.at[0, d], bo_sems.at[1, d], peers[d])
            for d in range(ny - 1)
        ]
        if ncore == 2:
            out.append(remote(bo_ref, bot_ref, bo_sems.at[0, ny - 1], bo_sems.at[1, ny - 1], twin))
        return out

    def bo_second():
        if ncore != 2:
            return []
        return [
            remote(boy_ref.at[d], boty_ref.at[d], bo_sems.at[0, ny + d], bo_sems.at[1, ny + d], twin)
            for d in range(ny - 1)
        ]

    def dh_copies():
        return [
            remote(
                dh_scr.at[pl.ds(pl.multiple_of(ys[d] * Ry, Ry), Ry)],
                dh_in.at[seq - 1, d],
                y_sems.at[0, seq - 1, d],
                y_sems.at[1, seq - 1, d],
                peers[d],
            )
            for d in range(ny - 1)
        ]

    def x_copy():
        return pltpu.make_async_copy(x_ref.at[core * nloc_static + seq - 1, yy], x_own, local.at[0])

    @pl.when(step == 0)
    def _():
        greet(peers + dp_peers + ([twin] if ncore == 2 else []))
        for copy in bo_first():
            copy.start()
        acc_scr[...] = jnp.zeros_like(acc_scr)
        gx_ref[...] = jnp.zeros_like(gx_ref)
        gbc_ref[...] = jnp.zeros_like(gbc_ref)
        gdt_ref[...] = jnp.zeros_like(gdt_ref)
        gpre_ref[...] = jnp.zeros_like(gpre_ref)

    events = 2 * nbits + 1
    for j in range(events):

        @pl.when(step == (j * last_step + nbits) // (events - 1))
        def _(j=j):
            for job in jobs:
                job.close(j)
            for job in jobs:
                job.begin(j)

    @pl.when(step == last_step // 2)
    def _():
        for copy in bo_first():
            copy.wait()
        for copy in bo_second():
            copy.start()

    @pl.when(jnp.logical_and(seq > 0, back == 0))
    def _():
        for copy in dh_copies():
            copy.start()
        x_copy().start()

    @pl.when(jnp.logical_and(seq > 0, back == spans - 2))
    def _():
        for copy in dh_copies():
            copy.wait()
        x_copy().wait()

        @pl.loop(0, Ry // 32)
        def _(i):
            rows = pl.ds(pl.multiple_of(i * 32, 32), 32)
            mine = pl.ds(pl.multiple_of(yy * Ry + i * 32, 32), 32)
            dh = dh_scr[mine, :].astype(f32)
            for d in range(ny - 1):
                dh = dh + dh_in[seq - 1, d, rows, :].astype(f32)
            corr_ref[seq - 1, rows, :] = correction(x_own[rows, :], dh, gain_ref[...]).astype(bf16)

    hp = hp_ref[...]

    @pl.when(back == 0)
    def _():
        ds_scr[...] = jnp.zeros_like(ds_scr)
        nx_scr[...] = jnp.zeros_like(nx_scr)
        nbc_scr[...] = jnp.zeros_like(nbc_scr)

        @pl.loop(0, spans)
        def _(c):
            t0 = pl.multiple_of(c * L, L)
            for half in range(2):
                lanes = slice(half * L, half * L + L)
                v = conv(bcl_ref[pl.ds(t0, L + PAD), lanes], bcp_ref[0:4, lanes], bcp_ref[4:5, lanes])
                bcc_scr[pl.ds(t0, L), lanes] = v
                bca_scr[pl.ds(t0, L), lanes] = (v * sigmoid(v)).astype(bf16)

    def one_chunk():
        c = spans - 1 - back
        t0 = pl.multiple_of(c * L, L)
        rows = pl.ds(t0, L)
        lane = lane_iota((L, L))
        lo = lane < HEAD
        mlo = (lane_iota((1, L)) < HEAD).astype(bf16)
        mhi = (lane_iota((1, L)) >= HEAD).astype(bf16)
        tri = row_iota((L, L)) >= lane
        pre, dt, cum, cum_t = span_decay(dtl_ref[rows, :], hp)
        bm = bca_scr[rows, 0:L]
        cm = bca_scr[rows, L : 2 * L]
        both = nt(cm, bm)
        sb = sin_ref[c]
        dsb_scr[...] = ds_scr[...].astype(bf16)
        cs_scr[...] = nn(cm, sb)
        bds_scr[...] = nn(bm, dsb_scr[...])
        d_both = jnp.zeros((L, L), f32)
        d_cum = jnp.zeros((L, L), f32)
        d_dt = jnp.zeros((L, L), f32)
        d_far = jnp.zeros((L, L), f32)
        d_end = jnp.zeros((1, L), f32)
        for p in range(pairs):
            lanes = slice(p * L, p * L + L)
            window = xl_ref[pl.ds(t0, L + PAD), lanes]
            shifted = [window[PAD - 3 + k : PAD - 3 + k + L] for k in range(4)]
            taps = prm_ref[0:4, lanes]
            xc = prm_ref[4:5, lanes]
            for k in range(4):
                xc = xc + shifted[k] * taps[k : k + 1]
            sg = sigmoid(xc)
            x = xc * sg
            h0, h1 = 2 * p, 2 * p + 1
            a0, a1 = spread(cum, h0), spread(cum, h1)
            ap = jnp.where(lo, a0, a1)
            e0 = jnp.exp(jnp.where(tri, a0 - cum_t[h0 : h0 + 1], -jnp.inf))
            e1 = jnp.exp(jnp.where(tri, a1 - cum_t[h1 : h1 + 1], -jnp.inf))
            k0 = (both * e0).astype(bf16)
            k1 = (both * e1).astype(bf16)
            dtp = jnp.where(lo, spread(dt, h0), spread(dt, h1))
            xdt = x * dtp
            xb = xdt.astype(bf16)
            bdx = jnp.concatenate([xb * mlo, xb * mhi], axis=0)
            ecum = jnp.exp(ap)
            fin = ap[L - 1 : L]
            sd = jnp.exp(fin - ap)
            y = nn(jnp.concatenate([k0, k1], axis=1), bdx) + ecum * cs_scr[:, lanes]
            dyb = dy_ref[rows, lanes]
            dy = dyb.astype(f32)
            dk = nt(dyb, bdx)
            d_both = d_both + dk[:, 0:L] * e0 + dk[:, L : 2 * L] * e1
            bdy = jnp.concatenate([dyb * mlo, dyb * mhi], axis=0)
            near = tn(jnp.concatenate([k0, k1], axis=0), bdy)
            far = sd * bds_scr[:, lanes]
            dxdt = near + far
            v = dy * y - xb.astype(f32) * near
            u = dxdt * x
            w = xdt * far
            ends = jnp.exp(fin)
            through = ends * jnp.sum(sb[:, lanes].astype(f32) * ds_scr[:, lanes], axis=0, keepdims=True)
            for h, keep in ((h0, lo), (h1, jnp.logical_not(lo))):
                here = lane == h
                d_cum = jnp.where(here, jnp.sum(jnp.where(keep, v, 0.0), axis=1, keepdims=True), d_cum)
                d_dt = jnp.where(here, jnp.sum(jnp.where(keep, u, 0.0), axis=1, keepdims=True), d_dt)
                d_far = jnp.where(here, jnp.sum(jnp.where(keep, w, 0.0), axis=1, keepdims=True), d_far)
                whole = jnp.sum(jnp.where(keep[0:1], through, 0.0), axis=1, keepdims=True)
                d_end = jnp.where(here[0:1], whole, d_end)
            dx = dxdt * dtp + dy * prm_ref[5:6, lanes]
            dxc = dx * (sg + x * (1.0 - sg))
            for k in range(4):
                gx_ref[k, :, lanes] += fold_rows(dxc * shifted[k])
            gx_ref[4, :, lanes] += fold_rows(dxc)
            gx_ref[5, :, lanes] += fold_rows(dy * x)
            ext = jnp.concatenate([dxc, nx_scr[:, lanes]], axis=0)
            dxl = ext[0:L] * taps[3:4]
            for k in range(3):
                dxl = dxl + ext[3 - k : 3 - k + L] * taps[k : k + 1]
            nx_scr[:, lanes] = dxc[0:8]
            d_scr[rows, lanes] = dxl.astype(bf16)
            xs_scr[:, lanes] = (xdt * sd).astype(bf16)
            dye_scr[:, lanes] = (dy * ecum).astype(bf16)
            ds_scr[:, lanes] = ds_scr[:, lanes] * ends
        ds_scr[...] += nn(cm.T, dye_scr[...])
        utri = (row_iota((L, L)) <= lane).astype(f32)
        before = (row_iota((L, L)) > lane).astype(f32)
        d_a = exact(utri, d_cum) + exact(before, d_far) + d_end
        d_dt = d_dt + d_a * hp[1:2]
        d_pre = d_dt * sigmoid(pre)
        gdt_ref[0] += fold_rows(d_pre)
        gdt_ref[1] += fold_rows(d_a * dt * hp[1:2])
        d_scr[rows, width + 256 : width + 384] = d_pre.astype(bf16)
        dgb = d_both.astype(bf16)
        d_c = nt(dye_scr[...], sb) + nn(dgb, bm)
        d_b = nt(xs_scr[...], dsb_scr[...]) + nn(dgb.T, cm)
        for half, dv in ((0, d_b), (1, d_c)):
            lanes = slice(half * L, half * L + L)
            pre_act = bcc_scr[rows, lanes]
            sg = sigmoid(pre_act)
            dvc = dv * (sg + pre_act * sg * (1.0 - sg))
            window = bcl_ref[pl.ds(t0, L + PAD), lanes]
            for k in range(4):
                gbc_ref[k, :, lanes] += fold_rows(dvc * window[PAD - 3 + k : PAD - 3 + k + L])
            gbc_ref[4, :, lanes] += fold_rows(dvc)
            ext = jnp.concatenate([dvc, nbc_scr[:, lanes]], axis=0)
            dvl = ext[0:L] * bcp_ref[3:4, lanes]
            for k in range(3):
                dvl = dvl + ext[3 - k : 3 - k + L] * bcp_ref[k : k + 1, lanes]
            nbc_scr[:, lanes] = dvc[0:8]
            d_scr[rows, width + half * L : width + half * L + L] = dvl.astype(bf16)

    one_chunk()

    @pl.when(back == spans - 1)
    def _():
        @pl.loop(0, model // 256)
        def _(j):
            cols = pl.ds(pl.multiple_of(j * 256, 256), 256)
            dh = nt(dz_ref[...], w_ref[cols, 0:width]) + nt(d_scr[...], w_ref[cols, width:])
            dh_scr[:, cols] = dh.astype(bf16)
            gpre_ref[:, cols] += fold_rows(dh * hid_ref[:, cols].astype(f32))
            acc_scr[cols, :] += tn(hid_ref[:, cols], d_scr[...])

    @pl.when(step == last_step)
    def _():
        tail = acc_scr[:, width + 256 : width + 384]
        if ncore == 2:
            send_scr[:, 0:own] = acc_scr[:, own:width].astype(bf16)
            send_scr[:, own : own + L] = tail.astype(bf16)
        dh_ref[...] = dh_scr[...]
        gbcw_ref[...] = acc_scr[:, width : width + 256].astype(gbcw_ref.dtype)
        if ncore == 2:
            copy = remote(send_scr, recv_scr, core_send, core_recv, twin)
            copy.start()
        rows = [jnp.sum(gx_ref[k], axis=0, keepdims=True) for k in range(6)]
        rows.append(jnp.sum(ggg_ref[...], axis=0, keepdims=True))
        dts = [jnp.sum(gdt_ref[k], axis=0, keepdims=True) for k in range(2)]
        small_ref[...] = jnp.zeros_like(small_ref)
        other_ref[...] = jnp.zeros_like(other_ref)
        for k in range(7):
            small_ref[k : k + 1, :] = rows[k][:, 0:own]
            if ncore == 2:
                other_ref[k : k + 1, :] = rows[k][:, own:width]
        for k in range(2):
            small_ref[7 + k : 8 + k, 0:L] = dts[k]
            if ncore == 2:
                moved = pltpu.roll(jnp.broadcast_to(dts[k], (8, L)), L - heads, axis=1)
                other_ref[7 + k : 8 + k, 0:L] = moved[0:1]
        shared_ref[...] = jnp.zeros_like(shared_ref)
        shared_ref[0:1, :] = jnp.sum(gpre_ref[...], axis=0, keepdims=True) / gain_ref[...]
        for k in range(5):
            shared_ref[k + 1 : k + 2, 0:256] = jnp.sum(gbc_ref[k], axis=0, keepdims=True)
        if ncore == 2:
            copy.wait()
            theirs = recv_scr[...].astype(f32)
            gw_ref[:, 0:own] = (acc_scr[:, 0:own] + theirs[:, 0:own]).astype(bf16)
            tail = tail + pltpu.roll(theirs[:, own : own + L], L - heads, axis=1)
        else:
            gw_ref[:, 0:own] = acc_scr[:, 0:own].astype(bf16)
        gw_ref[:, own : own + L] = tail.astype(bf16)
        for copy in bo_second():
            copy.wait()


def tail_kernel(
    own,
    ncore,
    ny,
    ndp,
    gw_ref,
    gbcw_ref,
    small_ref,
    other_ref,
    shared_ref,
    dh_ref,
    gain_ref,
    corr_ref,
    x_ref,
    fw_ref,
    fb_ref,
    small_out,
    shared_out,
    last_ref,
    cy_ref,
    ct_ref,
    cty_ref,
    ly_ref,
    lt_ref,
    lty_ref,
    dh_in,
    x_own,
    small_in,
    core_sems,
    y_sems,
    c_sems,
    l_sems,
    local,
    *machine,
):
    model = gw_ref.shape[0]
    Ry, nloc = x_own.shape[0], corr_ref.shape[0] + 1
    spot = lax.axis_index("tensor")
    core, yy = lax.rem(spot, ncore), spot // ncore
    twin = {"tensor": spot + 1 - 2 * core}
    ys = [lax.rem(yy + d, ny) for d in range(1, ny)]
    peers = [{"tensor": v * ncore + core} for v in ys]
    nbits = log2(ndp)
    dp_peers, dp_bits = bit_peers("dp", 1, 0, nbits)
    t_peers, t_bits = bit_peers("tensor", 1, 0, log2(ncore * ny))
    links = list(zip(dp_peers, dp_bits))
    swapped = [links[1], links[0]] + links[2:] if nbits > 1 else links
    t_links = list(zip(t_peers, t_bits))
    per = nbits + 2
    a, b = machine[:per], machine[per : 2 * per]
    per_bc = nbits + len(t_links) + 2
    c = machine[2 * per : 2 * per + per_bc]
    sm, sh = machine[2 * per + per_bc : 2 * per + per_bc + 3], machine[2 * per + per_bc + 3 :]
    mid = model // 2
    job_a = Halving(links, mid, gw_ref.at[0:mid], a[0], a[1:-1], fw_ref.at[0:mid], a[-1])
    job_b = Halving(swapped, mid, gw_ref.at[mid:model], b[0], b[1:-1], fw_ref.at[mid:model], b[-1])
    job_c = Halving(t_links + links, model, gbcw_ref, c[0], c[1:-1], fb_ref, c[-1])
    job_sm = Doubling(dp_peers, *sm)
    job_sh = Doubling(t_peers + dp_peers, *sh)

    def dh_copies():
        return [
            remote(
                dh_ref.at[pl.ds(pl.multiple_of(ys[d] * Ry, Ry), Ry)],
                dh_in.at[d],
                y_sems.at[0, d],
                y_sems.at[1, d],
                peers[d],
            )
            for d in range(ny - 1)
        ]

    def first(src, toy, tot, sems):
        out = [
            remote(src, toy.at[d], sems.at[0, d], sems.at[1, d], peers[d]) for d in range(ny - 1)
        ]
        if ncore == 2:
            out.append(remote(src, tot, sems.at[0, ny - 1], sems.at[1, ny - 1], twin))
        return out

    def second(toy, toty, sems):
        if ncore != 2:
            return []
        return [
            remote(toy.at[d], toty.at[d], sems.at[0, ny + d], sems.at[1, ny + d], twin)
            for d in range(ny - 1)
        ]

    early = (corr_ref, cy_ref, ct_ref, c_sems)
    late = (last_ref, ly_ref, lt_ref, l_sems)
    x_copy = pltpu.make_async_copy(x_ref.at[core * nloc + nloc - 1, yy], x_own, local.at[0])
    others = peers + ([twin] if ncore == 2 else [])
    greet(others + dp_peers)
    x_copy.start()

    def turn(*pairs):
        for job, j in pairs:
            job.close(j)
        for job, j in pairs:
            job.begin(j)

    job_sh.acc[0] = shared_ref[...]
    turn((job_c, 0), (job_a, 0), (job_b, 0))
    if ncore == 2:
        small_copy = remote(other_ref, small_in, core_sems.at[0], core_sems.at[1], twin)
        small_copy.start()
    turn((job_c, 1), (job_sh, 0))
    for copy in dh_copies():
        copy.start()
    for copy in first(*early):
        copy.start()
    if ncore == 2:
        small_copy.wait()
        job_sm.acc[0] = small_ref[...] + small_in[...]
    else:
        job_sm.acc[0] = small_ref[...]
    turn((job_sh, 1), (job_sm, 0))
    steps = [
        (job_c, iter(range(2, 2 * job_c.n + 1))),
        (job_sm, iter(range(1, len(job_sm.peers) + 1))),
        (job_sh, iter(range(2, len(job_sh.peers) + 1))),
    ]

    def smaller():
        found = []
        for job, left in steps:
            j = next(left, None)
            if j is not None:
                found.append((job, j))
        return found

    turn((job_a, 1), (job_b, 1), *smaller())
    for copy in dh_copies():
        copy.wait()
    x_copy.wait()

    @pl.loop(0, Ry // 32)
    def _(i):
        rows = pl.ds(pl.multiple_of(i * 32, 32), 32)
        mine = pl.ds(pl.multiple_of(yy * Ry + i * 32, 32), 32)
        dh = dh_ref[mine, :].astype(f32)
        for d in range(ny - 1):
            dh = dh + dh_in[d, rows, :].astype(f32)
        last_ref[rows, :] = correction(x_own[rows, :], dh, gain_ref[...]).astype(bf16)

    turn(*smaller())
    for copy in first(*late):
        copy.start()
    for j in range(2, 2 * nbits + 1):
        turn((job_a, j), (job_b, j), *smaller())
    for copy in first(*early):
        copy.wait()
    for copy in second(cy_ref, cty_ref, c_sems):
        copy.start()
    for _ in range(2 * job_c.n):
        turn(*smaller())
    small_out[...] = job_sm.acc[len(job_sm.peers)]
    shared_out[...] = job_sh.acc[len(job_sh.peers)]
    for copy in first(*late):
        copy.wait()
    for copy in second(ly_ref, lty_ref, l_sems):
        copy.start()
    for copy in second(cy_ref, cty_ref, c_sems) + second(ly_ref, lty_ref, l_sems):
        copy.wait()


def finish_kernel(pieces, nloc, _idx, g_ref, *refs):
    gi_ref, bo_ref = refs[-2:]
    early, late, outs = refs[:pieces], refs[pieces : 2 * pieces], refs[2 * pieces : 3 * pieces]
    last = pl.program_id(1) == nloc - 1
    for k in range(pieces):
        here = pl.program_id(0) == k

        @pl.when(here)
        def _(src=outs[k]):
            bo_ref[...] = src[...]

        @pl.when(jnp.logical_and(here, jnp.logical_not(last)))
        def _(src=early[k]):
            gi_ref[...] = g_ref[...].astype(f32) + src[...].astype(f32)

        @pl.when(jnp.logical_and(here, last))
        def _(src=late[k]):
            gi_ref[...] = g_ref[...].astype(f32) + src[...].astype(f32)


def unpack_kernel(own, gz_ref, go_ref, gw_ref, gzx_ref, gwo_ref):
    gzx_ref[:, 0, :] = gz_ref[...].astype(f32)
    gzx_ref[:, 1, :] = gw_ref[:, 0:own].astype(f32)
    v = go_ref[...].astype(f32)
    for k in range(own // L):
        gwo_ref[k * L : k * L + L, :] = v[:, k * L : k * L + L].T


def seq_spec(*shape):
    zeros = (0,) * len(shape)
    return pl.BlockSpec((None,) + shape, lambda i, s: (i,) + zeros)


def moved_spec(ncore, nloc, *shape):
    zeros = (0,) * len(shape)

    def index(i, s):
        return (i + lax.rem(lax.axis_index("tensor"), ncore) * nloc,) + zeros

    return pl.BlockSpec((None,) + shape, index)


def whole_spec(*shape):
    zeros = (0,) * len(shape)
    return pl.BlockSpec(shape, lambda *_: zeros, pipeline_mode=pl.Buffered(1))


def call(
    kernel, grid, in_specs, out_specs, out_shape, scratch, name, flops=0, moved=0, group=None
):
    return pl.pallas_call(
        kernel,
        grid_spec=pltpu.PrefetchScalarGridSpec(
            num_scalar_prefetch=1,
            grid=grid,
            in_specs=in_specs,
            out_specs=out_specs,
            scratch_shapes=scratch,
        ),
        out_shape=out_shape,
        cost_estimate=pl.CostEstimate(
            flops=int(flops), bytes_accessed=int(moved), transcendentals=0
        ),
        name=name,
        compiler_params=None
        if group is None
        else pltpu.CompilerParams(collective_id=group, has_side_effects=True),
    )


def sds(*shape, dtype=f32):
    return jax.ShapeDtypeStruct(shape, dtype)


def body(
    block_input,
    pre_gain,
    w_zx,
    w_bc,
    w_dt,
    conv_x_w,
    conv_x_b,
    conv_bc_w,
    conv_bc_b,
    dt_bias,
    a_log,
    d_skip,
    gate_gain,
    w_out,
    out_grad,
):
    tok, model = block_input.shape
    own = w_zx.shape[2]
    heads = w_dt.shape[1]
    nt = lax.axis_size("tensor")
    ndp = lax.axis_size("dp")
    inner_total = own * nt
    ncore = 2 if nt % 2 == 0 else 1
    ny = nt // ncore
    width = own * ncore
    t = lax.axis_index("tensor")
    me = lax.axis_index("dp")
    core, yy = t % ncore, t // ncore
    R = SEQ_LEN
    Ry = R // ny
    nseq = tok // R
    nloc = nseq // ncore
    spans = R // L
    wtot = 2 * width + 384

    def swap_core(v):
        return lax.ppermute(v, "tensor", [(i, i ^ 1) for i in range(nt)])

    def y_shift(v, d):
        pairs = [(i, ((i // ncore + d) % ny) * ncore + i % ncore) for i in range(nt)]
        return lax.ppermute(v, "tensor", pairs)

    def dp_shift(v, d):
        return lax.ppermute(v, "dp", [(i, (i + d) % ndp) for i in range(ndp)])

    def both_cores(v, axis):
        return jnp.concatenate([v, swap_core(v)], axis=axis) if ncore == 2 else v

    x3 = block_input.reshape(nseq, R, model)
    g3 = out_grad.reshape(nseq, R, model)
    x4 = block_input.reshape(nseq, ny, Ry, model)
    g4 = out_grad.reshape(nseq, ny, Ry, model)
    wz, wx = w_zx[:, 0], w_zx[:, 1]
    rowp = jnp.concatenate(
        [
            conv_x_w,
            conv_x_b[None],
            jnp.repeat(d_skip, HEAD)[None],
            gate_gain[None],
            jnp.pad(jnp.concatenate([dt_bias, -jnp.exp(a_log)]), (0, own - 2 * heads))[None],
        ],
        axis=0,
    )
    prm = both_cores(rowp, 1)
    hrow = prm[7].reshape(ncore, own)
    hp = jnp.stack([hrow[:, :heads].reshape(-1), hrow[:, heads : 2 * heads].reshape(-1)])
    hp = jnp.pad(hp, ((0, 6), (0, L - ncore * heads)))
    wdt = jnp.pad(both_cores(w_dt, 1), ((0, 0), (0, L - ncore * heads)))
    wcat = jnp.concatenate([both_cores(wz, 1), both_cores(wx, 1), w_bc, wdt], axis=1)
    wo = both_cores(w_out, 0)
    bcp = jnp.concatenate([conv_bc_w, conv_bc_b[None], jnp.zeros((3, 256), f32)], axis=0)
    gain = pre_gain[None]
    seq0 = jnp.array([core * nloc], jnp.int32)

    hid, z, xl, bcl, dtl, u, y, sin, st, po = call(
        partial(forward_kernel, width),
        (nloc,),
        [
            moved_spec(ncore, nloc, R, model),
            moved_spec(ncore, nloc, R, model),
            whole_spec(1, model),
            whole_spec(model, wtot),
            whole_spec(width, model),
            whole_spec(8, width),
            whole_spec(8, 256),
            whole_spec(8, L),
        ],
        [
            seq_spec(R, model),
            seq_spec(R, width),
            seq_spec(R + PAD, width),
            seq_spec(R + PAD, 256),
            seq_spec(R, L),
            seq_spec(R, width),
            seq_spec(R, width),
            seq_spec(spans, L, width),
            seq_spec(2, R),
            seq_spec(R, model),
        ],
        [
            sds(nloc, R, model, dtype=bf16),
            sds(nloc, R, width),
            sds(nloc, R + PAD, width),
            sds(nloc, R + PAD, 256),
            sds(nloc, R, L),
            sds(nloc, R, width),
            sds(nloc, R, width),
            sds(nloc, spans, L, width, dtype=bf16),
            sds(nloc, 2, R),
            sds(nloc, R, model, dtype=bf16),
        ],
        [
            pltpu.VMEM((R, width), bf16),
            pltpu.VMEM((R, 256), bf16),
            pltpu.VMEM((L, width), f32),
            pltpu.VMEM((L, width), f32),
            pltpu.VMEM((L, width), bf16),
        ],
        "forward",
        2 * nloc * R * model * (wtot + 2 * width),
        nloc * R * (6 * model + 20 * width),
    )(seq0, x3, g3, gain, wcat, wo, prm, bcp, hp)

    any_spec = pl.BlockSpec(memory_space=pl.ANY)
    nbits = log2(ndp)
    nother = max(ny - 1, 1)
    dma = pltpu.SemaphoreType.DMA
    po4 = po.reshape(nloc, ny, Ry, model)
    dz, dy, gz, go, ggg, bo, st = call(
        partial(gate_kernel, width, own, inner_total, ncore, ny),
        (nloc,),
        [
            whole_spec(nloc, 2, R),
            moved_spec(ncore, nloc, R, model),
            seq_spec(R, model),
            seq_spec(R, width),
            seq_spec(R, width),
            seq_spec(R, width),
            whole_spec(8, width),
            any_spec,
            any_spec,
        ],
        [
            seq_spec(R, width),
            seq_spec(R, width),
            whole_spec(model, own),
            whole_spec(model, own),
            whole_spec(8, width),
            whole_spec(nloc, Ry, model),
            whole_spec(nloc, 2, R),
        ],
        [
            sds(nloc, R, width, dtype=bf16),
            sds(nloc, R, width, dtype=bf16),
            sds(model, own, dtype=bf16),
            sds(model, own, dtype=bf16),
            sds(8, width),
            sds(nloc, Ry, model, dtype=bf16),
            sds(nloc, 2, R),
        ],
        [
            pltpu.VMEM((R, width), bf16),
            pltpu.VMEM((R, model), bf16),
            pltpu.VMEM((model, 2 * width), f32),
            pltpu.VMEM((nother, nloc, 2, R), f32),
            pltpu.VMEM((model, 2 * own), bf16),
            pltpu.VMEM((model, 2 * own), bf16),
            pltpu.VMEM((nother, nloc, Ry, model), bf16),
            pltpu.VMEM((nloc, Ry, model), bf16),
            pltpu.VMEM((nloc, Ry, model), bf16),
            dma((nother,)),
            dma((nother,)),
            dma,
            dma,
            dma((nother,)),
            dma((nother,)),
            dma((2,)),
        ],
        "gate",
        4 * nloc * R * model * width,
        nloc * R * (4 * model + 16 * width),
        1,
    )(seq0, st, g3, hid, z, y, u, prm, po4, x4)

    def chunk_spec(*shape):
        zeros = (0,) * len(shape)
        return pl.BlockSpec((None,) + shape, lambda i, b, s: (i,) + zeros)

    bc_type = bf16 if (model // (nt * ndp)) % 16 == 0 else f32
    dh, gw2, gbcw, small, other, shared, corr, fz, fo, boy, bot, boty = call(
        partial(scan_kernel, width, own, heads, ncore, ny, ndp, nloc),
        (nloc, spans),
        [
            chunk_spec(R, model),
            chunk_spec(R, width),
            chunk_spec(R, width),
            chunk_spec(R + PAD, width),
            chunk_spec(R + PAD, 256),
            chunk_spec(R, L),
            chunk_spec(spans, L, width),
            pl.BlockSpec((model, wtot), lambda i, b, s: (0, 0), pipeline_mode=pl.Buffered(1)),
            whole_spec(8, width),
            whole_spec(8, 256),
            whole_spec(8, L),
            whole_spec(8, width),
            whole_spec(1, model),
            whole_spec(model, own),
            whole_spec(model, own),
            any_spec,
            any_spec,
        ],
        [
            whole_spec(R, model),
            whole_spec(model, own + L),
            whole_spec(model, 256),
            whole_spec(16, own),
            whole_spec(16, own),
            whole_spec(8, model),
            whole_spec(nloc - 1, Ry, model),
        ]
        + [any_spec] * 5,
        [
            sds(R, model, dtype=bf16),
            sds(model, own + L, dtype=bf16),
            sds(model, 256, dtype=bc_type),
            sds(16, own),
            sds(16, own),
            sds(8, model),
            sds(nloc - 1, Ry, model, dtype=bf16),
            sds(model, own, dtype=bf16),
            sds(model, own, dtype=bf16),
            sds(nother, nloc, Ry, model, dtype=bf16),
            sds(nloc, Ry, model, dtype=bf16),
            sds(nother, nloc, Ry, model, dtype=bf16),
        ],
        [
            pltpu.VMEM((R, width + 384), bf16),
            pltpu.VMEM((R, 256), f32),
            pltpu.VMEM((R, 256), bf16),
            pltpu.VMEM((L, width), f32),
            pltpu.VMEM((L, width), bf16),
            pltpu.VMEM((L, width), f32),
            pltpu.VMEM((L, width), f32),
            pltpu.VMEM((L, width), bf16),
            pltpu.VMEM((L, width), bf16),
            pltpu.VMEM((8, width), f32),
            pltpu.VMEM((8, 256), f32),
            pltpu.VMEM((6, 8, width), f32),
            pltpu.VMEM((5, 8, 256), f32),
            pltpu.VMEM((2, 8, L), f32),
            pltpu.VMEM((8, model), f32),
            pltpu.VMEM((model, width + 384), f32),
            pltpu.VMEM((model, own + L), bf16),
            pltpu.VMEM((model, own + L), bf16),
            pltpu.VMEM((R, model), bf16),
            pltpu.VMEM((nloc - 1, nother, Ry, model), bf16),
            pltpu.VMEM((Ry, model), bf16),
            dma,
            dma,
            dma((2, nloc - 1, nother)),
            dma((2, 2 * ny)),
            dma((1,)),
        ]
        + Halving.scratch(model, own, nbits, bf16)
        + Halving.scratch(model, own, nbits, bf16),
        "scan_back",
        2 * nloc * R * model * (2 * wtot),
        nloc * R * (4 * model + 12 * width),
        2,
    )(seq0, hid, dz, dy, xl, bcl, dtl, sin, wcat, prm, bcp, hp, ggg, gain, gz, go, bo, x4)

    vm = pl.BlockSpec(memory_space=pltpu.VMEM)
    tbits = log2(nt)
    early_shape = sds(nother, nloc - 1, Ry, model, dtype=bf16)
    late_shape = sds(nother, Ry, model, dtype=bf16)
    fw, fb, small, shared, last, cy, ct, cty, ly, lt, lty = pl.pallas_call(
        partial(tail_kernel, own, ncore, ny, ndp),
        in_specs=[vm] * 7 + [any_spec] * 2,
        out_specs=[any_spec] * 2 + [vm] * 3 + [any_spec] * 6,
        out_shape=[
            sds(model, own + L, dtype=bf16),
            sds(model, 256, dtype=bc_type),
            sds(16, own),
            sds(8, model),
            sds(Ry, model, dtype=bf16),
            early_shape,
            sds(nloc - 1, Ry, model, dtype=bf16),
            early_shape,
            late_shape,
            sds(Ry, model, dtype=bf16),
            late_shape,
        ],
        scratch_shapes=[
            pltpu.VMEM((nother, Ry, model), bf16),
            pltpu.VMEM((Ry, model), bf16),
            pltpu.VMEM((16, own), f32),
            dma((2,)),
            dma((2, nother)),
            dma((2, 2 * ny)),
            dma((2, 2 * ny)),
            dma((1,)),
        ]
        + Halving.scratch(model // 2, own + L, nbits, bf16)
        + Halving.scratch(model // 2, own + L, nbits, bf16)
        + Halving.scratch(model, 256, nbits + tbits, bc_type)
        + Doubling.scratch(nbits, 16, own)
        + Doubling.scratch(nbits + tbits, 8, model),
        compiler_params=pltpu.CompilerParams(collective_id=3, has_side_effects=True),
        name="tail",
    )(gw2, gbcw, small, other, shared, dh, gain, corr, x4)

    pieces = ncore * ny
    where = jnp.stack([core, yy]).astype(jnp.int32)

    def out_index(k, i, s):
        return ((s[0] ^ (k // ny)) * nloc + i, (s[1] - k % ny + ny) % ny, 0, 0)

    def piece_spec(k, count):
        def index(j, i, s):
            i = jnp.minimum(i, count - 1)
            return (jnp.where(j == k, i, jnp.where(j > k, count - 1, 0)), 0, 0)

        return pl.BlockSpec((None, Ry, model), index)

    placed_spec = pl.BlockSpec((None, None, Ry, model), out_index)

    def all_pieces(mine, toy, tot, toty):
        got = [mine] + [toy[d] for d in range(ny - 1)]
        if ncore == 2:
            got = got + [tot] + [toty[d] for d in range(ny - 1)]
        return got

    early = all_pieces(corr, cy, ct, cty)
    late = all_pieces(last[None], ly[:, None], lt[None], lty[:, None])
    outs = all_pieces(bo, boy, bot, boty)
    grad_input, block_output = call(
        partial(finish_kernel, pieces, nloc),
        (pieces, nloc),
        [placed_spec]
        + [piece_spec(k, nloc - 1) for k in range(pieces)]
        + [piece_spec(k, 1) for k in range(pieces)]
        + [piece_spec(k, nloc) for k in range(pieces)],
        [placed_spec, placed_spec],
        [sds(nseq, ny, Ry, model), sds(nseq, ny, Ry, model, dtype=bf16)],
        [],
        "finish",
        0,
        12 * tok * model,
    )(where, g4, *early, *late, *outs)

    gzx, gwo = pl.pallas_call(
        partial(unpack_kernel, own),
        grid=(model // L,),
        in_specs=[
            pl.BlockSpec((L, own), lambda d: (d, 0)),
            pl.BlockSpec((L, own), lambda d: (d, 0)),
            pl.BlockSpec((L, own + L), lambda d: (d, 0)),
        ],
        out_specs=[
            pl.BlockSpec((L, 2, own), lambda d: (d, 0, 0)),
            pl.BlockSpec((own, L), lambda d: (0, d)),
        ],
        out_shape=[sds(model, 2, own), sds(own, model)],
        name="unpack",
    )(fz, fo, fw)
    tail = fw[:, own : own + heads].astype(f32)
    return (
        block_output.reshape(tok, model),
        grad_input.reshape(tok, model),
        shared[0],
        gzx,
        fb.astype(f32),
        tail,
        small[0:4],
        small[4],
        shared[1:5, 0:256],
        shared[5, 0:256],
        small[7, :heads],
        small[8, :heads],
        jnp.sum(small[5].reshape(heads, HEAD), axis=1),
        small[6],
        gwo,
    )


def solution(mesh):
    placed = (
        P("dp", None),
        P(),
        P(None, None, "tensor"),
        P(),
        P(None, "tensor"),
        P(None, "tensor"),
        P("tensor"),
        P(),
        P(),
        P("tensor"),
        P("tensor"),
        P("tensor"),
        P("tensor"),
        P("tensor", None),
        P("dp", None),
    )
    return jax.shard_map(
        body,
        mesh=mesh,
        in_specs=placed,
        out_specs=(
            P("dp", None),
            P("dp", None),
            P(),
            P(None, None, "tensor"),
            P(),
            P(None, "tensor"),
            P(None, "tensor"),
            P("tensor"),
            P(),
            P(),
            P("tensor"),
            P("tensor"),
            P("tensor"),
            P("tensor"),
            P("tensor", None),
        ),
        check_vma=False,
    )
```

time: 952 us -> 381 us (0.40); the launches traced: 941 us -> 380 us
  Pallas kernels: 0 us -> 345 us
  waiting for transfers between devices: 263 us -> 1.48 us
  matrix products: 227 us -> 0 us
  other arithmetic: 176 us -> 9.07 us
  local copies, waits for them, and re-layouts: 160 us -> 22.4 us
  blocking collectives: 100 us -> 0 us
  between operations: 15.2 us -> 0.95 us
    pallas_call x0 -> x6, Pallas kernels: none -> 345 us  [the longest x1 108 us: body(): call(partial(scan_kernel, width, own, heads, ncore, ny, ndp, nloc), (nloc...]
    psum x3 -> x0, waiting for transfers between devices: 263 us -> none  [the longest x1 194 us: body(): lax.psum(partial_out.astype(jnp.bfloat16), 'tensor').astype(jnp.float32)]
    dot_general x22 -> x0, matrix products: 220 us -> none  [the longest x3 89.2 us: ssd_scan(): jnp.einsum('schij,scjhp->scihp', kernel_mat, weighted, precision=precise)]
    psum x4 -> x0, blocking collectives: 100 us -> none  [the longest x1 39.6 us: body(): lax.psum((grad_pre_part, grad_w_bc_part, grad_conv_bc_w, grad_conv_bc_b),...]
    reshape x12 -> x0, local copies, waits for them, and re-layouts: 90.5 us -> none  [the longest x4 33.3 us: to_seqs(): return matrix.reshape(seq_count, SEQ_LEN, matrix.shape[-1])]
    reduce_sum x9 -> x1, other arithmetic: 50.2 us -> 0.63 us  [body(): jnp.sum(small[5].reshape(heads, HEAD), axis=1)]
    another operation x7 -> x2, other arithmetic: 47.2 us -> 1.27 us  [the longest x1 0.66 us: body(): where = jnp.stack([core, yy]).astype(jnp.int32)]
    mul x6 -> x0, other arithmetic: 31 us -> none  [the longest x1 14.4 us: mixer(): x_active = jax.nn.silu(causal_conv(x_linear, conv_weight, conv_bias))]
  transfers between devices with their start and end apart: 3 -> 5, of which waited for: 2 -> 1; matrix products, arithmetic and copies ran while one was open for 18% -> 2% of each run, Pallas kernels for 0% -> 0%
where the time goes in v1:
time: 381 us; the launch traced here: 380 us
  Pallas kernels  345 us (91%)
  local copies, waits for them, and re-layouts  22.4 us (6%)
  other arithmetic  9.07 us (2%)
    pallas_call x1, Pallas kernels, body(): call(partial(scan_kernel, width, own, heads, ncore, ny, ndp, nloc), (nloc...  108 us
    pallas_call x1, Pallas kernels, body(): pl.pallas_call(partial(tail_kernel, own, ncore, ny, ndp), in_specs=[vm] *...  98.1 us
    pallas_call x1, Pallas kernels, body(): call(partial(forward_kernel, width), (nloc,), [moved_spec(ncore, nloc, R,...  62 us
    pallas_call x1, Pallas kernels, body(): call(partial(gate_kernel, width, own, inner_total, ncore, ny), (nloc,), [...  51.9 us
    pallas_call x1, Pallas kernels, body(): call(partial(finish_kernel, pieces, nloc), (pieces, nloc), [placed_spec]...  17.3 us
  transfers between devices with their start and end apart: 5, of which 1 were waited for; matrix products, arithmetic and copies ran while one was open for 2% of the time, Pallas kernels for 0%

profile of v1, /device:TPU:0, one launch (start us, length us, event | category | flops | bytes accessed | tf_op | source)
XLA Modules:
  0.0 380.2 jit_solution(15023729028903672798)
XLA Ops:
  0.6 5.6 %fusion.2 = (bf16[1024,1,512]{2,1,0:T(2,128)(2,1)S(1)}, bf16[1024,1,512]{2,1,0:T(2,128)(2,1)S(1)}) fusion(bf16[1024,2,512]{2,1,0:T(2,128)(2,1)} %param.17), kind=kLoop, calls=%fused_computation.27 | loop fusion | bytes 4194304 | tf_op jit(solution)/shard_map/slice | solution.py:1165
  6.3 0.0 copy-start.8
  6.3 0.0 copy-start.9
  6.3 0.0 copy-start.3
  6.3 0.0 copy-start.6
  6.3 0.0 copy-start.2
  6.3 1.7 constant_dynamic-update-slice_fusion.4
  8.0 0.5 collective-permute-start
  8.5 0.1 broadcast_in_dim.33
  8.6 0.1 broadcast_in_dim_reshape.3
  8.7 0.1 select_maximum_fusion.1
  8.8 0.1 collective-permute-start.4
  8.9 0.5 collective-permute-start.2
  9.4 0.1 collective-permute-start.3
  9.5 0.1 pad.19.clone
  9.6 1.5 collective-permute-done
  11.0 1.1 constant_dynamic-update-slice_fusion.3
  12.1 1.8 constant_dynamic-update-slice_fusion.2
  13.9 0.4 collective-permute-start.1
  14.3 0.7 maximum_maximum_fusion.bcp_ref
  14.9 0.7 pad_add_fusion._idx
  15.6 0.1 fusion.4
  15.7 0.1 stack_reshape.6
  15.8 0.1 stack_reshape.7
  15.9 0.2 copy.37
  16.1 0.6 select_maximum_fusion.hp_ref
  16.7 0.6 pad_maximum_fusion.1.prm_ref
  17.3 2.7 pad_maximum_fusion.wo_ref
  20.0 1.1 constant_dynamic-update-slice_fusion.1
  21.1 0.9 constant_dynamic-update-slice_fusion
  22.0 0.8 pad_dynamic-update-slice_fusion.w_ref
  22.8 62.0 %forward.1 = (bf16[3,512,1024]{2,1,0:T(8,128)(2,1)}, f32[3,512,1024]{2,1,0:T(8,128)}, f32[3,520,1024]{2,1,0:T(8,128)}, f32[3,520,256]{2,1,0:T(8,128)}, f32[3,512...) custom-call(s32[1]{0:T(128)} %bitcast.3._seq, ...), custom_call_target="tpu_custom_call" | custom-call | flops 14092861440 | bytes 40894464 | tf_op jit(solution)/shard_map/forward/pallas_call | solution.py:1187
  84.8 51.9 %gate.1 = (bf16[3,512,1024]{2,1,0:T(8,128)(2,1)}, bf16[3,512,1024]{2,1,0:T(8,128)(2,1)}, bf16[1024,512]{1,0:T(8,128)(2,1)}, bf16[1024,512]{1,0:T(8,128)(2,1)}, f...) custom-call(s32[1]{0:T(128)} %bitcast.3._seq, f32[3,2,512]{2,1,0:T(2,128)} %get-tuple-element.59.st_ref, ...), custom_call_target="tpu_custom_call" | custom-call | flops 6442450944 | bytes 31457280 | tf_op jit(solution)/shard_map/gate/pallas_call | solution.py:1241
  136.7 108.0 %scan_back.1 = (bf16[512,1024]{1,0:T(8,128)(2,1)}, bf16[1024,640]{1,0:T(8,128)(2,1)}, bf16[1024,256]{1,0:T(8,128)(2,1)}, f32[16,512]{1,0:T(8,128)}, f32[16,512]{...) custom-call(s32[1]{0:T(128)} %bitcast.3._seq, ...), custom_call_target="tpu_custom_call" | custom-call | flops 15300820992 | bytes 25165824 | tf_op jit(solution)/shard_map/scan_back/pallas_call | solution.py:1302
  244.7 98.1 %tail.1 = (bf16[1024,640]{1,0:T(8,128)(2,1)}, bf16[1024,256]{1,0:T(8,128)(2,1)}, f32[16,512]{1,0:T(8,128)}, f32[8,1024]{1,0:T(8,128)}, bf16[256,1024]{1,0:T(8,12...) custom-call(bf16[1024,640]{1,0:T(8,128)(2,1)} %get-tuple-element.75., ...), custom_call_target="tpu_custom_call" | custom-call | tf_op jit(solution)/shard_map/tail/pallas_call | solution.py:1388
  342.9 1.3 slice.55
  344.1 1.3 slice.54
  345.4 1.4 slice.50
  346.8 1.2 slice_bitcast_fusion
  348.0 1.4 fusion.3
  349.4 1.3 slice.52
  350.7 0.1 reshape_squeeze.7
  350.8 0.6 reduce_sum.9
  351.4 1.0 slice_convert_fusion
  352.4 0.8 copy.38
  353.2 2.1 convert_element_type.12
  355.3 7.5 %unpack.1 = (f32[1024,2,512]{2,1,0:T(2,128)}, f32[512,1024]{1,0:T(8,128)}) custom-call(bf16[1024,512]{1,0:T(8,128)(2,1)} %get-tuple-element.94.gz_ref, bf16[1024,512]{1,0:T(8,128)(2,1)} %get-tuple-element.95.go_ref, bf16[1024,640]{1,0:T(8,128)(2,1)} %get-tuple-element.96.gw_ref), custom_call_target="tpu_custom_call" | custom-call | tf_op jit(solution)/shard_map/unpack/pallas_call | solution.py:1463
  362.8 17.3 %finish.1 = (f32[6,2,256,1024]{3,2,1,0:T(8,128)}, bf16[6,2,256,1024]{3,2,1,0:T(8,128)(2,1)}) custom-call(s32[2]{0:T(128)} %pad_add_fusion._idx, bf16[6,2,256,1024]{3,2,1,0:T(8,128)(2,1)} %bitcast.41, bf16[2,256,1024]{2,1,0:T(8,128)(2,1)} %get-tuple-element.74.corr_ref.refs_0_, bf16[2,256,1024]{2,1,0:T(8,128)(2,1)} %bitcast.45, ...), custom_call_target="tpu_custom_call" | custom-call | bytes 37748736 | tf_op jit(solution)/shard_map/finish/pallas_call | solution.py:1448
  (27 shorter events, 0.1 us)
Async XLA Ops:
  6.3 2.3 copy-start.8
  6.3 2.4 copy-start.10
  6.3 2.4 copy-start.9
  6.3 2.5 copy-start.3
  6.3 2.5 copy-start.5
  6.3 2.5 copy-start.6
  6.3 2.6 copy-start.2
  8.0 6.2 %copy-start.4 = (f32[4,256]{1,0:T(4,128)S(1)}, f32[4,256]{1,0:T(4,128)}, u32[]{:S(2)}) copy-start(f32[4,256]{1,0:T(4,128)} %param.22) | copy-start | bytes 12292
  8.0 6.2 %copy-start.7 = (f32[256]{0:T(256)S(1)}, f32[256]{0:T(256)}, u32[]{:S(2)}) copy-start(f32[256]{0:T(256)} %param.23) | copy-start | bytes 3076
  8.0 3.0 collective-permute-start
  8.8 6.8 %collective-permute-start.4 = (f32[8,512]{1,0:T(8,128)S(1)}, f32[8,512]{1,0:T(8,128)S(1)}, u32[]{:S(2)}, u32[]{:S(2)}) collective-permute-start(f32[8,512]{1,0:T(8,128)S(1)} %concatenate.25), channel_id=1, source_target_pairs={{0,1},{1,0},{2,3},{3,2},{4,5},{5,4},{6,7},{7,6},{8,9},{9,8},{10,11... | collective-permute-start | bytes 49160 | tf_op jit(solution)/shard_map/ppermute | solution.py:1149
  8.9 7.0 %collective-permute-start.2 = (bf16[1024,8]{0,1:T(8,128)(2,1)S(1)}, bf16[1024,8]{0,1:T(8,128)(2,1)S(1)}, u32[]{:S(2)}, u32[]{:S(2)}) collective-permute-start(bf16[1024,8]{0,1:T(8,128)(2,1)S(1)} %copy-done.2), channel_id=1, source_target_pairs={{0,1},{1,0},{2,3},{3,2},{4,5},{5,4},{6,7},{7,6},{8,9},{9,8},{10,11... | collective-permute-start | bytes 49160 | tf_op jit(solution)/shard_map/ppermute | solution.py:1149
  9.4 7.9 %collective-permute-start.3 = (bf16[512,1024]{1,0:T(8,128)(2,1)}, bf16[512,1024]{1,0:T(8,128)(2,1)}, u32[]{:S(2)}, u32[]{:S(2)}) collective-permute-start(bf16[512,1024]{1,0:T(8,128)(2,1)} %param.28), channel_id=1, source_target_pairs={{0,1},{1,0},{2,3},{3,2},{4,5},{5,4},{6,7},{7,6},{8,9},{9,8},{10,11... | collective-permute-start | bytes 3145736 | tf_op jit(solution)/shard_map/ppermute | solution.py:1149
  12.1 5.2 %copy-start = (bf16[512,1024]{1,0:T(8,128)(2,1)S(1)}, bf16[512,1024]{1,0:T(8,128)(2,1)}, u32[]{:S(2)}) copy-start(bf16[512,1024]{1,0:T(8,128)(2,1)} %param.28) | copy-start | bytes 3145732
  13.9 7.2 %copy-start.1 = (bf16[1024,256]{1,0:T(8,128)(2,1)S(1)}, bf16[1024,256]{1,0:T(8,128)(2,1)}, u32[]{:S(2)}) copy-start(bf16[1024,256]{1,0:T(8,128)(2,1)} %param.18) | copy-start | bytes 1572868
  13.9 6.1 %collective-permute-start.1 = (bf16[1024,512]{1,0:T(8,128)(2,1)}, bf16[1024,512]{1,0:T(8,128)(2,1)S(1)}, u32[]{:S(2)}, u32[]{:S(2)}) collective-permute-start(bf16[1024,512]{1,0:T(8,128)(2,1)} %get-tuple-element.132), channel_id=1, source_target_pairs={{0,1},{1,0},{2,3},{3,2},{4,5},{5,4},{6,7},{7,6},{8,9},{9,8},{10,11... | collective-permute-start | bytes 3145736 | tf_op jit(solution)/shard_map/ppermute | solution.py:1149

commit v2 on v1

--- a/solution.py
+++ b/solution.py
@@ -235,21 +235,37 @@
     return r * (dn - normed * jnp.mean(dn * normed, axis=1, keepdims=True))
 
 
+def places(ncore, ny):
+    spot = lax.axis_index("tensor")
+    core, yy = lax.rem(spot, ncore), spot // ncore
+    ys = [lax.rem(yy + d, ny) for d in range(1, ny)]
+    peers = [{"tensor": v * ncore + core} for v in ys]
+    return core, yy, {"tensor": spot + 1 - 2 * core}, ys, peers
+
+
 def log2(n):
     return n.bit_length() - 1
 
 
 def forward_kernel(
-    width,
+    own,
+    heads,
+    ncore,
+    ny,
+    inner_total,
+    nloc,
     _seq,
     x_ref,
     g_ref,
     gain_ref,
-    w_ref,
+    wz_ref,
+    wx_ref,
+    wbc_ref,
+    wdt_ref,
     wo_ref,
-    prm_ref,
+    sm_ref,
     bcp_ref,
-    hp_ref,
+    x4_ref,
     hid_ref,
     z_ref,
     xl_ref,
@@ -259,16 +275,91 @@
     y_ref,
     sin_ref,
     st_ref,
+    stot_ref,
     po_ref,
+    bo_ref,
+    prm_ref,
+    hp_ref,
+    wdt_out,
+    wz_out,
+    wx_out,
     q_scr,
     bca_scr,
     s_scr,
     cs_scr,
     xs_scr,
+    wz_in,
+    wx_in,
+    wo_in,
+    wdt_in,
+    sm_in,
+    po_scr,
+    po_in,
+    st_in,
+    x_own,
+    w_sems,
+    po_sems,
+    st_sems,
+    local,
 ):
     rows_all = x_ref.shape[0]
     model = x_ref.shape[1]
+    width = own * ncore
     pairs = width // L
+    Ry = rows_all // ny
+    here = pl.program_id(0)
+    core, yy, twin, ys, peers = places(ncore, ny)
+
+    def weight_copies():
+        both = ((sm_ref, sm_in), (wdt_ref, wdt_in), (wz_ref, wz_in), (wx_ref, wx_in), (wo_ref, wo_in))
+        return [
+            remote(src, dst, w_sems.at[0, k], w_sems.at[1, k], twin)
+            for k, (src, dst) in enumerate(both)
+        ]
+
+    def weight_stores():
+        return [
+            pltpu.make_async_copy(wz_in, wz_out, local.at[1]),
+            pltpu.make_async_copy(wx_in, wx_out, local.at[2]),
+        ]
+
+    def row_copies():
+        last = here - 1
+        return [
+            remote(
+                st_ref.at[last],
+                st_in.at[last, d],
+                st_sems.at[0, last, d],
+                st_sems.at[1, last, d],
+                peers[d],
+            )
+            for d in range(ny - 1)
+        ] + [
+            remote(
+                po_scr.at[pl.ds(pl.multiple_of(ys[d] * Ry, Ry), Ry)],
+                po_in.at[last, d],
+                po_sems.at[0, last, d],
+                po_sems.at[1, last, d],
+                peers[d],
+            )
+            for d in range(ny - 1)
+        ]
+
+    def x_copy():
+        return pltpu.make_async_copy(x4_ref.at[core * nloc + here - 1, yy], x_own, local.at[0])
+
+    @pl.when(here == 0)
+    def _():
+        greet(peers + ([twin] if ncore == 2 else []))
+        if ncore == 2:
+            for copy in weight_copies():
+                copy.start()
+
+    @pl.when(here > 0)
+    def _():
+        for copy in row_copies():
+            copy.start()
+        x_copy().start()
 
     @pl.loop(0, rows_all // 32)
     def _(i):
@@ -280,24 +371,36 @@
     xl_ref[0:PAD, :] = jnp.zeros((PAD, width), f32)
     bcl_ref[0:PAD, :] = jnp.zeros((PAD, 256), f32)
 
-    @pl.loop(0, width // 256)
-    def _(j):
-        cols = pl.ds(pl.multiple_of(j * 256, 256), 256)
-        z_ref[:, cols] = nn(hid_ref[...], w_ref[:, cols])
-
-    @pl.loop(0, width // 256)
-    def _(j):
-        cols = pl.ds(pl.multiple_of(j * 256, 256), 256)
-        wcols = pl.ds(pl.multiple_of(width + j * 256, 256), 256)
-        xl_ref[PAD : PAD + rows_all, cols] = nn(hid_ref[...], w_ref[:, wcols])
-
-    bcl_ref[PAD : PAD + rows_all, :] = nn(hid_ref[...], w_ref[:, 2 * width : 2 * width + 256])
-    dtl_ref[...] = nn(hid_ref[...], w_ref[:, 2 * width + 256 : 2 * width + 384])
-
-    @pl.loop(0, width // 256)
-    def _(j):
-        cols = pl.ds(pl.multiple_of(j * 256, 256), 256)
-        u_ref[:, cols] = nt(g_ref[...], wo_ref[cols, :])
+    def project(wz, wx, wo, base):
+        @pl.loop(0, own // 256)
+        def _(j):
+            src = pl.ds(pl.multiple_of(j * 256, 256), 256)
+            cols = pl.ds(pl.multiple_of(base + j * 256, 256), 256)
+            z_ref[:, cols] = nn(hid_ref[...], wz[:, src])
+            xl_ref[PAD : PAD + rows_all, cols] = nn(hid_ref[...], wx[:, src])
+            u_ref[:, cols] = nt(g_ref[...], wo[src, :])
+
+    project(wz_ref, wx_ref, wo_ref, 0)
+    bcl_ref[PAD : PAD + rows_all, :] = nn(hid_ref[...], wbc_ref[...])
+
+    @pl.when(here == 0)
+    def _():
+        prm_ref[:, 0:own] = sm_ref[0:8, :]
+        hp_ref[...] = sm_ref[8:16, 0:L]
+        wdt_out[...] = wdt_ref[...]
+        if ncore == 2:
+            for copy in weight_copies():
+                copy.wait()
+            for copy in weight_stores():
+                copy.start()
+            prm_ref[:, own : 2 * own] = sm_in[0:8, :]
+            hp_ref[...] += pltpu.roll(sm_in[8:16, 0:L], heads, axis=1)
+            theirs = pltpu.roll(wdt_in[...].astype(f32), heads, axis=1)
+            wdt_out[...] = (wdt_ref[...].astype(f32) + theirs).astype(bf16)
+
+    if ncore == 2:
+        project(wz_in, wx_in, wo_in, own)
+    dtl_ref[...] = nn(hid_ref[...], wdt_out[...])
 
     @pl.loop(0, rows_all // L)
     def _(c):
@@ -358,12 +461,52 @@
         s1 = jnp.sum(inner, axis=1, keepdims=True)
         lane = lane_iota((L, L))
         stat = jnp.where(lane == 0, s0, jnp.where(lane == 1, s1, 0.0))
-        st_ref[:, rows] = stat.T[0:2]
+        st_ref[here, :, rows] = stat.T[0:2]
+
+    @pl.when(here > 0)
+    def _():
+        for copy in row_copies():
+            copy.wait()
+        x_copy().wait()
+        total = st_ref[here - 1]
+        for d in range(ny - 1):
+            total = total + st_in[here - 1, d]
+        stot_ref[here - 1] = total
+        parts = [po_in.at[here - 1, d] for d in range(ny - 1)]
+        mine = po_scr.at[pl.ds(pl.multiple_of(yy * Ry, Ry), Ry)]
+        block_out(inner_total, stot_ref.at[here - 1], yy, mine, parts, x_own, bo_ref.at[here - 1])
 
     @pl.loop(0, model // 256)
     def _(j):
         cols = pl.ds(pl.multiple_of(j * 256, 256), 256)
-        po_ref[:, cols] = nn(q_scr[...], wo_ref[:, cols]).astype(bf16)
+        po = nn(q_scr[:, 0:own], wo_ref[:, cols])
+        if ncore == 2:
+            po = po + nn(q_scr[:, own : 2 * own], wo_in[:, cols])
+        po_scr[:, cols] = po.astype(bf16)
+
+    @pl.when(here == nloc - 1)
+    def _():
+        po_ref[...] = po_scr[...]
+        if ncore == 2:
+            for copy in weight_stores():
+                copy.wait()
+
+
+def block_out(inner_total, stot, yy, mine, parts, x_own, bo):
+    Ry, model = x_own.shape
+    for h in range(Ry // L):
+        lanes = pl.ds(pl.multiple_of(yy * Ry + h * L, L), L)
+        r_row = lax.rsqrt(stot[0:1, lanes] / inner_total + epsilon)
+        r = jnp.broadcast_to(r_row, (8, L)).T[:, 0:1]
+
+        @pl.loop(0, model // L)
+        def _(m, h=h, r=r):
+            cols = pl.ds(pl.multiple_of(m * L, L), L)
+            rows = slice(h * L, h * L + L)
+            total = mine[rows, cols].astype(f32)
+            for part in parts:
+                total = total + part[rows, cols].astype(f32)
+            bo[rows, cols] = (x_own[rows, cols].astype(f32) + r * total).astype(bf16)
 
 
 def gate_kernel(
@@ -374,6 +517,7 @@
     ny,
     _seq,
     st_ref,
+    stin_ref,
     g_ref,
     hid_ref,
     z_ref,
@@ -381,6 +525,7 @@
     u_ref,
     prm_ref,
     po_ref,
+    bo01_ref,
     x_ref,
     dz_ref,
     dy_ref,
@@ -388,70 +533,69 @@
     go_ref,
     ggg_ref,
     bo_ref,
-    stot_ref,
     q_scr,
     sc_scr,
     acc_scr,
+    stot_ref,
     st_in,
     send_scr,
     recv_scr,
     po_in,
-    po_own,
     x_own,
-    st_send,
-    st_recv,
+    st_sems,
     core_send,
     core_recv,
-    po_send,
-    po_recv,
+    po_sems,
     local,
 ):
     rows_all = z_ref.shape[0]
+    model = g_ref.shape[1]
+    pairs = width // L
     here = pl.program_id(0)
-    spot = lax.axis_index("tensor")
-    core, yy = lax.rem(spot, ncore), spot // ncore
-    ys = [lax.rem(yy + d, ny) for d in range(1, ny)]
-    peers = [{"tensor": v * ncore + core} for v in ys]
-    twin = {"tensor": spot + 1 - 2 * core}
-    nloc, _, Ry, _ = po_ref.shape
+    core, yy, twin, ys, peers = places(ncore, ny)
+    nloc, Ry, _ = bo_ref.shape
+    last = nloc - 1
+
+    def row_copies():
+        return [
+            remote(st_ref.at[last], st_in.at[d], st_sems.at[0, d], st_sems.at[1, d], peers[d])
+            for d in range(ny - 1)
+        ]
 
     def po_copies():
         return [
-            remote(po_ref.at[:, ys[d]], po_in.at[d], po_send.at[d], po_recv.at[d], peers[d])
+            remote(
+                po_ref.at[pl.ds(pl.multiple_of(ys[d] * Ry, Ry), Ry)],
+                po_in.at[d],
+                po_sems.at[0, d],
+                po_sems.at[1, d],
+                peers[d],
+            )
             for d in range(ny - 1)
         ]
 
-    def own_copies():
-        return [
-            pltpu.make_async_copy(po_ref.at[:, yy], po_own, local.at[0]),
-            pltpu.make_async_copy(x_ref.at[pl.ds(core * nloc, nloc), yy], x_own, local.at[1]),
-        ]
+    def x_copy():
+        return pltpu.make_async_copy(x_ref.at[core * nloc + last, yy], x_own, local.at[0])
 
     @pl.when(here == 0)
     def _():
         greet(peers + ([twin] if ncore == 2 else []))
-        copies = [
-            remote(st_ref, st_in.at[d], st_send.at[d], st_recv.at[d], peers[d])
-            for d in range(ny - 1)
-        ]
-        for copy in copies:
+        for copy in row_copies() + po_copies() + [x_copy()]:
             copy.start()
-        for copy in copies:
+        stot_ref[...] = stin_ref[...]
+        for i in range(last):
+            bo_ref[i] = bo01_ref[i]
+        acc_scr[...] = jnp.zeros_like(acc_scr)
+        ggg_ref[...] = jnp.zeros_like(ggg_ref)
+
+    @pl.when(here == last)
+    def _():
+        for copy in row_copies():
             copy.wait()
-        total = st_ref[...]
+        total = st_ref[last]
         for d in range(ny - 1):
             total = total + st_in[d]
-        stot_ref[...] = total
-        for copy in po_copies() + own_copies():
-            copy.start()
-
-    model = g_ref.shape[1]
-    pairs = width // L
-
-    @pl.when(pl.program_id(0) == 0)
-    def _():
-        acc_scr[...] = jnp.zeros_like(acc_scr)
-        ggg_ref[...] = jnp.zeros_like(ggg_ref)
+        stot_ref[last] = total
 
     @pl.loop(0, rows_all // L)
     def _(c):
@@ -500,22 +644,11 @@
         gz_ref[...] = (acc_scr[:, 0:own] + theirs[:, 0:own]).astype(bf16)
         mine = acc_scr[:, width : width + own] + theirs[:, own : 2 * own]
         go_ref[...] = mine.astype(bf16)
-        for copy in po_copies() + own_copies():
+        for copy in po_copies() + [x_copy()]:
             copy.wait()
-        for i in range(nloc):
-            for h in range(Ry // L):
-                lanes = pl.ds(pl.multiple_of(yy * Ry + h * L, L), L)
-                r_row = lax.rsqrt(stot_ref[i, 0:1, lanes] / inner_total + epsilon)
-                r = jnp.broadcast_to(r_row, (8, L)).T[:, 0:1]
-
-                @pl.loop(0, model // L)
-                def _(m, i=i, h=h, r=r):
-                    cols = pl.ds(pl.multiple_of(m * L, L), L)
-                    rows = slice(h * L, h * L + L)
-                    total = po_own[i, rows, cols].astype(f32)
-                    for d in range(ny - 1):
-                        total = total + po_in[d, i, rows, cols].astype(f32)
-                    bo_ref[i, rows, cols] = (x_own[i, rows, cols].astype(f32) + r * total).astype(bf16)
+        parts = [po_in.at[d] for d in range(ny - 1)]
+        mine = po_ref.at[pl.ds(pl.multiple_of(yy * Ry, Ry), Ry)]
+        block_out(inner_total, stot_ref.at[last], yy, mine, parts, x_own, bo_ref.at[last])
 
 
 def scan_kernel(
@@ -534,7 +667,12 @@
     bcl_ref,
     dtl_ref,
     sin_ref,
-    w_ref,
+    wz_ref,
+    wzo_ref,
+    wx_ref,
+    wxo_ref,
+    wbc_ref,
+    wdt_ref,
     prm_ref,
     bcp_ref,
     hp_ref,
@@ -556,6 +694,9 @@
     boy_ref,
     bot_ref,
     boty_ref,
+    cy_ref,
+    ct_ref,
+    cty_ref,
     d_scr,
     bcc_scr,
     bca_scr,
@@ -581,6 +722,7 @@
     core_recv,
     y_sems,
     bo_sems,
+    c_sems,
     local,
     *machine,
 ):
@@ -591,11 +733,7 @@
     Ry = rows_all // ny
     seq, back = pl.program_id(0), pl.program_id(1)
     step = seq * spans + back
-    spot = lax.axis_index("tensor")
-    core, yy = lax.rem(spot, ncore), spot // ncore
-    twin = {"tensor": spot + 1 - 2 * core}
-    ys = [lax.rem(yy + d, ny) for d in range(1, ny)]
-    peers = [{"tensor": v * ncore + core} for v in ys]
+    core, yy, twin, ys, peers = places(ncore, ny)
     nbits = log2(ndp)
     dp_peers, dp_bits = bit_peers("dp", 1, 0, nbits)
     links = list(zip(dp_peers, dp_bits))
@@ -651,10 +789,11 @@
         gdt_ref[...] = jnp.zeros_like(gdt_ref)
         gpre_ref[...] = jnp.zeros_like(gpre_ref)
 
-    events = 2 * nbits + 1
-    for j in range(events):
-
-        @pl.when(step == (j * last_step + nbits) // (events - 1))
+    spans_of = ([2] + [1] * (nbits - 2) + [2])[:nbits]
+    spans_of = spans_of + spans_of[::-1]
+    for j in range(2 * nbits + 1):
+
+        @pl.when(step == sum(spans_of[:j]) * last_step // sum(spans_of))
         def _(j=j):
             for job in jobs:
                 job.close(j)
@@ -667,6 +806,44 @@
             copy.wait()
         for copy in bo_second():
             copy.start()
+
+    def corr_first(i):
+        out = [
+            remote(corr_ref.at[i], cy_ref.at[d, i], c_sems.at[0, i, d], c_sems.at[1, i, d], peers[d])
+            for d in range(ny - 1)
+        ]
+        if ncore == 2:
+            d = ny - 1
+            out.append(remote(corr_ref.at[i], ct_ref.at[i], c_sems.at[0, i, d], c_sems.at[1, i, d], twin))
+        return out
+
+    def corr_second(i):
+        if ncore != 2:
+            return []
+        return [
+            remote(
+                cy_ref.at[d, i],
+                cty_ref.at[d, i],
+                c_sems.at[0, i, ny + d],
+                c_sems.at[1, i, ny + d],
+                twin,
+            )
+            for d in range(ny - 1)
+        ]
+
+    for i in range(nloc_static - 2):
+
+        @pl.when(step == (i + 2) * spans - 1)
+        def _(i=i):
+            for copy in corr_first(i):
+                copy.start()
+
+        @pl.when(step == (i + 2) * spans + 2)
+        def _(i=i):
+            for copy in corr_first(i):
+                copy.wait()
+            for copy in corr_second(i):
+                copy.start()
 
     @pl.when(jnp.logical_and(seq > 0, back == 0))
     def _():
@@ -823,7 +1000,12 @@
         @pl.loop(0, model // 256)
         def _(j):
             cols = pl.ds(pl.multiple_of(j * 256, 256), 256)
-            dh = nt(dz_ref[...], w_ref[cols, 0:width]) + nt(d_scr[...], w_ref[cols, width:])
+            dh = nt(dz_ref[:, 0:own], wz_ref[cols, :]) + nt(d_scr[:, 0:own], wx_ref[cols, :])
+            if ncore == 2:
+                dh = dh + nt(dz_ref[:, own:width], wzo_ref[cols, :])
+                dh = dh + nt(d_scr[:, own:width], wxo_ref[cols, :])
+            dh = dh + nt(d_scr[:, width : width + 256], wbc_ref[cols, :])
+            dh = dh + nt(d_scr[:, width + 256 :], wdt_ref[cols, :])
             dh_scr[:, cols] = dh.astype(bf16)
             gpre_ref[:, cols] += fold_rows(dh * hid_ref[:, cols].astype(f32))
             acc_scr[cols, :] += tn(hid_ref[:, cols], d_scr[...])
@@ -867,6 +1049,9 @@
         gw_ref[:, own : own + L] = tail.astype(bf16)
         for copy in bo_second():
             copy.wait()
+        for i in range(nloc_static - 2):
+            for copy in corr_second(i):
+                copy.wait()
 
 
 def tail_kernel(
@@ -906,11 +1091,7 @@
 ):
     model = gw_ref.shape[0]
     Ry, nloc = x_own.shape[0], corr_ref.shape[0] + 1
-    spot = lax.axis_index("tensor")
-    core, yy = lax.rem(spot, ncore), spot // ncore
-    twin = {"tensor": spot + 1 - 2 * core}
-    ys = [lax.rem(yy + d, ny) for d in range(1, ny)]
-    peers = [{"tensor": v * ncore + core} for v in ys]
+    core, yy, twin, ys, peers = places(ncore, ny)
     nbits = log2(ndp)
     dp_peers, dp_bits = bit_peers("dp", 1, 0, nbits)
     t_peers, t_bits = bit_peers("tensor", 1, 0, log2(ncore * ny))
@@ -957,7 +1138,7 @@
             for d in range(ny - 1)
         ]
 
-    early = (corr_ref, cy_ref, ct_ref, c_sems)
+    early = (corr_ref.at[nloc - 2], cy_ref, ct_ref, c_sems)
     late = (last_ref, ly_ref, lt_ref, l_sems)
     x_copy = pltpu.make_async_copy(x_ref.at[core * nloc + nloc - 1, yy], x_own, local.at[0])
     others = peers + ([twin] if ncore == 2 else [])
@@ -971,11 +1152,11 @@
             job.begin(j)
 
     job_sh.acc[0] = shared_ref[...]
-    turn((job_c, 0), (job_a, 0), (job_b, 0))
+    turn((job_c, 0), (job_a, 0), (job_b, 0), (job_sh, 0))
     if ncore == 2:
         small_copy = remote(other_ref, small_in, core_sems.at[0], core_sems.at[1], twin)
         small_copy.start()
-    turn((job_c, 1), (job_sh, 0))
+    turn((job_c, 1), (job_sh, 1))
     for copy in dh_copies():
         copy.start()
     for copy in first(*early):
@@ -985,7 +1166,7 @@
         job_sm.acc[0] = small_ref[...] + small_in[...]
     else:
         job_sm.acc[0] = small_ref[...]
-    turn((job_sh, 1), (job_sm, 0))
+    turn((job_sm, 0))
     steps = [
         (job_c, iter(range(2, 2 * job_c.n + 1))),
         (job_sm, iter(range(1, len(job_sm.peers) + 1))),
@@ -1037,22 +1218,24 @@
 
 def finish_kernel(pieces, nloc, _idx, g_ref, *refs):
     gi_ref, bo_ref = refs[-2:]
-    early, late, outs = refs[:pieces], refs[pieces : 2 * pieces], refs[2 * pieces : 3 * pieces]
-    last = pl.program_id(1) == nloc - 1
+    groups = [refs[n * pieces : (n + 1) * pieces] for n in range(4)]
+    now = pl.program_id(1)
     for k in range(pieces):
         here = pl.program_id(0) == k
 
         @pl.when(here)
-        def _(src=outs[k]):
+        def _(src=groups[3][k]):
             bo_ref[...] = src[...]
 
-        @pl.when(jnp.logical_and(here, jnp.logical_not(last)))
-        def _(src=early[k]):
-            gi_ref[...] = g_ref[...].astype(f32) + src[...].astype(f32)
-
-        @pl.when(jnp.logical_and(here, last))
-        def _(src=late[k]):
-            gi_ref[...] = g_ref[...].astype(f32) + src[...].astype(f32)
+        for n in range(3):
+            if n == 0:
+                turn = now < nloc - 2
+            else:
+                turn = now == nloc - 3 + n
+
+            @pl.when(jnp.logical_and(here, turn))
+            def _(src=groups[n][k]):
+                gi_ref[...] = g_ref[...].astype(f32) + src[...].astype(f32)
 
 
 def unpack_kernel(own, gz_ref, go_ref, gw_ref, gzx_ref, gwo_ref):
@@ -1136,7 +1319,6 @@
     ny = nt // ncore
     width = own * ncore
     t = lax.axis_index("tensor")
-    me = lax.axis_index("dp")
     core, yy = t % ncore, t // ncore
     R = SEQ_LEN
     Ry = R // ny
@@ -1145,57 +1327,45 @@
     spans = R // L
     wtot = 2 * width + 384
 
-    def swap_core(v):
-        return lax.ppermute(v, "tensor", [(i, i ^ 1) for i in range(nt)])
-
-    def y_shift(v, d):
-        pairs = [(i, ((i // ncore + d) % ny) * ncore + i % ncore) for i in range(nt)]
-        return lax.ppermute(v, "tensor", pairs)
-
-    def dp_shift(v, d):
-        return lax.ppermute(v, "dp", [(i, (i + d) % ndp) for i in range(ndp)])
-
-    def both_cores(v, axis):
-        return jnp.concatenate([v, swap_core(v)], axis=axis) if ncore == 2 else v
-
     x3 = block_input.reshape(nseq, R, model)
     g3 = out_grad.reshape(nseq, R, model)
     x4 = block_input.reshape(nseq, ny, Ry, model)
     g4 = out_grad.reshape(nseq, ny, Ry, model)
     wz, wx = w_zx[:, 0], w_zx[:, 1]
-    rowp = jnp.concatenate(
+    sm = jnp.concatenate(
         [
             conv_x_w,
             conv_x_b[None],
             jnp.repeat(d_skip, HEAD)[None],
             gate_gain[None],
-            jnp.pad(jnp.concatenate([dt_bias, -jnp.exp(a_log)]), (0, own - 2 * heads))[None],
+            jnp.zeros((1, own), f32),
+            jnp.pad(jnp.stack([dt_bias, -jnp.exp(a_log)]), ((0, 6), (0, own - heads))),
         ],
         axis=0,
     )
-    prm = both_cores(rowp, 1)
-    hrow = prm[7].reshape(ncore, own)
-    hp = jnp.stack([hrow[:, :heads].reshape(-1), hrow[:, heads : 2 * heads].reshape(-1)])
-    hp = jnp.pad(hp, ((0, 6), (0, L - ncore * heads)))
-    wdt = jnp.pad(both_cores(w_dt, 1), ((0, 0), (0, L - ncore * heads)))
-    wcat = jnp.concatenate([both_cores(wz, 1), both_cores(wx, 1), w_bc, wdt], axis=1)
-    wo = both_cores(w_out, 0)
+    wdt = jnp.pad(w_dt, ((0, 0), (0, L - heads)))
     bcp = jnp.concatenate([conv_bc_w, conv_bc_b[None], jnp.zeros((3, 256), f32)], axis=0)
     gain = pre_gain[None]
-    seq0 = jnp.array([core * nloc], jnp.int32)
-
-    hid, z, xl, bcl, dtl, u, y, sin, st, po = call(
-        partial(forward_kernel, width),
+    seq0 = jnp.zeros((1,), jnp.int32)
+    any_spec = pl.BlockSpec(memory_space=pl.ANY)
+    nother = max(ny - 1, 1)
+    dma = pltpu.SemaphoreType.DMA
+
+    hid, z, xl, bcl, dtl, u, y, sin, st, stot, po, bo01, prm, hp, wdt, wzo, wxo = call(
+        partial(forward_kernel, own, heads, ncore, ny, inner_total, nloc),
         (nloc,),
         [
             moved_spec(ncore, nloc, R, model),
             moved_spec(ncore, nloc, R, model),
             whole_spec(1, model),
-            whole_spec(model, wtot),
-            whole_spec(width, model),
-            whole_spec(8, width),
+            whole_spec(model, own),
+            whole_spec(model, own),
+            whole_spec(model, 256),
+            whole_spec(model, L),
+            whole_spec(own, model),
+            whole_spec(16, own),
             whole_spec(8, 256),
-            whole_spec(8, L),
+            any_spec,
         ],
         [
             seq_spec(R, model),
@@ -1206,8 +1376,15 @@
             seq_spec(R, width),
             seq_spec(R, width),
             seq_spec(spans, L, width),
-            seq_spec(2, R),
-            seq_spec(R, model),
+            whole_spec(nloc, 2, R),
+            whole_spec(nloc, 2, R),
+            whole_spec(R, model),
+            whole_spec(nloc - 1, Ry, model),
+            whole_spec(8, width),
+            whole_spec(8, L),
+            whole_spec(model, L),
+            any_spec,
+            any_spec,
         ],
         [
             sds(nloc, R, model, dtype=bf16),
@@ -1219,7 +1396,14 @@
             sds(nloc, R, width),
             sds(nloc, spans, L, width, dtype=bf16),
             sds(nloc, 2, R),
-            sds(nloc, R, model, dtype=bf16),
+            sds(nloc, 2, R),
+            sds(R, model, dtype=bf16),
+            sds(nloc - 1, Ry, model, dtype=bf16),
+            sds(8, width),
+            sds(8, L),
+            sds(model, L, dtype=bf16),
+            sds(model, own, dtype=bf16),
+            sds(model, own, dtype=bf16),
         ],
         [
             pltpu.VMEM((R, width), bf16),
@@ -1227,21 +1411,32 @@
             pltpu.VMEM((L, width), f32),
             pltpu.VMEM((L, width), f32),
             pltpu.VMEM((L, width), bf16),
+            pltpu.VMEM((model, own), bf16),
+            pltpu.VMEM((model, own), bf16),
+            pltpu.VMEM((own, model), bf16),
+            pltpu.VMEM((model, L), bf16),
+            pltpu.VMEM((16, own), f32),
+            pltpu.VMEM((R, model), bf16),
+            pltpu.VMEM((nloc - 1, nother, Ry, model), bf16),
+            pltpu.VMEM((nloc - 1, nother, 2, R), f32),
+            pltpu.VMEM((Ry, model), bf16),
+            dma((2, 5)),
+            dma((2, nloc - 1, nother)),
+            dma((2, nloc - 1, nother)),
+            dma((3,)),
         ],
         "forward",
         2 * nloc * R * model * (wtot + 2 * width),
         nloc * R * (6 * model + 20 * width),
-    )(seq0, x3, g3, gain, wcat, wo, prm, bcp, hp)
-
-    any_spec = pl.BlockSpec(memory_space=pl.ANY)
+        4,
+    )(seq0, x3, g3, gain, wz, wx, w_bc, wdt, w_out, sm, bcp, x4)
+
     nbits = log2(ndp)
-    nother = max(ny - 1, 1)
-    dma = pltpu.SemaphoreType.DMA
-    po4 = po.reshape(nloc, ny, Ry, model)
-    dz, dy, gz, go, ggg, bo, st = call(
+    dz, dy, gz, go, ggg, bo = call(
         partial(gate_kernel, width, own, inner_total, ncore, ny),
         (nloc,),
         [
+            whole_spec(nloc, 2, R),
             whole_spec(nloc, 2, R),
             moved_spec(ncore, nloc, R, model),
             seq_spec(R, model),
@@ -1249,7 +1444,8 @@
             seq_spec(R, width),
             seq_spec(R, width),
             whole_spec(8, width),
-            any_spec,
+            whole_spec(R, model),
+            whole_spec(nloc - 1, Ry, model),
             any_spec,
         ],
         [
@@ -1259,7 +1455,6 @@
             whole_spec(model, own),
             whole_spec(8, width),
             whole_spec(nloc, Ry, model),
-            whole_spec(nloc, 2, R),
         ],
         [
             sds(nloc, R, width, dtype=bf16),
@@ -1268,38 +1463,36 @@
             sds(model, own, dtype=bf16),
             sds(8, width),
             sds(nloc, Ry, model, dtype=bf16),
-            sds(nloc, 2, R),
         ],
         [
             pltpu.VMEM((R, width), bf16),
             pltpu.VMEM((R, model), bf16),
             pltpu.VMEM((model, 2 * width), f32),
-            pltpu.VMEM((nother, nloc, 2, R), f32),
+            pltpu.VMEM((nloc, 2, R), f32),
+            pltpu.VMEM((nother, 2, R), f32),
             pltpu.VMEM((model, 2 * own), bf16),
             pltpu.VMEM((model, 2 * own), bf16),
-            pltpu.VMEM((nother, nloc, Ry, model), bf16),
-            pltpu.VMEM((nloc, Ry, model), bf16),
-            pltpu.VMEM((nloc, Ry, model), bf16),
-            dma((nother,)),
-            dma((nother,)),
+            pltpu.VMEM((nother, Ry, model), bf16),
+            pltpu.VMEM((Ry, model), bf16),
+            dma((2, nother)),
             dma,
             dma,
-            dma((nother,)),
-            dma((nother,)),
-            dma((2,)),
+            dma((2, nother)),
+            dma((1,)),
         ],
         "gate",
         4 * nloc * R * model * width,
         nloc * R * (4 * model + 16 * width),
         1,
-    )(seq0, st, g3, hid, z, y, u, prm, po4, x4)
+    )(seq0, st, stot, g3, hid, z, y, u, prm, po, bo01, x4)
 
     def chunk_spec(*shape):
         zeros = (0,) * len(shape)
         return pl.BlockSpec((None,) + shape, lambda i, b, s: (i,) + zeros)
 
     bc_type = bf16 if (model // (nt * ndp)) % 16 == 0 else f32
-    dh, gw2, gbcw, small, other, shared, corr, fz, fo, boy, bot, boty = call(
+    early_n = max(nloc - 2, 1)
+    dh, gw2, gbcw, small, other, shared, corr, fz, fo, boy, bot, boty, cy0, ct0, cty0 = call(
         partial(scan_kernel, width, own, heads, ncore, ny, ndp, nloc),
         (nloc, spans),
         [
@@ -1310,7 +1503,12 @@
             chunk_spec(R + PAD, 256),
             chunk_spec(R, L),
             chunk_spec(spans, L, width),
-            pl.BlockSpec((model, wtot), lambda i, b, s: (0, 0), pipeline_mode=pl.Buffered(1)),
+            whole_spec(model, own),
+            whole_spec(model, own),
+            whole_spec(model, own),
+            whole_spec(model, own),
+            whole_spec(model, 256),
+            whole_spec(model, L),
             whole_spec(8, width),
             whole_spec(8, 256),
             whole_spec(8, L),
@@ -1330,7 +1528,7 @@
             whole_spec(8, model),
             whole_spec(nloc - 1, Ry, model),
         ]
-        + [any_spec] * 5,
+        + [any_spec] * 8,
         [
             sds(R, model, dtype=bf16),
             sds(model, own + L, dtype=bf16),
@@ -1344,6 +1542,9 @@
             sds(nother, nloc, Ry, model, dtype=bf16),
             sds(nloc, Ry, model, dtype=bf16),
             sds(nother, nloc, Ry, model, dtype=bf16),
+            sds(nother, early_n, Ry, model, dtype=bf16),
+            sds(early_n, Ry, model, dtype=bf16),
+            sds(nother, early_n, Ry, model, dtype=bf16),
         ],
         [
             pltpu.VMEM((R, width + 384), bf16),
@@ -1371,6 +1572,7 @@
             dma,
             dma((2, nloc - 1, nother)),
             dma((2, 2 * ny)),
+            dma((2, early_n, 2 * ny)),
             dma((1,)),
         ]
         + Halving.scratch(model, own, nbits, bf16)
@@ -1379,11 +1581,10 @@
         2 * nloc * R * model * (2 * wtot),
         nloc * R * (4 * model + 12 * width),
         2,
-    )(seq0, hid, dz, dy, xl, bcl, dtl, sin, wcat, prm, bcp, hp, ggg, gain, gz, go, bo, x4)
+    )(seq0, hid, dz, dy, xl, bcl, dtl, sin, wz, wzo, wx, wxo, w_bc, wdt, prm, bcp, hp, ggg, gain, gz, go, bo, x4)
 
     vm = pl.BlockSpec(memory_space=pltpu.VMEM)
     tbits = log2(nt)
-    early_shape = sds(nother, nloc - 1, Ry, model, dtype=bf16)
     late_shape = sds(nother, Ry, model, dtype=bf16)
     fw, fb, small, shared, last, cy, ct, cty, ly, lt, lty = pl.pallas_call(
         partial(tail_kernel, own, ncore, ny, ndp),
@@ -1395,9 +1596,9 @@
             sds(16, own),
             sds(8, model),
             sds(Ry, model, dtype=bf16),
-            early_shape,
-            sds(nloc - 1, Ry, model, dtype=bf16),
-            early_shape,
+            late_shape,
+            sds(Ry, model, dtype=bf16),
+            late_shape,
             late_shape,
             sds(Ry, model, dtype=bf16),
             late_shape,
@@ -1427,38 +1628,55 @@
     def out_index(k, i, s):
         return ((s[0] ^ (k // ny)) * nloc + i, (s[1] - k % ny + ny) % ny, 0, 0)
 
-    def piece_spec(k, count):
-        def index(j, i, s):
-            i = jnp.minimum(i, count - 1)
-            return (jnp.where(j == k, i, jnp.where(j > k, count - 1, 0)), 0, 0)
-
-        return pl.BlockSpec((None, Ry, model), index)
+    def spec_of(base, seq_of, d):
+        if d is None:
+            return pl.BlockSpec(
+                (None, Ry, model), lambda j, i, s: (seq_of(j, i) - base, 0, 0)
+            )
+        return pl.BlockSpec(
+            (None, None, Ry, model), lambda j, i, s: (d, seq_of(j, i) - base, 0, 0)
+        )
 
     placed_spec = pl.BlockSpec((None, None, Ry, model), out_index)
-
-    def all_pieces(mine, toy, tot, toty):
-        got = [mine] + [toy[d] for d in range(ny - 1)]
-        if ncore == 2:
-            got = got + [tot] + [toty[d] for d in range(ny - 1)]
-        return got
-
-    early = all_pieces(corr, cy, ct, cty)
-    late = all_pieces(last[None], ly[:, None], lt[None], lty[:, None])
-    outs = all_pieces(bo, boy, bot, boty)
+    specs, arrays = [], []
+
+    def add_group(first, count, mine, mine_base, toy, tot, toty):
+        for k in range(pieces):
+
+            def seq_of(j, i, k=k):
+                i = jnp.clip(i, first, first + count - 1)
+                return jnp.where(j == k, i, jnp.where(j > k, first + count - 1, first))
+
+            d = k % ny - 1
+            if k == 0:
+                array, spec = mine, spec_of(mine_base, seq_of, None)
+            elif k < ny:
+                array, spec = toy, spec_of(first, seq_of, d)
+            elif d < 0:
+                array, spec = tot, spec_of(first, seq_of, None)
+            else:
+                array, spec = toty, spec_of(first, seq_of, d)
+            arrays.append(array)
+            specs.append(spec)
+
+    def as_seq(v, axis):
+        return jnp.expand_dims(v, axis)
+
+    add_group(0, early_n, corr, 0, cy0, ct0, cty0)
+    add_group(nloc - 2, 1, corr, 0, as_seq(cy, 1), as_seq(ct, 0), as_seq(cty, 1))
+    add_group(nloc - 1, 1, as_seq(last, 0), nloc - 1, as_seq(ly, 1), as_seq(lt, 0), as_seq(lty, 1))
+    add_group(0, nloc, bo, 0, boy, bot, boty)
     grad_input, block_output = call(
         partial(finish_kernel, pieces, nloc),
         (pieces, nloc),
-        [placed_spec]
-        + [piece_spec(k, nloc - 1) for k in range(pieces)]
-        + [piece_spec(k, 1) for k in range(pieces)]
-        + [piece_spec(k, nloc) for k in range(pieces)],
+        [placed_spec] + specs,
         [placed_spec, placed_spec],
         [sds(nseq, ny, Ry, model), sds(nseq, ny, Ry, model, dtype=bf16)],
         [],
         "finish",
         0,
         12 * tok * model,
-    )(where, g4, *early, *late, *outs)
+    )(where, g4, *arrays)
 
     gzx, gwo = pl.pallas_call(
         partial(unpack_kernel, own),

time: 381 us -> 326 us (0.86)
  Pallas kernels: 345 us -> 301 us
  other arithmetic: 9.07 us -> 3.93 us
    pallas_call x1, Pallas kernels: 98.1 us -> 71.1 us  [body(): pl.pallas_call(partial(tail_kernel, own, ncore, ny, ndp), in_specs=[vm] *...]
    pallas_call x1, Pallas kernels: 51.9 us -> 30.4 us  [body(): call(partial(gate_kernel, width, own, inner_total, ncore, ny), (nloc,), [...]
    unnamed x28 -> x22, local copies, waits for them, and re-layouts: 7.38 us -> 1.01 us
    pallas_call x1, Pallas kernels: 62 us -> 66.2 us  [body(): call(partial(forward_kernel, own, heads, ncore, ny, inner_total, nloc), (...]
  transfers between devices with their start and end apart: 5 -> 0, of which waited for: 1 -> 0; matrix products, arithmetic and copies ran while one was open for 2% -> 0% of each run, Pallas kernels for 0% -> 0%
where the time goes in v2:
time: 326 us; the launch traced here: 325 us
  Pallas kernels  301 us (92%)
  local copies, waits for them, and re-layouts  18.7 us (6%)
  other arithmetic  3.93 us (1%)
    pallas_call x1, Pallas kernels, body(): call(partial(scan_kernel, width, own, heads, ncore, ny, ndp, nloc), (nloc...  109 us
    pallas_call x1, Pallas kernels, body(): pl.pallas_call(partial(tail_kernel, own, ncore, ny, ndp), in_specs=[vm] *...  71.1 us
    pallas_call x1, Pallas kernels, body(): call(partial(forward_kernel, own, heads, ncore, ny, inner_total, nloc), (...  66.2 us
    pallas_call x1, Pallas kernels, body(): call(partial(gate_kernel, width, own, inner_total, ncore, ny), (nloc,), [...  30.4 us
    pallas_call x1, Pallas kernels, body(): call(partial(finish_kernel, pieces, nloc), (pieces, nloc), [placed_spec]...  17.2 us
    pallas_call x1, Pallas kernels, body(): pl.pallas_call(partial(unpack_kernel, own), grid=(model // L,), in_specs=...  7.5 us

profile of v2, /device:TPU:0, one launch (start us, length us, event | category | flops | bytes accessed | tf_op | source)
XLA Modules:
  0.0 324.8 jit_solution(10491908765167606061)
XLA Ops:
  0.6 5.6 %fusion = (bf16[1024,1,512]{2,1,0:T(2,128)(2,1)S(1)}, bf16[1024,1,512]{2,1,0:T(2,128)(2,1)S(1)}) fusion(bf16[1024,2,512]{2,1,0:T(2,128)(2,1)} %param.17), kind=kLoop, calls=%fused_computation.12 | loop fusion | bytes 4194304 | tf_op jit(solution)/shard_map/slice | solution.py:1334
  6.3 0.0 copy-start.3
  6.3 0.0 copy-start.6
  6.3 0.0 copy-start.1
  6.3 0.0 copy-start.9
  6.3 0.0 copy-start.7
  6.3 0.0 copy-start.8
  6.3 0.0 copy-start.2
  6.3 0.0 copy-start.4
  6.4 0.0 copy-start.5
  6.4 1.9 copy_bitcast_fusion
  8.3 0.1 pad.12.clone
  8.4 0.0 copy-done.3
  8.4 0.0 copy-done.6
  8.4 0.7 maximum_maximum_fusion.bcp_ref
  9.0 0.0 copy-done.1
  9.0 0.2 copy.32
  9.2 0.8 pad.8.wdt_ref
  10.0 0.0 copy-done.9
  10.0 0.0 copy-done.7
  10.0 0.0 copy-done.8
  10.0 0.1 broadcast_in_dim.44
  10.1 0.1 broadcast_in_dim_reshape.3
  10.2 0.0 copy-done.2
  10.2 0.0 copy-done.4
  10.2 0.0 copy-done.5
  10.2 1.2 concatenate.6.sm_ref
  11.4 66.2 %forward.1 = (bf16[3,512,1024]{2,1,0:T(8,128)(2,1)}, f32[3,512,1024]{2,1,0:T(8,128)}, f32[3,520,1024]{2,1,0:T(8,128)}, f32[3,520,256]{2,1,0:T(8,128)}, f32[3,512...) custom-call(s32[1]{0:T(128)} %constant.35.clone.1._seq, ...), custom_call_target="tpu_custom_call" | custom-call | flops 14092861440 | bytes 40894464 | tf_op jit(solution)/shard_map/forward/pallas_call | solution.py:1354
  77.7 30.4 %gate.1 = (bf16[3,512,1024]{2,1,0:T(8,128)(2,1)}, bf16[3,512,1024]{2,1,0:T(8,128)(2,1)}, bf16[1024,512]{1,0:T(8,128)(2,1)}, bf16[1024,512]{1,0:T(8,128)(2,1)}, f...) custom-call(s32[1]{0:T(128)} %constant.35.clone.1._seq, f32[3,2,512]{2,1,0:T(2,128)} %get-tuple-element.69.st_ref, ...), custom_call_target="tpu_custom_call" | custom-call | flops 6442450944 | bytes 31457280 | tf_op jit(solution)/shard_map/gate/pallas_call | solution.py:1435
  108.1 108.9 %scan_back.1 = (bf16[512,1024]{1,0:T(8,128)(2,1)}, bf16[1024,640]{1,0:T(8,128)(2,1)}, bf16[1024,256]{1,0:T(8,128)(2,1)}, f32[16,512]{1,0:T(8,128)}, f32[16,512]{...) custom-call(s32[1]{0:T(128)} %constant.35.clone.1._seq, ...), custom_call_target="tpu_custom_call" | custom-call | flops 15300820992 | bytes 25165824 | tf_op jit(solution)/shard_map/scan_back/pallas_call | solution.py:1495
  217.0 71.1 %tail.1 = (bf16[1024,640]{1,0:T(8,128)(2,1)}, bf16[1024,256]{1,0:T(8,128)(2,1)}, f32[16,512]{1,0:T(8,128)}, f32[8,1024]{1,0:T(8,128)}, bf16[256,1024]{1,0:T(8,12...) custom-call(bf16[1024,640]{1,0:T(8,128)(2,1)} %get-tuple-element.95., ...), custom_call_target="tpu_custom_call" | custom-call | tf_op jit(solution)/shard_map/tail/pallas_call | solution.py:1589
  288.2 7.5 %unpack.1 = (f32[1024,2,512]{2,1,0:T(2,128)}, f32[512,1024]{1,0:T(8,128)}) custom-call(bf16[1024,512]{1,0:T(8,128)(2,1)} %get-tuple-element.114.gz_ref, bf16[1024,512]{1,0:T(8,128)(2,1)} %get-tuple-element.115.go_ref, bf16[1024,640]{1,0:T(8,128)(2,1)} %get-tuple-element.116.gw_ref), custom_call_target="tpu_custom_call" | custom-call | tf_op jit(solution)/shard_map/unpack/pallas_call | solution.py:1681
  295.7 0.6 pad_add_fusion._idx
  296.3 0.0 copy-start
  296.3 17.2 %finish.1 = (f32[6,2,256,1024]{3,2,1,0:T(8,128)}, bf16[6,2,256,1024]{3,2,1,0:T(8,128)(2,1)}) custom-call(s32[2]{0:T(128)} %pad_add_fusion._idx, bf16[6,2,256,1024]{3,2,1,0:T(8,128)(2,1)} %bitcast.41, bf16[2,256,1024]{2,1,0:T(8,128)(2,1)} %get-tuple-element.91.corr_ref.refs_0_.refs_4_, bf16[1,1,256,1024]{3,2,1,0:T(8,128)(2,1)} %get-tuple-element.92.refs_1_, ...), custom_call_target="tpu_custom_call" | custom-call | bytes 37748736 | tf_op jit(solution)/shard_map/finish/pallas_call | solution.py:1669
  313.4 0.0 copy-done
  313.4 1.0 convert_element_type.10
  314.5 1.0 slice_convert_fusion
  315.5 0.8 copy.33
  316.2 1.4 fusion.1
  317.7 0.1 reshape_squeeze.3
  317.7 0.6 reduce_sum.9
  318.4 1.3 slice.40
  319.7 1.4 slice.38
  321.0 1.3 slice.42
  322.3 1.2 slice_bitcast_fusion
  323.5 1.3 slice.43
  (4 shorter events, 0.0 us)
Async XLA Ops:
  6.3 2.1 copy-start.3
  6.3 2.1 copy-start.6
  6.3 2.8 copy-start.1
  6.3 3.7 %copy-start.9 = (f32[8]{0:T(128)S(1)}, f32[8]{0:T(128)}, u32[]{:S(2)}) copy-start(f32[8]{0:T(128)} %param.25) | copy-start | bytes 100
  6.3 3.7 %copy-start.7 = (f32[8]{0:T(128)S(1)}, f32[8]{0:T(128)}, u32[]{:S(2)}) copy-start(f32[8]{0:T(128)} %param.24) | copy-start | bytes 100
  6.3 3.7 %copy-start.8 = (f32[8]{0:T(128)S(1)}, f32[8]{0:T(128)}, u32[]{:S(2)}) copy-start(f32[8]{0:T(128)} %param.26) | copy-start | bytes 100
  6.3 3.8 %copy-start.2 = (f32[4,512]{1,0:T(4,128)S(1)}, f32[4,512]{1,0:T(4,128)}, u32[]{:S(2)}) copy-start(f32[4,512]{1,0:T(4,128)} %param.20) | copy-start | bytes 24580
  6.3 3.8 %copy-start.4 = (f32[512]{0:T(512)S(1)}, f32[512]{0:T(512)}, u32[]{:S(2)}) copy-start(f32[512]{0:T(512)} %param.21) | copy-start | bytes 6148
  6.4 3.8 %copy-start.5 = (f32[512]{0:T(512)S(1)}, f32[512]{0:T(512)}, u32[]{:S(2)}) copy-start(f32[512]{0:T(512)} %param.27) | copy-start | bytes 6148
  296.3 17.2 %copy-start = (bf16[1024,256]{1,0:T(8,128)(2,1)S(1)}, bf16[1024,256]{1,0:T(8,128)(2,1)}, u32[]{:S(2)}) copy-start(bf16[1024,256]{1,0:T(8,128)(2,1)} %get-tuple-element.118) | copy-start | bytes 1572868

commit v3 on v2

--- a/solution.py
+++ b/solution.py
@@ -10,6 +10,7 @@
 SEQ_LEN = 512
 L = 128
 HEAD = 64
+LOG2E = 1.4426950408889634
 PAD = 8
 epsilon = 1e-05
 f32 = jnp.float32
@@ -57,10 +58,15 @@
     return lax.broadcasted_iota(jnp.int32, shape, 0)
 
 
-def conv(window, taps, bias):
+def tap(win, k):
+    return win[PAD - 3 + k : PAD - 3 + k + L, :]
+
+
+def conv(ref, t0, win, lanes, taps, bias):
+    win[...] = ref[pl.ds(t0, L + PAD), lanes]
     total = bias
     for k in range(4):
-        total = total + window[PAD - 3 + k : PAD - 3 + k + L] * taps[k : k + 1]
+        total = total + tap(win, k) * taps[k : k + 1]
     return total
 
 
@@ -72,7 +78,7 @@
     pre = dtl + hp[0:1]
     dt = softplus(pre)
     ltri = (row_iota((L, L)) >= lane_iota((L, L))).astype(f32)
-    cum = exact(ltri, dt * hp[1:2])
+    cum = exact(ltri, dt * (hp[1:2] * LOG2E))
     return pre, dt, cum, cum.T
 
 
@@ -225,6 +231,45 @@
             pltpu.VMEM((n, rows, cols), f32),
             pltpu.SemaphoreType.DMA((2, n)),
         ]
+
+
+class Spread:
+    def __init__(self, src, toy, tot, toty, sems, place):
+        self.src, self.toy, self.tot, self.toty, self.sems = src, toy, tot, toty, sems
+        self.twin, self.peers, self.ncore = place
+
+    def first(self):
+        n = len(self.peers)
+        sems = self.sems
+        out = [
+            remote(self.src, self.toy.at[d], sems.at[0, d], sems.at[1, d], self.peers[d])
+            for d in range(n)
+        ]
+        if self.ncore == 2:
+            out.append(remote(self.src, self.tot, sems.at[0, n], sems.at[1, n], self.twin))
+        return out
+
+    def second(self):
+        n = len(self.peers)
+        if self.ncore != 2:
+            return []
+        sems = self.sems
+        return [
+            remote(
+                self.toy.at[d], self.toty.at[d], sems.at[0, n + 1 + d], sems.at[1, n + 1 + d], self.twin
+            )
+            for d in range(n)
+        ]
+
+
+def start(copies):
+    for copy in copies:
+        copy.start()
+
+
+def wait(copies):
+    for copy in copies:
+        copy.wait()
 
 
 def correction(x, dh, gain):
@@ -283,11 +328,16 @@
     wdt_out,
     wz_out,
     wx_out,
+    boy_ref,
+    bot_ref,
+    boty_ref,
     q_scr,
     bca_scr,
     s_scr,
     cs_scr,
     xs_scr,
+    wx_scr,
+    wbc_scr,
     wz_in,
     wx_in,
     wo_in,
@@ -300,6 +350,7 @@
     w_sems,
     po_sems,
     st_sems,
+    bo_sems,
     local,
 ):
     rows_all = x_ref.shape[0]
@@ -336,7 +387,7 @@
             for d in range(ny - 1)
         ] + [
             remote(
-                po_scr.at[pl.ds(pl.multiple_of(ys[d] * Ry, Ry), Ry)],
+                po_scr.at[lax.rem(last, 2), pl.ds(pl.multiple_of(ys[d] * Ry, Ry), Ry)],
                 po_in.at[last, d],
                 po_sems.at[0, last, d],
                 po_sems.at[1, last, d],
@@ -348,6 +399,16 @@
     def x_copy():
         return pltpu.make_async_copy(x4_ref.at[core * nloc + here - 1, yy], x_own, local.at[0])
 
+    def bo_spread(i):
+        return Spread(
+            bo_ref.at[i],
+            boy_ref.at[:, i],
+            bot_ref.at[i],
+            boty_ref.at[:, i],
+            bo_sems.at[:, i],
+            (twin, peers, ncore),
+        )
+
     @pl.when(here == 0)
     def _():
         greet(peers + ([twin] if ncore == 2 else []))
@@ -357,8 +418,7 @@
 
     @pl.when(here > 0)
     def _():
-        for copy in row_copies():
-            copy.start()
+        start(row_copies())
         x_copy().start()
 
     @pl.loop(0, rows_all // 32)
@@ -407,14 +467,32 @@
         t0 = pl.multiple_of(c * L, L)
         for half in range(2):
             lanes = slice(half * L, half * L + L)
-            v = conv(bcl_ref[pl.ds(t0, L + PAD), lanes], bcp_ref[0:4, lanes], bcp_ref[4:5, lanes])
+            v = conv(bcl_ref, t0, wbc_scr.at[half], lanes, bcp_ref[0:4, lanes], bcp_ref[4:5, lanes])
             bca_scr[pl.ds(t0, L), lanes] = (v * sigmoid(v)).astype(bf16)
 
     s_scr[...] = jnp.zeros_like(s_scr)
     hp = hp_ref[...]
 
+    def block_done():
+        wait(row_copies())
+        x_copy().wait()
+        total = st_ref[here - 1]
+        for d in range(ny - 1):
+            total = total + st_in[here - 1, d]
+        stot_ref[here - 1] = total
+        parts = [po_in.at[here - 1, d] for d in range(ny - 1)]
+        mine = po_scr.at[lax.rem(here - 1, 2), pl.ds(pl.multiple_of(yy * Ry, Ry), Ry)]
+        block_out(inner_total, stot_ref.at[here - 1], yy, mine, parts, x_own, bo_ref.at[here - 1])
+
     @pl.loop(0, rows_all // L)
     def _(c):
+        early = jnp.logical_and(here > 0, here < nloc - 1)
+
+        @pl.when(jnp.logical_and(early, c == rows_all // L - 1))
+        def _():
+            block_done()
+            start(bo_spread(here - 1).first())
+
         t0 = pl.multiple_of(c * L, L)
         rows = pl.ds(t0, L)
         lo = lane_iota((L, L)) < HEAD
@@ -432,13 +510,13 @@
         inner = jnp.zeros((L, L), f32)
         for p in range(pairs):
             lanes = slice(p * L, p * L + L)
-            xc = conv(xl_ref[pl.ds(t0, L + PAD), lanes], prm_ref[0:4, lanes], prm_ref[4:5, lanes])
+            xc = conv(xl_ref, t0, wx_scr.at[p], lanes, prm_ref[0:4, lanes], prm_ref[4:5, lanes])
             x = xc * sigmoid(xc)
             h0, h1 = 2 * p, 2 * p + 1
             a0, a1 = spread(cum, h0), spread(cum, h1)
             ap = jnp.where(lo, a0, a1)
-            k0 = both * jnp.exp(jnp.where(tri, a0 - cum_t[h0 : h0 + 1], -jnp.inf))
-            k1 = both * jnp.exp(jnp.where(tri, a1 - cum_t[h1 : h1 + 1], -jnp.inf))
+            k0 = both * jnp.exp2(jnp.where(tri, a0 - cum_t[h0 : h0 + 1], -jnp.inf))
+            k1 = both * jnp.exp2(jnp.where(tri, a1 - cum_t[h1 : h1 + 1], -jnp.inf))
             xdt = x * jnp.where(lo, spread(dt, h0), spread(dt, h1))
             xb = xdt.astype(bf16)
             fin = ap[L - 1 : L]
@@ -446,9 +524,9 @@
                 jnp.concatenate([k0.astype(bf16), k1.astype(bf16)], axis=1),
                 jnp.concatenate([xb * mlo, xb * mhi], axis=0),
             )
-            y = within + jnp.exp(ap) * cs_scr[:, lanes] + prm_ref[5:6, lanes] * x
-            xs_scr[:, lanes] = (xdt * jnp.exp(fin - ap)).astype(bf16)
-            s_scr[:, lanes] = s_scr[:, lanes] * jnp.exp(fin)
+            y = within + jnp.exp2(ap) * cs_scr[:, lanes] + prm_ref[5:6, lanes] * x
+            xs_scr[:, lanes] = (xdt * jnp.exp2(fin - ap)).astype(bf16)
+            s_scr[:, lanes] = s_scr[:, lanes] * jnp.exp2(fin)
             y_ref[rows, lanes] = y
             z = z_ref[rows, lanes]
             gated = y * (z * sigmoid(z))
@@ -463,30 +541,30 @@
         stat = jnp.where(lane == 0, s0, jnp.where(lane == 1, s1, 0.0))
         st_ref[here, :, rows] = stat.T[0:2]
 
-    @pl.when(here > 0)
-    def _():
-        for copy in row_copies():
-            copy.wait()
-        x_copy().wait()
-        total = st_ref[here - 1]
-        for d in range(ny - 1):
-            total = total + st_in[here - 1, d]
-        stot_ref[here - 1] = total
-        parts = [po_in.at[here - 1, d] for d in range(ny - 1)]
-        mine = po_scr.at[pl.ds(pl.multiple_of(yy * Ry, Ry), Ry)]
-        block_out(inner_total, stot_ref.at[here - 1], yy, mine, parts, x_own, bo_ref.at[here - 1])
-
     @pl.loop(0, model // 256)
     def _(j):
         cols = pl.ds(pl.multiple_of(j * 256, 256), 256)
         po = nn(q_scr[:, 0:own], wo_ref[:, cols])
         if ncore == 2:
             po = po + nn(q_scr[:, own : 2 * own], wo_in[:, cols])
-        po_scr[:, cols] = po.astype(bf16)
+        po_scr[lax.rem(here, 2), :, cols] = po.astype(bf16)
+
+    @pl.when(here > 1)
+    def _():
+        wait(bo_spread(here - 2).first())
+        start(bo_spread(here - 2).second())
 
     @pl.when(here == nloc - 1)
     def _():
-        po_ref[...] = po_scr[...]
+        po_ref[...] = po_scr[(nloc - 1) % 2]
+        block_done()
+
+    @pl.when(here > 1)
+    def _():
+        wait(bo_spread(here - 2).second())
+
+    @pl.when(here == nloc - 1)
+    def _():
         if ncore == 2:
             for copy in weight_stores():
                 copy.wait()
@@ -533,9 +611,12 @@
     go_ref,
     ggg_ref,
     bo_ref,
+    boy_ref,
+    bot_ref,
+    boty_ref,
     q_scr,
     sc_scr,
-    acc_scr,
+    dz_scr,
     stot_ref,
     st_in,
     send_scr,
@@ -546,6 +627,7 @@
     core_send,
     core_recv,
     po_sems,
+    bo_sems,
     local,
 ):
     rows_all = z_ref.shape[0]
@@ -577,15 +659,17 @@
     def x_copy():
         return pltpu.make_async_copy(x_ref.at[core * nloc + last, yy], x_own, local.at[0])
 
+    spread = Spread(
+        bo01_ref.at[last - 1], boy_ref, bot_ref, boty_ref, bo_sems, (twin, peers, ncore)
+    )
+
     @pl.when(here == 0)
     def _():
         greet(peers + ([twin] if ncore == 2 else []))
-        for copy in row_copies() + po_copies() + [x_copy()]:
-            copy.start()
+        start(row_copies() + po_copies() + [x_copy()] + spread.first())
         stot_ref[...] = stin_ref[...]
         for i in range(last):
             bo_ref[i] = bo01_ref[i]
-        acc_scr[...] = jnp.zeros_like(acc_scr)
         ggg_ref[...] = jnp.zeros_like(ggg_ref)
 
     @pl.when(here == last)
@@ -608,7 +692,7 @@
         c2 = jnp.broadcast_to(cols8[:, 1:2], (L, L))
         for m in range(model // L):
             lanes = slice(m * L, m * L + L)
-            sc_scr[rows, lanes] = (g_ref[rows, lanes].astype(f32) * r).astype(bf16)
+            sc_scr[here, rows, lanes] = (g_ref[rows, lanes].astype(f32) * r).astype(bf16)
         for p in range(pairs):
             lanes = slice(p * L, p * L + L)
             gg = prm_ref[6:7, lanes]
@@ -617,38 +701,57 @@
             sg = sigmoid(z)
             silz = z * sg
             gated = y * silz
-            q_scr[rows, lanes] = (gated * gg).astype(bf16)
+            q_scr[here, rows, lanes] = (gated * gg).astype(bf16)
             dq = r * u_ref[rows, lanes]
             ggg_ref[:, lanes] += fold_rows(dq * gated)
             dgated = dq * gg - c2 * gated
             dy_ref[rows, lanes] = (dgated * silz).astype(bf16)
-            dz_ref[rows, lanes] = (dgated * y * (sg + silz * (1.0 - sg))).astype(bf16)
-
-    @pl.loop(0, model // 256)
-    def _(j):
-        cols = pl.ds(pl.multiple_of(j * 256, 256), 256)
-        acc_scr[cols, 0:width] += tn(hid_ref[:, cols], dz_ref[...])
-        acc_scr[cols, width : 2 * width] += tn(sc_scr[:, cols], q_scr[...])
-
-    @pl.when(here == pl.num_programs(0) - 1)
+            dz = (dgated * y * (sg + silz * (1.0 - sg))).astype(bf16)
+            dz_ref[rows, lanes] = dz
+            dz_scr[here, rows, lanes] = dz
+
+    @pl.when(here == last)
     def _():
+        hid = hid_ref.reshape(nloc * rows_all, model)
+        dz = dz_scr.reshape(nloc * rows_all, width)
+        q = q_scr.reshape(nloc * rows_all, width)
+        sc = sc_scr.reshape(nloc * rows_all, model)
+
+        def sums(half, out_z, out_o):
+            lanes = slice(half * own, half * own + own)
+
+            @pl.loop(0, model // 256)
+            def _(j):
+                cols = pl.ds(pl.multiple_of(j * 256, 256), 256)
+                gz = tn(hid[:, cols], dz[:, lanes])
+                go = tn(sc[:, cols], q[:, lanes])
+                out_z[cols, :] = gz.astype(bf16)
+                out_o[cols, :] = go.astype(bf16)
+
         if ncore == 2:
-            send_scr[:, 0:own] = acc_scr[:, own:width].astype(bf16)
-            send_scr[:, own : 2 * own] = acc_scr[:, width + own : 2 * width].astype(bf16)
+            sums(1, send_scr.at[:, 0:own], send_scr.at[:, own : 2 * own])
+        if ncore == 2:
             copy = remote(send_scr, recv_scr, core_send, core_recv, twin)
             copy.start()
+        sums(0, gz_ref, go_ref)
+        if ncore == 2:
             copy.wait()
-            theirs = recv_scr[...].astype(f32)
-        else:
-            theirs = jnp.zeros((model, 2 * own), f32)
-        gz_ref[...] = (acc_scr[:, 0:own] + theirs[:, 0:own]).astype(bf16)
-        mine = acc_scr[:, width : width + own] + theirs[:, own : 2 * own]
-        go_ref[...] = mine.astype(bf16)
+
+            @pl.loop(0, model // 64)
+            def _(j):
+                rows = pl.ds(pl.multiple_of(j * 64, 64), 64)
+                for ref, first in ((gz_ref, 0), (go_ref, own)):
+                    theirs = recv_scr[rows, first : first + own].astype(f32)
+                    ref[rows, :] = (ref[rows, :].astype(f32) + theirs).astype(bf16)
+
         for copy in po_copies() + [x_copy()]:
             copy.wait()
         parts = [po_in.at[d] for d in range(ny - 1)]
         mine = po_ref.at[pl.ds(pl.multiple_of(yy * Ry, Ry), Ry)]
         block_out(inner_total, stot_ref.at[last], yy, mine, parts, x_own, bo_ref.at[last])
+        wait(spread.first())
+        start(spread.second())
+        wait(spread.second())
 
 
 def scan_kernel(
@@ -708,6 +811,11 @@
     dye_scr,
     nx_scr,
     nbc_scr,
+    wx_scr,
+    wbc_scr,
+    red_scr,
+    end_scr,
+    pick_scr,
     gx_ref,
     gbc_ref,
     gdt_ref,
@@ -746,22 +854,13 @@
     ]
     last_step = nloc_static * spans - 1
 
-    def bo_first():
-        out = [
-            remote(bo_ref, boy_ref.at[d], bo_sems.at[0, d], bo_sems.at[1, d], peers[d])
-            for d in range(ny - 1)
-        ]
-        if ncore == 2:
-            out.append(remote(bo_ref, bot_ref, bo_sems.at[0, ny - 1], bo_sems.at[1, ny - 1], twin))
-        return out
-
-    def bo_second():
-        if ncore != 2:
-            return []
-        return [
-            remote(boy_ref.at[d], boty_ref.at[d], bo_sems.at[0, ny + d], bo_sems.at[1, ny + d], twin)
-            for d in range(ny - 1)
-        ]
+    place = (twin, peers, ncore)
+    bo_spread = Spread(bo_ref.at[nloc_static - 1], boy_ref, bot_ref, boty_ref, bo_sems, place)
+
+    def corr_spread(i):
+        return Spread(
+            corr_ref.at[i], cy_ref.at[:, i], ct_ref.at[i], cty_ref.at[:, i], c_sems.at[:, i], place
+        )
 
     def dh_copies():
         return [
@@ -781,9 +880,11 @@
     @pl.when(step == 0)
     def _():
         greet(peers + dp_peers + ([twin] if ncore == 2 else []))
-        for copy in bo_first():
-            copy.start()
+        start(bo_spread.first())
         acc_scr[...] = jnp.zeros_like(acc_scr)
+        end_scr[...] = jnp.zeros_like(end_scr)
+        pick = row_iota((width, L)) // HEAD == lane_iota((width, L))
+        pick_scr[...] = pick.astype(f32).astype(bf16)
         gx_ref[...] = jnp.zeros_like(gx_ref)
         gbc_ref[...] = jnp.zeros_like(gbc_ref)
         gdt_ref[...] = jnp.zeros_like(gdt_ref)
@@ -800,50 +901,17 @@
             for job in jobs:
                 job.begin(j)
 
-    @pl.when(step == last_step // 2)
+    @pl.when(step == spans)
     def _():
-        for copy in bo_first():
-            copy.wait()
-        for copy in bo_second():
-            copy.start()
-
-    def corr_first(i):
-        out = [
-            remote(corr_ref.at[i], cy_ref.at[d, i], c_sems.at[0, i, d], c_sems.at[1, i, d], peers[d])
-            for d in range(ny - 1)
-        ]
-        if ncore == 2:
-            d = ny - 1
-            out.append(remote(corr_ref.at[i], ct_ref.at[i], c_sems.at[0, i, d], c_sems.at[1, i, d], twin))
-        return out
-
-    def corr_second(i):
-        if ncore != 2:
-            return []
-        return [
-            remote(
-                cy_ref.at[d, i],
-                cty_ref.at[d, i],
-                c_sems.at[0, i, ny + d],
-                c_sems.at[1, i, ny + d],
-                twin,
-            )
-            for d in range(ny - 1)
-        ]
+        wait(bo_spread.first())
+        start(bo_spread.second())
 
     for i in range(nloc_static - 2):
-
-        @pl.when(step == (i + 2) * spans - 1)
-        def _(i=i):
-            for copy in corr_first(i):
-                copy.start()
 
         @pl.when(step == (i + 2) * spans + 2)
         def _(i=i):
-            for copy in corr_first(i):
-                copy.wait()
-            for copy in corr_second(i):
-                copy.start()
+            wait(corr_spread(i).first())
+            start(corr_spread(i).second())
 
     @pl.when(jnp.logical_and(seq > 0, back == 0))
     def _():
@@ -851,7 +919,7 @@
             copy.start()
         x_copy().start()
 
-    @pl.when(jnp.logical_and(seq > 0, back == spans - 2))
+    @pl.when(jnp.logical_and(seq > 0, back == spans - 1))
     def _():
         for copy in dh_copies():
             copy.wait()
@@ -866,6 +934,8 @@
                 dh = dh + dh_in[seq - 1, d, rows, :].astype(f32)
             corr_ref[seq - 1, rows, :] = correction(x_own[rows, :], dh, gain_ref[...]).astype(bf16)
 
+        start(corr_spread(seq - 1).first())
+
     hp = hp_ref[...]
 
     @pl.when(back == 0)
@@ -879,7 +949,7 @@
             t0 = pl.multiple_of(c * L, L)
             for half in range(2):
                 lanes = slice(half * L, half * L + L)
-                v = conv(bcl_ref[pl.ds(t0, L + PAD), lanes], bcp_ref[0:4, lanes], bcp_ref[4:5, lanes])
+                v = conv(bcl_ref, t0, wbc_scr.at[half], lanes, bcp_ref[0:4, lanes], bcp_ref[4:5, lanes])
                 bcc_scr[pl.ds(t0, L), lanes] = v
                 bca_scr[pl.ds(t0, L), lanes] = (v * sigmoid(v)).astype(bf16)
 
@@ -901,34 +971,26 @@
         cs_scr[...] = nn(cm, sb)
         bds_scr[...] = nn(bm, dsb_scr[...])
         d_both = jnp.zeros((L, L), f32)
-        d_cum = jnp.zeros((L, L), f32)
-        d_dt = jnp.zeros((L, L), f32)
-        d_far = jnp.zeros((L, L), f32)
-        d_end = jnp.zeros((1, L), f32)
         for p in range(pairs):
             lanes = slice(p * L, p * L + L)
-            window = xl_ref[pl.ds(t0, L + PAD), lanes]
-            shifted = [window[PAD - 3 + k : PAD - 3 + k + L] for k in range(4)]
             taps = prm_ref[0:4, lanes]
-            xc = prm_ref[4:5, lanes]
-            for k in range(4):
-                xc = xc + shifted[k] * taps[k : k + 1]
+            xc = conv(xl_ref, t0, wx_scr.at[p], lanes, taps, prm_ref[4:5, lanes])
             sg = sigmoid(xc)
             x = xc * sg
             h0, h1 = 2 * p, 2 * p + 1
             a0, a1 = spread(cum, h0), spread(cum, h1)
             ap = jnp.where(lo, a0, a1)
-            e0 = jnp.exp(jnp.where(tri, a0 - cum_t[h0 : h0 + 1], -jnp.inf))
-            e1 = jnp.exp(jnp.where(tri, a1 - cum_t[h1 : h1 + 1], -jnp.inf))
+            e0 = jnp.exp2(jnp.where(tri, a0 - cum_t[h0 : h0 + 1], -jnp.inf))
+            e1 = jnp.exp2(jnp.where(tri, a1 - cum_t[h1 : h1 + 1], -jnp.inf))
             k0 = (both * e0).astype(bf16)
             k1 = (both * e1).astype(bf16)
             dtp = jnp.where(lo, spread(dt, h0), spread(dt, h1))
             xdt = x * dtp
             xb = xdt.astype(bf16)
             bdx = jnp.concatenate([xb * mlo, xb * mhi], axis=0)
-            ecum = jnp.exp(ap)
+            ecum = jnp.exp2(ap)
             fin = ap[L - 1 : L]
-            sd = jnp.exp(fin - ap)
+            sd = jnp.exp2(fin - ap)
             y = nn(jnp.concatenate([k0, k1], axis=1), bdx) + ecum * cs_scr[:, lanes]
             dyb = dy_ref[rows, lanes]
             dy = dyb.astype(f32)
@@ -941,31 +1003,35 @@
             v = dy * y - xb.astype(f32) * near
             u = dxdt * x
             w = xdt * far
-            ends = jnp.exp(fin)
+            ends = jnp.exp2(fin)
             through = ends * jnp.sum(sb[:, lanes].astype(f32) * ds_scr[:, lanes], axis=0, keepdims=True)
-            for h, keep in ((h0, lo), (h1, jnp.logical_not(lo))):
-                here = lane == h
-                d_cum = jnp.where(here, jnp.sum(jnp.where(keep, v, 0.0), axis=1, keepdims=True), d_cum)
-                d_dt = jnp.where(here, jnp.sum(jnp.where(keep, u, 0.0), axis=1, keepdims=True), d_dt)
-                d_far = jnp.where(here, jnp.sum(jnp.where(keep, w, 0.0), axis=1, keepdims=True), d_far)
-                whole = jnp.sum(jnp.where(keep[0:1], through, 0.0), axis=1, keepdims=True)
-                d_end = jnp.where(here[0:1], whole, d_end)
+            v_hi = v.astype(bf16)
+            red_scr[0:L, lanes] = v_hi
+            red_scr[L : 2 * L, lanes] = (v - v_hi.astype(f32)).astype(bf16)
+            red_scr[2 * L : 3 * L, lanes] = u.astype(bf16)
+            red_scr[3 * L : 4 * L, lanes] = w.astype(bf16)
+            end_scr[0:1, lanes] = through
             dx = dxdt * dtp + dy * prm_ref[5:6, lanes]
             dxc = dx * (sg + x * (1.0 - sg))
             for k in range(4):
-                gx_ref[k, :, lanes] += fold_rows(dxc * shifted[k])
+                gx_ref[k, :, lanes] += fold_rows(dxc * tap(wx_scr.at[p], k))
             gx_ref[4, :, lanes] += fold_rows(dxc)
             gx_ref[5, :, lanes] += fold_rows(dy * x)
-            ext = jnp.concatenate([dxc, nx_scr[:, lanes]], axis=0)
-            dxl = ext[0:L] * taps[3:4]
+            nx_scr[p, L : L + 8] = nx_scr[p, 0:8]
+            nx_scr[p, 0:L] = dxc
+            dxl = dxc * taps[3:4]
             for k in range(3):
-                dxl = dxl + ext[3 - k : 3 - k + L] * taps[k : k + 1]
-            nx_scr[:, lanes] = dxc[0:8]
+                dxl = dxl + nx_scr[p, 3 - k : 3 - k + L] * taps[k : k + 1]
             d_scr[rows, lanes] = dxl.astype(bf16)
             xs_scr[:, lanes] = (xdt * sd).astype(bf16)
             dye_scr[:, lanes] = (dy * ecum).astype(bf16)
             ds_scr[:, lanes] = ds_scr[:, lanes] * ends
         ds_scr[...] += nn(cm.T, dye_scr[...])
+        sums = nn(red_scr[...], pick_scr[...])
+        d_cum = sums[0:L] + sums[L : 2 * L]
+        d_dt = sums[2 * L : 3 * L]
+        d_far = sums[3 * L : 4 * L]
+        d_end = exact(end_scr[...], pick_scr[...].astype(f32))[0:1]
         utri = (row_iota((L, L)) <= lane).astype(f32)
         before = (row_iota((L, L)) > lane).astype(f32)
         d_a = exact(utri, d_cum) + exact(before, d_far) + d_end
@@ -982,15 +1048,15 @@
             pre_act = bcc_scr[rows, lanes]
             sg = sigmoid(pre_act)
             dvc = dv * (sg + pre_act * sg * (1.0 - sg))
-            window = bcl_ref[pl.ds(t0, L + PAD), lanes]
+            wbc_scr[half] = bcl_ref[pl.ds(t0, L + PAD), lanes]
             for k in range(4):
-                gbc_ref[k, :, lanes] += fold_rows(dvc * window[PAD - 3 + k : PAD - 3 + k + L])
+                gbc_ref[k, :, lanes] += fold_rows(dvc * tap(wbc_scr.at[half], k))
             gbc_ref[4, :, lanes] += fold_rows(dvc)
-            ext = jnp.concatenate([dvc, nbc_scr[:, lanes]], axis=0)
-            dvl = ext[0:L] * bcp_ref[3:4, lanes]
+            nbc_scr[half, L : L + 8] = nbc_scr[half, 0:8]
+            nbc_scr[half, 0:L] = dvc
+            dvl = dvc * bcp_ref[3:4, lanes]
             for k in range(3):
-                dvl = dvl + ext[3 - k : 3 - k + L] * bcp_ref[k : k + 1, lanes]
-            nbc_scr[:, lanes] = dvc[0:8]
+                dvl = dvl + nbc_scr[half, 3 - k : 3 - k + L] * bcp_ref[k : k + 1, lanes]
             d_scr[rows, width + half * L : width + half * L + L] = dvl.astype(bf16)
 
     one_chunk()
@@ -1047,11 +1113,12 @@
         else:
             gw_ref[:, 0:own] = acc_scr[:, 0:own].astype(bf16)
         gw_ref[:, own : own + L] = tail.astype(bf16)
-        for copy in bo_second():
-            copy.wait()
-        for i in range(nloc_static - 2):
-            for copy in corr_second(i):
-                copy.wait()
+        final = corr_spread(nloc_static - 2)
+        wait(final.first())
+        start(final.second())
+        wait(bo_spread.second())
+        for i in range(nloc_static - 1):
+            wait(corr_spread(i).second())
 
 
 def tail_kernel(
@@ -1059,6 +1126,7 @@
     ncore,
     ny,
     ndp,
+    nloc,
     gw_ref,
     gbcw_ref,
     small_ref,
@@ -1066,16 +1134,12 @@
     shared_ref,
     dh_ref,
     gain_ref,
-    corr_ref,
     x_ref,
     fw_ref,
     fb_ref,
     small_out,
     shared_out,
     last_ref,
-    cy_ref,
-    ct_ref,
-    cty_ref,
     ly_ref,
     lt_ref,
     lty_ref,
@@ -1084,13 +1148,12 @@
     small_in,
     core_sems,
     y_sems,
-    c_sems,
     l_sems,
     local,
     *machine,
 ):
     model = gw_ref.shape[0]
-    Ry, nloc = x_own.shape[0], corr_ref.shape[0] + 1
+    Ry = x_own.shape[0]
     core, yy, twin, ys, peers = places(ncore, ny)
     nbits = log2(ndp)
     dp_peers, dp_bits = bit_peers("dp", 1, 0, nbits)
@@ -1122,24 +1185,7 @@
             for d in range(ny - 1)
         ]
 
-    def first(src, toy, tot, sems):
-        out = [
-            remote(src, toy.at[d], sems.at[0, d], sems.at[1, d], peers[d]) for d in range(ny - 1)
-        ]
-        if ncore == 2:
-            out.append(remote(src, tot, sems.at[0, ny - 1], sems.at[1, ny - 1], twin))
-        return out
-
-    def second(toy, toty, sems):
-        if ncore != 2:
-            return []
-        return [
-            remote(toy.at[d], toty.at[d], sems.at[0, ny + d], sems.at[1, ny + d], twin)
-            for d in range(ny - 1)
-        ]
-
-    early = (corr_ref.at[nloc - 2], cy_ref, ct_ref, c_sems)
-    late = (last_ref, ly_ref, lt_ref, l_sems)
+    late = Spread(last_ref, ly_ref, lt_ref, lty_ref, l_sems, (twin, peers, ncore))
     x_copy = pltpu.make_async_copy(x_ref.at[core * nloc + nloc - 1, yy], x_own, local.at[0])
     others = peers + ([twin] if ncore == 2 else [])
     greet(others + dp_peers)
@@ -1152,15 +1198,12 @@
             job.begin(j)
 
     job_sh.acc[0] = shared_ref[...]
-    turn((job_c, 0), (job_a, 0), (job_b, 0), (job_sh, 0))
+    turn((job_sh, 0), (job_c, 0), (job_a, 0), (job_b, 0))
     if ncore == 2:
         small_copy = remote(other_ref, small_in, core_sems.at[0], core_sems.at[1], twin)
         small_copy.start()
     turn((job_c, 1), (job_sh, 1))
-    for copy in dh_copies():
-        copy.start()
-    for copy in first(*early):
-        copy.start()
+    start(dh_copies())
     if ncore == 2:
         small_copy.wait()
         job_sm.acc[0] = small_ref[...] + small_in[...]
@@ -1181,7 +1224,7 @@
                 found.append((job, j))
         return found
 
-    turn((job_a, 1), (job_b, 1), *smaller())
+    turn(*smaller(), (job_a, 1), (job_b, 1))
     for copy in dh_copies():
         copy.wait()
     x_copy.wait()
@@ -1196,54 +1239,64 @@
         last_ref[rows, :] = correction(x_own[rows, :], dh, gain_ref[...]).astype(bf16)
 
     turn(*smaller())
-    for copy in first(*late):
-        copy.start()
+    start(late.first())
     for j in range(2, 2 * nbits + 1):
-        turn((job_a, j), (job_b, j), *smaller())
-    for copy in first(*early):
-        copy.wait()
-    for copy in second(cy_ref, cty_ref, c_sems):
-        copy.start()
+        turn(*smaller(), (job_a, j), (job_b, j))
     for _ in range(2 * job_c.n):
         turn(*smaller())
     small_out[...] = job_sm.acc[len(job_sm.peers)]
     shared_out[...] = job_sh.acc[len(job_sh.peers)]
-    for copy in first(*late):
-        copy.wait()
-    for copy in second(ly_ref, lty_ref, l_sems):
-        copy.start()
-    for copy in second(cy_ref, cty_ref, c_sems) + second(ly_ref, lty_ref, l_sems):
-        copy.wait()
+    wait(late.first())
+    start(late.second())
+    wait(late.second())
 
 
 def finish_kernel(pieces, nloc, _idx, g_ref, *refs):
     gi_ref, bo_ref = refs[-2:]
-    groups = [refs[n * pieces : (n + 1) * pieces] for n in range(4)]
+    groups = [refs[n * pieces : (n + 1) * pieces] for n in range(5)]
     now = pl.program_id(1)
     for k in range(pieces):
         here = pl.program_id(0) == k
 
-        @pl.when(here)
-        def _(src=groups[3][k]):
-            bo_ref[...] = src[...]
-
-        for n in range(3):
-            if n == 0:
-                turn = now < nloc - 2
-            else:
-                turn = now == nloc - 3 + n
-
-            @pl.when(jnp.logical_and(here, turn))
+        def when(turn, here=here):
+            return pl.when(jnp.logical_and(here, turn))
+
+        for n, turn in ((0, now < nloc - 1), (1, now == nloc - 1)):
+
+            @when(turn)
             def _(src=groups[n][k]):
                 gi_ref[...] = g_ref[...].astype(f32) + src[...].astype(f32)
 
-
-def unpack_kernel(own, gz_ref, go_ref, gw_ref, gzx_ref, gwo_ref):
+        for n, turn in ((2, now < nloc - 2), (3, now == nloc - 2), (4, now == nloc - 1)):
+
+            @when(turn)
+            def _(src=groups[n][k]):
+                bo_ref[...] = src[...]
+
+
+def unpack_kernel(own, heads, gz_ref, go_ref, gw_ref, fb_ref, small_ref, shared_ref, *outs):
+    gzx_ref, gwo_ref, gwdt_ref, gwbc_ref = outs[:4]
+    gcxw_ref, gcxb_ref, gd_ref, ggg_ref, gdtb_ref, galog_ref, gpre_ref, gcbw_ref, gcbb_ref = outs[4:]
     gzx_ref[:, 0, :] = gz_ref[...].astype(f32)
     gzx_ref[:, 1, :] = gw_ref[:, 0:own].astype(f32)
+    gwdt_ref[...] = gw_ref[:, own : own + L].astype(f32)[:, 0:heads]
+    gwbc_ref[...] = fb_ref[...].astype(f32)
     v = go_ref[...].astype(f32)
     for k in range(own // L):
         gwo_ref[k * L : k * L + L, :] = v[:, k * L : k * L + L].T
+
+    @pl.when(pl.program_id(0) == 0)
+    def _():
+        gcxw_ref[...] = small_ref[0:4]
+        gcxb_ref[...] = small_ref[4:5]
+        ggg_ref[...] = small_ref[6:7]
+        gdtb_ref[...] = small_ref[7:8, 0:heads]
+        galog_ref[...] = small_ref[8:9, 0:heads]
+        pick = (row_iota((own, L)) // HEAD == lane_iota((own, L))).astype(f32)
+        gd_ref[...] = exact(small_ref[0:8], pick)[5:6, 0:heads]
+        gpre_ref[...] = shared_ref[0:1]
+        gcbw_ref[...] = shared_ref[1:5, 0:256]
+        gcbb_ref[...] = shared_ref[5:6, 0:256]
 
 
 def seq_spec(*shape):
@@ -1326,6 +1379,7 @@
     nloc = nseq // ncore
     spans = R // L
     wtot = 2 * width + 384
+    pairs = width // L
 
     x3 = block_input.reshape(nseq, R, model)
     g3 = out_grad.reshape(nseq, R, model)
@@ -1351,7 +1405,8 @@
     nother = max(ny - 1, 1)
     dma = pltpu.SemaphoreType.DMA
 
-    hid, z, xl, bcl, dtl, u, y, sin, st, stot, po, bo01, prm, hp, wdt, wzo, wxo = call(
+    early_n = max(nloc - 2, 1)
+    f_out = call(
         partial(forward_kernel, own, heads, ncore, ny, inner_total, nloc),
         (nloc,),
         [
@@ -1383,9 +1438,8 @@
             whole_spec(8, width),
             whole_spec(8, L),
             whole_spec(model, L),
-            any_spec,
-            any_spec,
-        ],
+        ]
+        + [any_spec] * 5,
         [
             sds(nloc, R, model, dtype=bf16),
             sds(nloc, R, width),
@@ -1404,6 +1458,9 @@
             sds(model, L, dtype=bf16),
             sds(model, own, dtype=bf16),
             sds(model, own, dtype=bf16),
+            sds(nother, early_n, Ry, model, dtype=bf16),
+            sds(early_n, Ry, model, dtype=bf16),
+            sds(nother, early_n, Ry, model, dtype=bf16),
         ],
         [
             pltpu.VMEM((R, width), bf16),
@@ -1411,18 +1468,21 @@
             pltpu.VMEM((L, width), f32),
             pltpu.VMEM((L, width), f32),
             pltpu.VMEM((L, width), bf16),
+            pltpu.VMEM((pairs, L + PAD, L), f32),
+            pltpu.VMEM((2, L + PAD, L), f32),
             pltpu.VMEM((model, own), bf16),
             pltpu.VMEM((model, own), bf16),
             pltpu.VMEM((own, model), bf16),
             pltpu.VMEM((model, L), bf16),
             pltpu.VMEM((16, own), f32),
-            pltpu.VMEM((R, model), bf16),
+            pltpu.VMEM((2, R, model), bf16),
             pltpu.VMEM((nloc - 1, nother, Ry, model), bf16),
             pltpu.VMEM((nloc - 1, nother, 2, R), f32),
             pltpu.VMEM((Ry, model), bf16),
             dma((2, 5)),
             dma((2, nloc - 1, nother)),
             dma((2, nloc - 1, nother)),
+            dma((2, early_n, 2 * ny)),
             dma((3,)),
         ],
         "forward",
@@ -1430,16 +1490,19 @@
         nloc * R * (6 * model + 20 * width),
         4,
     )(seq0, x3, g3, gain, wz, wx, w_bc, wdt, w_out, sm, bcp, x4)
+    hid, z, xl, bcl, dtl, u, y, sin, st, stot, po, bo01, prm, hp, wdt, wzo, wxo = f_out[:17]
+    bo_early = f_out[17:]
 
     nbits = log2(ndp)
-    dz, dy, gz, go, ggg, bo = call(
+    one = sds(nother, Ry, model, dtype=bf16)
+    dz, dy, gz, go, ggg, bo, *bo_mid = call(
         partial(gate_kernel, width, own, inner_total, ncore, ny),
         (nloc,),
         [
             whole_spec(nloc, 2, R),
             whole_spec(nloc, 2, R),
             moved_spec(ncore, nloc, R, model),
-            seq_spec(R, model),
+            whole_spec(nloc, R, model),
             seq_spec(R, width),
             seq_spec(R, width),
             seq_spec(R, width),
@@ -1455,7 +1518,8 @@
             whole_spec(model, own),
             whole_spec(8, width),
             whole_spec(nloc, Ry, model),
-        ],
+        ]
+        + [any_spec] * 3,
         [
             sds(nloc, R, width, dtype=bf16),
             sds(nloc, R, width, dtype=bf16),
@@ -1463,11 +1527,14 @@
             sds(model, own, dtype=bf16),
             sds(8, width),
             sds(nloc, Ry, model, dtype=bf16),
+            one,
+            sds(Ry, model, dtype=bf16),
+            one,
         ],
         [
-            pltpu.VMEM((R, width), bf16),
-            pltpu.VMEM((R, model), bf16),
-            pltpu.VMEM((model, 2 * width), f32),
+            pltpu.VMEM((nloc, R, width), bf16),
+            pltpu.VMEM((nloc, R, model), bf16),
+            pltpu.VMEM((nloc, R, width), bf16),
             pltpu.VMEM((nloc, 2, R), f32),
             pltpu.VMEM((nother, 2, R), f32),
             pltpu.VMEM((model, 2 * own), bf16),
@@ -1478,6 +1545,7 @@
             dma,
             dma,
             dma((2, nother)),
+            dma((2, 2 * ny)),
             dma((1,)),
         ],
         "gate",
@@ -1491,7 +1559,6 @@
         return pl.BlockSpec((None,) + shape, lambda i, b, s: (i,) + zeros)
 
     bc_type = bf16 if (model // (nt * ndp)) % 16 == 0 else f32
-    early_n = max(nloc - 2, 1)
     dh, gw2, gbcw, small, other, shared, corr, fz, fo, boy, bot, boty, cy0, ct0, cty0 = call(
         partial(scan_kernel, width, own, heads, ncore, ny, ndp, nloc),
         (nloc, spans),
@@ -1539,12 +1606,12 @@
             sds(nloc - 1, Ry, model, dtype=bf16),
             sds(model, own, dtype=bf16),
             sds(model, own, dtype=bf16),
-            sds(nother, nloc, Ry, model, dtype=bf16),
-            sds(nloc, Ry, model, dtype=bf16),
-            sds(nother, nloc, Ry, model, dtype=bf16),
-            sds(nother, early_n, Ry, model, dtype=bf16),
-            sds(early_n, Ry, model, dtype=bf16),
-            sds(nother, early_n, Ry, model, dtype=bf16),
+            one,
+            sds(Ry, model, dtype=bf16),
+            one,
+            sds(nother, nloc - 1, Ry, model, dtype=bf16),
+            sds(nloc - 1, Ry, model, dtype=bf16),
+            sds(nother, nloc - 1, Ry, model, dtype=bf16),
         ],
         [
             pltpu.VMEM((R, width + 384), bf16),
@@ -1556,8 +1623,13 @@
             pltpu.VMEM((L, width), f32),
             pltpu.VMEM((L, width), bf16),
             pltpu.VMEM((L, width), bf16),
+            pltpu.VMEM((pairs, L + 8, L), f32),
+            pltpu.VMEM((2, L + 8, L), f32),
+            pltpu.VMEM((pairs, L + PAD, L), f32),
+            pltpu.VMEM((2, L + PAD, L), f32),
+            pltpu.VMEM((4 * L, width), bf16),
             pltpu.VMEM((8, width), f32),
-            pltpu.VMEM((8, 256), f32),
+            pltpu.VMEM((width, L), bf16),
             pltpu.VMEM((6, 8, width), f32),
             pltpu.VMEM((5, 8, 256), f32),
             pltpu.VMEM((2, 8, L), f32),
@@ -1572,7 +1644,7 @@
             dma,
             dma((2, nloc - 1, nother)),
             dma((2, 2 * ny)),
-            dma((2, early_n, 2 * ny)),
+            dma((2, nloc - 1, 2 * ny)),
             dma((1,)),
         ]
         + Halving.scratch(model, own, nbits, bf16)
@@ -1586,19 +1658,16 @@
     vm = pl.BlockSpec(memory_space=pltpu.VMEM)
     tbits = log2(nt)
     late_shape = sds(nother, Ry, model, dtype=bf16)
-    fw, fb, small, shared, last, cy, ct, cty, ly, lt, lty = pl.pallas_call(
-        partial(tail_kernel, own, ncore, ny, ndp),
-        in_specs=[vm] * 7 + [any_spec] * 2,
-        out_specs=[any_spec] * 2 + [vm] * 3 + [any_spec] * 6,
+    fw, fb, small, shared, last, ly, lt, lty = pl.pallas_call(
+        partial(tail_kernel, own, ncore, ny, ndp, nloc),
+        in_specs=[vm] * 7 + [any_spec],
+        out_specs=[any_spec] * 2 + [vm] * 3 + [any_spec] * 3,
         out_shape=[
             sds(model, own + L, dtype=bf16),
             sds(model, 256, dtype=bc_type),
             sds(16, own),
             sds(8, model),
             sds(Ry, model, dtype=bf16),
-            late_shape,
-            sds(Ry, model, dtype=bf16),
-            late_shape,
             late_shape,
             sds(Ry, model, dtype=bf16),
             late_shape,
@@ -1610,7 +1679,6 @@
             dma((2,)),
             dma((2, nother)),
             dma((2, 2 * ny)),
-            dma((2, 2 * ny)),
             dma((1,)),
         ]
         + Halving.scratch(model // 2, own + L, nbits, bf16)
@@ -1620,7 +1688,7 @@
         + Doubling.scratch(nbits + tbits, 8, model),
         compiler_params=pltpu.CompilerParams(collective_id=3, has_side_effects=True),
         name="tail",
-    )(gw2, gbcw, small, other, shared, dh, gain, corr, x4)
+    )(gw2, gbcw, small, other, shared, dh, gain, x4)
 
     pieces = ncore * ny
     where = jnp.stack([core, yy]).astype(jnp.int32)
@@ -1662,10 +1730,16 @@
     def as_seq(v, axis):
         return jnp.expand_dims(v, axis)
 
-    add_group(0, early_n, corr, 0, cy0, ct0, cty0)
-    add_group(nloc - 2, 1, corr, 0, as_seq(cy, 1), as_seq(ct, 0), as_seq(cty, 1))
+    add_group(0, nloc - 1, corr, 0, cy0, ct0, cty0)
     add_group(nloc - 1, 1, as_seq(last, 0), nloc - 1, as_seq(ly, 1), as_seq(lt, 0), as_seq(lty, 1))
-    add_group(0, nloc, bo, 0, boy, bot, boty)
+
+    def add_late(first, got):
+        toy, tot, toty = got
+        add_group(first, 1, bo, 0, as_seq(toy, 1), as_seq(tot, 0), as_seq(toty, 1))
+
+    add_group(0, early_n, bo, 0, *bo_early)
+    add_late(nloc - 2, bo_mid)
+    add_late(nloc - 1, (boy, bot, boty))
     grad_input, block_output = call(
         partial(finish_kernel, pieces, nloc),
         (pieces, nloc),
@@ -1678,37 +1752,62 @@
         12 * tok * model,
     )(where, g4, *arrays)
 
-    gzx, gwo = pl.pallas_call(
-        partial(unpack_kernel, own),
+    def row_block(cols):
+        return pl.BlockSpec((L, cols), lambda d: (d, 0))
+
+    outs = pl.pallas_call(
+        partial(unpack_kernel, own, heads),
         grid=(model // L,),
-        in_specs=[
-            pl.BlockSpec((L, own), lambda d: (d, 0)),
-            pl.BlockSpec((L, own), lambda d: (d, 0)),
-            pl.BlockSpec((L, own + L), lambda d: (d, 0)),
-        ],
+        in_specs=[row_block(own), row_block(own), row_block(own + L), row_block(256)]
+        + [whole_spec(16, own), whole_spec(8, model)],
         out_specs=[
             pl.BlockSpec((L, 2, own), lambda d: (d, 0, 0)),
             pl.BlockSpec((own, L), lambda d: (0, d)),
+            row_block(heads),
+            row_block(256),
+            whole_spec(4, own),
+            whole_spec(1, own),
+            whole_spec(1, heads),
+            whole_spec(1, own),
+            whole_spec(1, heads),
+            whole_spec(1, heads),
+            whole_spec(1, model),
+            whole_spec(4, 256),
+            whole_spec(1, 256),
         ],
-        out_shape=[sds(model, 2, own), sds(own, model)],
+        out_shape=[
+            sds(model, 2, own),
+            sds(own, model),
+            sds(model, heads),
+            sds(model, 256),
+            sds(4, own),
+            sds(1, own),
+            sds(1, heads),
+            sds(1, own),
+            sds(1, heads),
+            sds(1, heads),
+            sds(1, model),
+            sds(4, 256),
+            sds(1, 256),
+        ],
         name="unpack",
-    )(fz, fo, fw)
-    tail = fw[:, own : own + heads].astype(f32)
+    )(fz, fo, fw, fb, small, shared)
+    gzx, gwo, gwdt, gwbc, gcxw, gcxb, gd, ggg, gdtb, galog, gpre, gcbw, gcbb = outs
     return (
         block_output.reshape(tok, model),
         grad_input.reshape(tok, model),
-        shared[0],
+        gpre[0],
         gzx,
-        fb.astype(f32),
-        tail,
-        small[0:4],
-        small[4],
-        shared[1:5, 0:256],
-        shared[5, 0:256],
-        small[7, :heads],
-        small[8, :heads],
-        jnp.sum(small[5].reshape(heads, HEAD), axis=1),
-        small[6],
+        gwbc,
+        gwdt,
+        gcxw,
+        gcxb[0],
+        gcbw,
+        gcbb[0],
+        gdtb[0],
+        galog[0],
+        gd[0],
+        ggg[0],
         gwo,
     )
 

time: 326 us -> 314 us (0.963)
  local copies, waits for them, and re-layouts: 18.7 us -> 11.8 us
    pallas_call x1, Pallas kernels: 109 us -> 101 us  [body(): call(partial(scan_kernel, width, own, heads, ncore, ny, ndp, nloc), (nloc...]
    slice x5 -> x0, local copies, waits for them, and re-layouts: 6.63 us -> none  [the longest x1 1.42 us: body(): small[6]]
    pallas_call x1, Pallas kernels: 30.4 us -> 34.3 us  [body(): call(partial(gate_kernel, width, own, inner_total, ncore, ny), (nloc,), [...]
where the time goes in v3:
time: 314 us; the launch traced here: 313 us
  Pallas kernels  298 us (95%)
  local copies, waits for them, and re-layouts  11.8 us (4%)
    pallas_call x1, Pallas kernels, body(): call(partial(scan_kernel, width, own, heads, ncore, ny, ndp, nloc), (nloc...  101 us
    pallas_call x1, Pallas kernels, body(): pl.pallas_call(partial(tail_kernel, own, ncore, ny, ndp, nloc), in_specs=...  69.2 us
    pallas_call x1, Pallas kernels, body(): call(partial(forward_kernel, own, heads, ncore, ny, inner_total, nloc), (...  68.6 us
    pallas_call x1, Pallas kernels, body(): call(partial(gate_kernel, width, own, inner_total, ncore, ny), (nloc,), [...  34.3 us
    pallas_call x1, Pallas kernels, body(): call(partial(finish_kernel, pieces, nloc), (pieces, nloc), [placed_spec]...  16.7 us
    pallas_call x1, Pallas kernels, body(): pl.pallas_call(partial(unpack_kernel, own, heads), grid=(model // L,), in...  8.47 us

profile of v3, /device:TPU:0, one launch (start us, length us, event | category | flops | bytes accessed | tf_op | source)
XLA Modules:
  0.0 312.6 jit_solution(16450258874381574782)
XLA Ops:
  0.6 5.6 %fusion = (bf16[1024,1,512]{2,1,0:T(2,128)(2,1)S(1)}, bf16[1024,1,512]{2,1,0:T(2,128)(2,1)S(1)}) fusion(bf16[1024,2,512]{2,1,0:T(2,128)(2,1)} %param.17), kind=kLoop, calls=%fused_computation.8 | loop fusion | bytes 4194304 | tf_op jit(solution)/shard_map/slice | solution.py:1388
  6.3 0.0 copy-start.2
  6.3 0.0 copy-start.5
  6.3 0.0 copy-start
  6.3 0.0 copy-start.8
  6.3 0.0 copy-start.6
  6.3 0.0 copy-start.7
  6.3 0.0 copy-start.1
  6.3 0.0 copy-start.3
  6.4 0.0 copy-start.4
  6.4 1.9 copy_bitcast_fusion
  8.3 0.1 pad.12.clone
  8.4 0.0 copy-done.2
  8.4 0.0 copy-done.5
  8.4 0.7 maximum_maximum_fusion.bcp_ref
  9.0 0.0 copy-done
  9.0 0.2 copy.32
  9.2 0.8 pad.8.wdt_ref
  10.0 0.0 copy-done.8
  10.0 0.0 copy-done.6
  10.0 0.0 copy-done.7
  10.0 0.1 broadcast_in_dim.53
  10.1 0.1 broadcast_in_dim_reshape.3
  10.2 0.0 copy-done.1
  10.2 0.0 copy-done.3
  10.2 0.0 copy-done.4
  10.2 1.2 concatenate.6.sm_ref
  11.4 68.6 %forward.1 = (bf16[3,512,1024]{2,1,0:T(8,128)(2,1)}, f32[3,512,1024]{2,1,0:T(8,128)}, f32[3,520,1024]{2,1,0:T(8,128)}, f32[3,520,256]{2,1,0:T(8,128)}, f32[3,512...) custom-call(s32[1]{0:T(128)} %constant.34.clone.1._seq, ...), custom_call_target="tpu_custom_call" | custom-call | flops 14092861440 | bytes 40894464 | tf_op jit(solution)/shard_map/forward/pallas_call | solution.py:1409
  80.1 34.3 %gate.1 = (bf16[3,512,1024]{2,1,0:T(8,128)(2,1)}, bf16[3,512,1024]{2,1,0:T(8,128)(2,1)}, bf16[1024,512]{1,0:T(8,128)(2,1)}, bf16[1024,512]{1,0:T(8,128)(2,1)}, f...) custom-call(s32[1]{0:T(128)} %constant.34.clone.1._seq, ...), custom_call_target="tpu_custom_call" | custom-call | flops 6442450944 | bytes 31457280 | tf_op jit(solution)/shard_map/gate/pallas_call | solution.py:1498
  114.4 101.1 %scan_back.1 = (bf16[512,1024]{1,0:T(8,128)(2,1)}, bf16[1024,640]{1,0:T(8,128)(2,1)}, bf16[1024,256]{1,0:T(8,128)(2,1)}, f32[16,512]{1,0:T(8,128)}, f32[16,512]{...) custom-call(s32[1]{0:T(128)} %constant.34.clone.1._seq, ...), custom_call_target="tpu_custom_call" | custom-call | flops 15300820992 | bytes 25165824 | tf_op jit(solution)/shard_map/scan_back/pallas_call | solution.py:1562
  215.6 69.2 %tail.1 = (bf16[1024,640]{1,0:T(8,128)(2,1)}, bf16[1024,256]{1,0:T(8,128)(2,1)}, f32[16,512]{1,0:T(8,128)}, f32[8,1024]{1,0:T(8,128)}, bf16[256,1024]{1,0:T(8,12...) custom-call(bf16[1024,640]{1,0:T(8,128)(2,1)} %get-tuple-element.109.gw_ref, ...), custom_call_target="tpu_custom_call" | custom-call | tf_op jit(solution)/shard_map/tail/pallas_call | solution.py:1661
  284.7 8.5 %unpack.1 = (f32[1024,2,512]{2,1,0:T(2,128)}, f32[512,1024]{1,0:T(8,128)}, f32[1024,8]{1,0:T(8,128)}, f32[1024,256]{1,0:T(8,128)}, f32[4,512]{1,0:T(4,128)}, /*i...) custom-call(bf16[1024,512]{1,0:T(8,128)(2,1)} %get-tuple-element.130, ...), custom_call_target="tpu_custom_call" | custom-call | tf_op jit(solution)/shard_map/unpack/pallas_call | solution.py:1758
  293.2 1.8 copy.33
  295.0 0.7 pad_add_fusion._idx
  295.7 16.7 %finish.1 = (f32[6,2,256,1024]{3,2,1,0:T(8,128)}, bf16[6,2,256,1024]{3,2,1,0:T(8,128)(2,1)}) custom-call(s32[2]{0:T(128)} %pad_add_fusion._idx, bf16[6,2,256,1024]{3,2,1,0:T(8,128)(2,1)} %bitcast.43, bf16[2,256,1024]{2,1,0:T(8,128)(2,1)} %get-tuple-element.105.refs_0_, bf16[1,2,256,1024]{3,2,1,0:T(8,128)(2,1)} %get-tuple-element.106.refs_1_, ...), custom_call_target="tpu_custom_call" | custom-call | bytes 37748736 | tf_op jit(solution)/shard_map/finish/pallas_call | solution.py:1743
  (4 shorter events, 0.0 us)
Async XLA Ops:
  6.3 2.1 copy-start.2
  6.3 2.1 copy-start.5
  6.3 2.8 copy-start
  6.3 3.7 %copy-start.8 = (f32[8]{0:T(128)S(1)}, f32[8]{0:T(128)}, u32[]{:S(2)}) copy-start(f32[8]{0:T(128)} %param.25) | copy-start | bytes 100
  6.3 3.7 %copy-start.6 = (f32[8]{0:T(128)S(1)}, f32[8]{0:T(128)}, u32[]{:S(2)}) copy-start(f32[8]{0:T(128)} %param.24) | copy-start | bytes 100
  6.3 3.7 %copy-start.7 = (f32[8]{0:T(128)S(1)}, f32[8]{0:T(128)}, u32[]{:S(2)}) copy-start(f32[8]{0:T(128)} %param.26) | copy-start | bytes 100
  6.3 3.8 %copy-start.1 = (f32[4,512]{1,0:T(4,128)S(1)}, f32[4,512]{1,0:T(4,128)}, u32[]{:S(2)}) copy-start(f32[4,512]{1,0:T(4,128)} %param.20) | copy-start | bytes 24580
  6.3 3.8 %copy-start.3 = (f32[512]{0:T(512)S(1)}, f32[512]{0:T(512)}, u32[]{:S(2)}) copy-start(f32[512]{0:T(512)} %param.21) | copy-start | bytes 6148
  6.4 3.8 %copy-start.4 = (f32[512]{0:T(512)S(1)}, f32[512]{0:T(512)}, u32[]{:S(2)}) copy-start(f32[512]{0:T(512)} %param.27) | copy-start | bytes 6148

commit v4 on v3

--- a/solution.py
+++ b/solution.py
@@ -328,9 +328,8 @@
     wdt_out,
     wz_out,
     wx_out,
-    boy_ref,
-    bot_ref,
-    boty_ref,
+    z_scr,
+    u_scr,
     q_scr,
     bca_scr,
     s_scr,
@@ -350,7 +349,6 @@
     w_sems,
     po_sems,
     st_sems,
-    bo_sems,
     local,
 ):
     rows_all = x_ref.shape[0]
@@ -399,16 +397,6 @@
     def x_copy():
         return pltpu.make_async_copy(x4_ref.at[core * nloc + here - 1, yy], x_own, local.at[0])
 
-    def bo_spread(i):
-        return Spread(
-            bo_ref.at[i],
-            boy_ref.at[:, i],
-            bot_ref.at[i],
-            boty_ref.at[:, i],
-            bo_sems.at[:, i],
-            (twin, peers, ncore),
-        )
-
     @pl.when(here == 0)
     def _():
         greet(peers + ([twin] if ncore == 2 else []))
@@ -436,9 +424,9 @@
         def _(j):
             src = pl.ds(pl.multiple_of(j * 256, 256), 256)
             cols = pl.ds(pl.multiple_of(base + j * 256, 256), 256)
-            z_ref[:, cols] = nn(hid_ref[...], wz[:, src])
+            z_scr[:, cols] = nn(hid_ref[...], wz[:, src])
             xl_ref[PAD : PAD + rows_all, cols] = nn(hid_ref[...], wx[:, src])
-            u_ref[:, cols] = nt(g_ref[...], wo[src, :])
+            u_scr[:, cols] = nt(g_ref[...], wo[src, :])
 
     project(wz_ref, wx_ref, wo_ref, 0)
     bcl_ref[PAD : PAD + rows_all, :] = nn(hid_ref[...], wbc_ref[...])
@@ -491,7 +479,6 @@
         @pl.when(jnp.logical_and(early, c == rows_all // L - 1))
         def _():
             block_done()
-            start(bo_spread(here - 1).first())
 
         t0 = pl.multiple_of(c * L, L)
         rows = pl.ds(t0, L)
@@ -527,13 +514,16 @@
             y = within + jnp.exp2(ap) * cs_scr[:, lanes] + prm_ref[5:6, lanes] * x
             xs_scr[:, lanes] = (xdt * jnp.exp2(fin - ap)).astype(bf16)
             s_scr[:, lanes] = s_scr[:, lanes] * jnp.exp2(fin)
-            y_ref[rows, lanes] = y
-            z = z_ref[rows, lanes]
+            y_ref[rows, lanes] = y.astype(bf16)
+            z = z_scr[rows, lanes]
+            u = u_scr[rows, lanes]
+            z_ref[rows, lanes] = z.astype(bf16)
+            u_ref[rows, lanes] = u.astype(bf16)
             gated = y * (z * sigmoid(z))
             q = gated * prm_ref[6:7, lanes]
             q_scr[rows, lanes] = q.astype(bf16)
             squares = squares + gated * gated
-            inner = inner + u_ref[rows, lanes] * q
+            inner = inner + u * q
         s_scr[...] += nn(bm.T, xs_scr[...])
         s0 = jnp.sum(squares, axis=1, keepdims=True)
         s1 = jnp.sum(inner, axis=1, keepdims=True)
@@ -549,22 +539,10 @@
             po = po + nn(q_scr[:, own : 2 * own], wo_in[:, cols])
         po_scr[lax.rem(here, 2), :, cols] = po.astype(bf16)
 
-    @pl.when(here > 1)
-    def _():
-        wait(bo_spread(here - 2).first())
-        start(bo_spread(here - 2).second())
-
     @pl.when(here == nloc - 1)
     def _():
         po_ref[...] = po_scr[(nloc - 1) % 2]
         block_done()
-
-    @pl.when(here > 1)
-    def _():
-        wait(bo_spread(here - 2).second())
-
-    @pl.when(here == nloc - 1)
-    def _():
         if ncore == 2:
             for copy in weight_stores():
                 copy.wait()
@@ -611,9 +589,6 @@
     go_ref,
     ggg_ref,
     bo_ref,
-    boy_ref,
-    bot_ref,
-    boty_ref,
     q_scr,
     sc_scr,
     dz_scr,
@@ -627,7 +602,6 @@
     core_send,
     core_recv,
     po_sems,
-    bo_sems,
     local,
 ):
     rows_all = z_ref.shape[0]
@@ -659,14 +633,10 @@
     def x_copy():
         return pltpu.make_async_copy(x_ref.at[core * nloc + last, yy], x_own, local.at[0])
 
-    spread = Spread(
-        bo01_ref.at[last - 1], boy_ref, bot_ref, boty_ref, bo_sems, (twin, peers, ncore)
-    )
-
     @pl.when(here == 0)
     def _():
         greet(peers + ([twin] if ncore == 2 else []))
-        start(row_copies() + po_copies() + [x_copy()] + spread.first())
+        start(row_copies() + po_copies() + [x_copy()])
         stot_ref[...] = stin_ref[...]
         for i in range(last):
             bo_ref[i] = bo01_ref[i]
@@ -696,13 +666,13 @@
         for p in range(pairs):
             lanes = slice(p * L, p * L + L)
             gg = prm_ref[6:7, lanes]
-            z = z_ref[rows, lanes]
-            y = y_ref[rows, lanes]
+            z = z_ref[rows, lanes].astype(f32)
+            y = y_ref[rows, lanes].astype(f32)
             sg = sigmoid(z)
             silz = z * sg
             gated = y * silz
             q_scr[here, rows, lanes] = (gated * gg).astype(bf16)
-            dq = r * u_ref[rows, lanes]
+            dq = r * u_ref[rows, lanes].astype(f32)
             ggg_ref[:, lanes] += fold_rows(dq * gated)
             dgated = dq * gg - c2 * gated
             dy_ref[rows, lanes] = (dgated * silz).astype(bf16)
@@ -749,9 +719,6 @@
         parts = [po_in.at[d] for d in range(ny - 1)]
         mine = po_ref.at[pl.ds(pl.multiple_of(yy * Ry, Ry), Ry)]
         block_out(inner_total, stot_ref.at[last], yy, mine, parts, x_own, bo_ref.at[last])
-        wait(spread.first())
-        start(spread.second())
-        wait(spread.second())
 
 
 def scan_kernel(
@@ -855,7 +822,8 @@
     last_step = nloc_static * spans - 1
 
     place = (twin, peers, ncore)
-    bo_spread = Spread(bo_ref.at[nloc_static - 1], boy_ref, bot_ref, boty_ref, bo_sems, place)
+    some = pl.ds(0, nloc_static - 1)
+    bo_spread = Spread(bo_ref.at[some], boy_ref, bot_ref, boty_ref, bo_sems, place)
 
     def corr_spread(i):
         return Spread(
@@ -890,18 +858,19 @@
         gdt_ref[...] = jnp.zeros_like(gdt_ref)
         gpre_ref[...] = jnp.zeros_like(gpre_ref)
 
-    spans_of = ([2] + [1] * (nbits - 2) + [2])[:nbits]
-    spans_of = spans_of + spans_of[::-1]
-    for j in range(2 * nbits + 1):
-
-        @pl.when(step == sum(spans_of[:j]) * last_step // sum(spans_of))
+    when = [0.0, 0.25, 0.33, 0.58, 0.67, 0.83]
+    if nbits != 3:
+        when = [j / (2 * nbits) for j in range(2 * nbits)]
+    for j in range(2 * nbits):
+
+        @pl.when(step == int(when[j] * (last_step + 1) + 0.1))
         def _(j=j):
             for job in jobs:
                 job.close(j)
             for job in jobs:
                 job.begin(j)
 
-    @pl.when(step == spans)
+    @pl.when(step == spans + 2)
     def _():
         wait(bo_spread.first())
         start(bo_spread.second())
@@ -1119,6 +1088,8 @@
         wait(bo_spread.second())
         for i in range(nloc_static - 1):
             wait(corr_spread(i).second())
+        for job in jobs:
+            job.close(2 * nbits)
 
 
 def tail_kernel(
@@ -1135,6 +1106,7 @@
     dh_ref,
     gain_ref,
     x_ref,
+    bo_ref,
     fw_ref,
     fb_ref,
     small_out,
@@ -1143,12 +1115,16 @@
     ly_ref,
     lt_ref,
     lty_ref,
+    boy_ref,
+    bot_ref,
+    boty_ref,
     dh_in,
     x_own,
     small_in,
     core_sems,
     y_sems,
     l_sems,
+    bo_sems,
     local,
     *machine,
 ):
@@ -1185,7 +1161,9 @@
             for d in range(ny - 1)
         ]
 
-    late = Spread(last_ref, ly_ref, lt_ref, lty_ref, l_sems, (twin, peers, ncore))
+    place = (twin, peers, ncore)
+    late = Spread(last_ref, ly_ref, lt_ref, lty_ref, l_sems, place)
+    ready = [Spread(bo_ref.at[nloc - 1], boy_ref, bot_ref, boty_ref, bo_sems, place)]
     x_copy = pltpu.make_async_copy(x_ref.at[core * nloc + nloc - 1, yy], x_own, local.at[0])
     others = peers + ([twin] if ncore == 2 else [])
     greet(others + dp_peers)
@@ -1204,6 +1182,8 @@
         small_copy.start()
     turn((job_c, 1), (job_sh, 1))
     start(dh_copies())
+    for spread in ready:
+        start(spread.first())
     if ncore == 2:
         small_copy.wait()
         job_sm.acc[0] = small_ref[...] + small_in[...]
@@ -1241,19 +1221,24 @@
     turn(*smaller())
     start(late.first())
     for j in range(2, 2 * nbits + 1):
+        turn(*smaller())
         turn(*smaller(), (job_a, j), (job_b, j))
+    for spread in ready:
+        wait(spread.first())
+        start(spread.second())
     for _ in range(2 * job_c.n):
         turn(*smaller())
     small_out[...] = job_sm.acc[len(job_sm.peers)]
     shared_out[...] = job_sh.acc[len(job_sh.peers)]
     wait(late.first())
     start(late.second())
-    wait(late.second())
+    for spread in ready + [late]:
+        wait(spread.second())
 
 
 def finish_kernel(pieces, nloc, _idx, g_ref, *refs):
     gi_ref, bo_ref = refs[-2:]
-    groups = [refs[n * pieces : (n + 1) * pieces] for n in range(5)]
+    groups = [refs[n * pieces : (n + 1) * pieces] for n in range(4)]
     now = pl.program_id(1)
     for k in range(pieces):
         here = pl.program_id(0) == k
@@ -1267,7 +1252,7 @@
             def _(src=groups[n][k]):
                 gi_ref[...] = g_ref[...].astype(f32) + src[...].astype(f32)
 
-        for n, turn in ((2, now < nloc - 2), (3, now == nloc - 2), (4, now == nloc - 1)):
+        for n, turn in ((2, now < nloc - 1), (3, now == nloc - 1)):
 
             @when(turn)
             def _(src=groups[n][k]):
@@ -1405,8 +1390,7 @@
     nother = max(ny - 1, 1)
     dma = pltpu.SemaphoreType.DMA
 
-    early_n = max(nloc - 2, 1)
-    f_out = call(
+    hid, z, xl, bcl, dtl, u, y, sin, st, stot, po, bo01, prm, hp, wdt, wzo, wxo = call(
         partial(forward_kernel, own, heads, ncore, ny, inner_total, nloc),
         (nloc,),
         [
@@ -1439,15 +1423,15 @@
             whole_spec(8, L),
             whole_spec(model, L),
         ]
-        + [any_spec] * 5,
+        + [any_spec] * 2,
         [
             sds(nloc, R, model, dtype=bf16),
-            sds(nloc, R, width),
+            sds(nloc, R, width, dtype=bf16),
             sds(nloc, R + PAD, width),
             sds(nloc, R + PAD, 256),
             sds(nloc, R, L),
-            sds(nloc, R, width),
-            sds(nloc, R, width),
+            sds(nloc, R, width, dtype=bf16),
+            sds(nloc, R, width, dtype=bf16),
             sds(nloc, spans, L, width, dtype=bf16),
             sds(nloc, 2, R),
             sds(nloc, 2, R),
@@ -1458,11 +1442,10 @@
             sds(model, L, dtype=bf16),
             sds(model, own, dtype=bf16),
             sds(model, own, dtype=bf16),
-            sds(nother, early_n, Ry, model, dtype=bf16),
-            sds(early_n, Ry, model, dtype=bf16),
-            sds(nother, early_n, Ry, model, dtype=bf16),
         ],
         [
+            pltpu.VMEM((R, width), f32),
+            pltpu.VMEM((R, width), f32),
             pltpu.VMEM((R, width), bf16),
             pltpu.VMEM((R, 256), bf16),
             pltpu.VMEM((L, width), f32),
@@ -1482,7 +1465,6 @@
             dma((2, 5)),
             dma((2, nloc - 1, nother)),
             dma((2, nloc - 1, nother)),
-            dma((2, early_n, 2 * ny)),
             dma((3,)),
         ],
         "forward",
@@ -1490,12 +1472,9 @@
         nloc * R * (6 * model + 20 * width),
         4,
     )(seq0, x3, g3, gain, wz, wx, w_bc, wdt, w_out, sm, bcp, x4)
-    hid, z, xl, bcl, dtl, u, y, sin, st, stot, po, bo01, prm, hp, wdt, wzo, wxo = f_out[:17]
-    bo_early = f_out[17:]
 
     nbits = log2(ndp)
-    one = sds(nother, Ry, model, dtype=bf16)
-    dz, dy, gz, go, ggg, bo, *bo_mid = call(
+    dz, dy, gz, go, ggg, bo = call(
         partial(gate_kernel, width, own, inner_total, ncore, ny),
         (nloc,),
         [
@@ -1518,8 +1497,7 @@
             whole_spec(model, own),
             whole_spec(8, width),
             whole_spec(nloc, Ry, model),
-        ]
-        + [any_spec] * 3,
+        ],
         [
             sds(nloc, R, width, dtype=bf16),
             sds(nloc, R, width, dtype=bf16),
@@ -1527,9 +1505,6 @@
             sds(model, own, dtype=bf16),
             sds(8, width),
             sds(nloc, Ry, model, dtype=bf16),
-            one,
-            sds(Ry, model, dtype=bf16),
-            one,
         ],
         [
             pltpu.VMEM((nloc, R, width), bf16),
@@ -1545,7 +1520,6 @@
             dma,
             dma,
             dma((2, nother)),
-            dma((2, 2 * ny)),
             dma((1,)),
         ],
         "gate",
@@ -1606,9 +1580,9 @@
             sds(nloc - 1, Ry, model, dtype=bf16),
             sds(model, own, dtype=bf16),
             sds(model, own, dtype=bf16),
-            one,
-            sds(Ry, model, dtype=bf16),
-            one,
+            sds(nother, nloc - 1, Ry, model, dtype=bf16),
+            sds(nloc - 1, Ry, model, dtype=bf16),
+            sds(nother, nloc - 1, Ry, model, dtype=bf16),
             sds(nother, nloc - 1, Ry, model, dtype=bf16),
             sds(nloc - 1, Ry, model, dtype=bf16),
             sds(nother, nloc - 1, Ry, model, dtype=bf16),
@@ -1658,26 +1632,25 @@
     vm = pl.BlockSpec(memory_space=pltpu.VMEM)
     tbits = log2(nt)
     late_shape = sds(nother, Ry, model, dtype=bf16)
-    fw, fb, small, shared, last, ly, lt, lty = pl.pallas_call(
+    fw, fb, small, shared, last, *late_got = pl.pallas_call(
         partial(tail_kernel, own, ncore, ny, ndp, nloc),
-        in_specs=[vm] * 7 + [any_spec],
-        out_specs=[any_spec] * 2 + [vm] * 3 + [any_spec] * 3,
+        in_specs=[vm] * 7 + [any_spec] * 2,
+        out_specs=[any_spec] * 2 + [vm] * 3 + [any_spec] * 6,
         out_shape=[
             sds(model, own + L, dtype=bf16),
             sds(model, 256, dtype=bc_type),
             sds(16, own),
             sds(8, model),
             sds(Ry, model, dtype=bf16),
-            late_shape,
-            sds(Ry, model, dtype=bf16),
-            late_shape,
-        ],
+        ]
+        + [late_shape, sds(Ry, model, dtype=bf16), late_shape] * 2,
         scratch_shapes=[
             pltpu.VMEM((nother, Ry, model), bf16),
             pltpu.VMEM((Ry, model), bf16),
             pltpu.VMEM((16, own), f32),
             dma((2,)),
             dma((2, nother)),
+            dma((2, 2 * ny)),
             dma((2, 2 * ny)),
             dma((1,)),
         ]
@@ -1688,7 +1661,7 @@
         + Doubling.scratch(nbits + tbits, 8, model),
         compiler_params=pltpu.CompilerParams(collective_id=3, has_side_effects=True),
         name="tail",
-    )(gw2, gbcw, small, other, shared, dh, gain, x4)
+    )(gw2, gbcw, small, other, shared, dh, gain, x4, bo)
 
     pieces = ncore * ny
     where = jnp.stack([core, yy]).astype(jnp.int32)
@@ -1730,16 +1703,14 @@
     def as_seq(v, axis):
         return jnp.expand_dims(v, axis)
 
+    def add_late(first, mine, base, got):
+        toy, tot, toty = got
+        add_group(first, 1, mine, base, as_seq(toy, 1), as_seq(tot, 0), as_seq(toty, 1))
+
     add_group(0, nloc - 1, corr, 0, cy0, ct0, cty0)
-    add_group(nloc - 1, 1, as_seq(last, 0), nloc - 1, as_seq(ly, 1), as_seq(lt, 0), as_seq(lty, 1))
-
-    def add_late(first, got):
-        toy, tot, toty = got
-        add_group(first, 1, bo, 0, as_seq(toy, 1), as_seq(tot, 0), as_seq(toty, 1))
-
-    add_group(0, early_n, bo, 0, *bo_early)
-    add_late(nloc - 2, bo_mid)
-    add_late(nloc - 1, (boy, bot, boty))
+    add_late(nloc - 1, as_seq(last, 0), nloc - 1, late_got[0:3])
+    add_group(0, nloc - 1, bo, 0, boy, bot, boty)
+    add_late(nloc - 1, bo, 0, late_got[3:6])
     grad_input, block_output = call(
         partial(finish_kernel, pieces, nloc),
         (pieces, nloc),

time: 314 us -> 282 us (0.90)
  Pallas kernels: 298 us -> 268 us
    pallas_call x1, Pallas kernels: 101 us -> 89 us  [body(): call(partial(scan_kernel, width, own, heads, ncore, ny, ndp, nloc), (nloc...]
    pallas_call x1, Pallas kernels: 68.6 us -> 60.5 us  [body(): call(partial(forward_kernel, own, heads, ncore, ny, inner_total, nloc), (...]
    pallas_call x1, Pallas kernels: 34.3 us -> 27 us  [body(): call(partial(gate_kernel, width, own, inner_total, ncore, ny), (nloc,), [...]
where the time goes in v4:
time: 282 us
  Pallas kernels  268 us (95%)
  local copies, waits for them, and re-layouts  11.8 us (4%)
    pallas_call x1, Pallas kernels, body(): call(partial(scan_kernel, width, own, heads, ncore, ny, ndp, nloc), (nloc...  89 us
    pallas_call x1, Pallas kernels, body(): pl.pallas_call(partial(tail_kernel, own, ncore, ny, ndp, nloc), in_specs=...  66.2 us
    pallas_call x1, Pallas kernels, body(): call(partial(forward_kernel, own, heads, ncore, ny, inner_total, nloc), (...  60.5 us
    pallas_call x1, Pallas kernels, body(): call(partial(gate_kernel, width, own, inner_total, ncore, ny), (nloc,), [...  27 us
    pallas_call x1, Pallas kernels, body(): call(partial(finish_kernel, pieces, nloc), (pieces, nloc), [placed_spec]...  16.5 us
    pallas_call x1, Pallas kernels, body(): pl.pallas_call(partial(unpack_kernel, own, heads), grid=(model // L,), in...  8.47 us

profile of v4, /device:TPU:0, one launch (start us, length us, event | category | flops | bytes accessed | tf_op | source)
XLA Modules:
  0.0 281.7 jit_solution(12660396107466037655)
XLA Ops:
  0.6 5.6 %fusion = (bf16[1024,1,512]{2,1,0:T(2,128)(2,1)S(1)}, bf16[1024,1,512]{2,1,0:T(2,128)(2,1)S(1)}) fusion(bf16[1024,2,512]{2,1,0:T(2,128)(2,1)} %param.17), kind=kLoop, calls=%fused_computation.8 | loop fusion | bytes 4194304 | tf_op jit(solution)/shard_map/slice | solution.py:1373
  6.3 0.0 copy-start.2
  6.3 0.0 copy-start.5
  6.3 0.0 copy-start
  6.3 0.0 copy-start.8
  6.3 0.0 copy-start.6
  6.3 0.0 copy-start.7
  6.3 0.0 copy-start.1
  6.3 0.0 copy-start.3
  6.4 0.0 copy-start.4
  6.4 1.9 copy_bitcast_fusion
  8.3 0.1 pad.12.clone
  8.4 0.0 copy-done.2
  8.4 0.0 copy-done.5
  8.4 0.7 maximum_maximum_fusion.bcp_ref
  9.0 0.0 copy-done
  9.0 0.2 copy.32
  9.2 0.8 pad.8.wdt_ref
  10.0 0.0 copy-done.8
  10.0 0.0 copy-done.6
  10.0 0.0 copy-done.7
  10.0 0.1 broadcast_in_dim.44
  10.1 0.1 broadcast_in_dim_reshape.3
  10.2 0.0 copy-done.1
  10.2 0.0 copy-done.3
  10.2 0.0 copy-done.4
  10.2 1.2 concatenate.6.sm_ref
  11.4 60.5 %forward.1 = (bf16[3,512,1024]{2,1,0:T(8,128)(2,1)}, bf16[3,512,1024]{2,1,0:T(8,128)(2,1)}, f32[3,520,1024]{2,1,0:T(8,128)}, f32[3,520,256]{2,1,0:T(8,128)}, f32...) custom-call(s32[1]{0:T(128)} %constant.34.clone.1._seq, ...), custom_call_target="tpu_custom_call" | custom-call | flops 14092861440 | bytes 40894464 | tf_op jit(solution)/shard_map/forward/pallas_call | solution.py:1393
  71.9 27.0 %gate.1 = (bf16[3,512,1024]{2,1,0:T(8,128)(2,1)}, bf16[3,512,1024]{2,1,0:T(8,128)(2,1)}, bf16[1024,512]{1,0:T(8,128)(2,1)}, bf16[1024,512]{1,0:T(8,128)(2,1)}, f...) custom-call(s32[1]{0:T(128)} %constant.34.clone.1._seq, f32[3,2,512]{2,1,0:T(2,128)} %get-tuple-element.80.st_ref, ...), custom_call_target="tpu_custom_call" | custom-call | flops 6442450944 | bytes 31457280 | tf_op jit(solution)/shard_map/gate/pallas_call | solution.py:1477
  98.9 89.0 %scan_back.1 = (bf16[512,1024]{1,0:T(8,128)(2,1)}, bf16[1024,640]{1,0:T(8,128)(2,1)}, bf16[1024,256]{1,0:T(8,128)(2,1)}, f32[16,512]{1,0:T(8,128)}, f32[16,512]{...) custom-call(s32[1]{0:T(128)} %constant.34.clone.1._seq, ...), custom_call_target="tpu_custom_call" | custom-call | flops 15300820992 | bytes 25165824 | tf_op jit(solution)/shard_map/scan_back/pallas_call | solution.py:1536
  187.9 66.2 %tail.1 = (bf16[1024,640]{1,0:T(8,128)(2,1)}, bf16[1024,256]{1,0:T(8,128)(2,1)}, f32[16,512]{1,0:T(8,128)}, f32[8,1024]{1,0:T(8,128)}, bf16[256,1024]{1,0:T(8,12...) custom-call(bf16[1024,640]{1,0:T(8,128)(2,1)} %get-tuple-element.106, ...), custom_call_target="tpu_custom_call" | custom-call | tf_op jit(solution)/shard_map/tail/pallas_call | solution.py:1635
  254.1 8.5 %unpack.1 = (f32[1024,2,512]{2,1,0:T(2,128)}, f32[512,1024]{1,0:T(8,128)}, f32[1024,8]{1,0:T(8,128)}, f32[1024,256]{1,0:T(8,128)}, f32[4,512]{1,0:T(4,128)}, /*i...) custom-call(bf16[1024,512]{1,0:T(8,128)(2,1)} %get-tuple-element.124, ...), custom_call_target="tpu_custom_call" | custom-call | tf_op jit(solution)/shard_map/unpack/pallas_call | solution.py:1729
  262.6 1.8 copy.33
  264.4 0.6 pad_add_fusion._idx
  265.0 16.5 %finish.1 = (f32[6,2,256,1024]{3,2,1,0:T(8,128)}, bf16[6,2,256,1024]{3,2,1,0:T(8,128)(2,1)}) custom-call(s32[2]{0:T(128)} %pad_add_fusion._idx, bf16[6,2,256,1024]{3,2,1,0:T(8,128)(2,1)} %bitcast.40, bf16[2,256,1024]{2,1,0:T(8,128)(2,1)} %get-tuple-element.102.refs_0_, bf16[1,2,256,1024]{3,2,1,0:T(8,128)(2,1)} %get-tuple-element.103.refs_1_, ...), custom_call_target="tpu_custom_call" | custom-call | bytes 37748736 | tf_op jit(solution)/shard_map/finish/pallas_call | solution.py:1714
  (4 shorter events, 0.0 us)
Async XLA Ops:
  6.3 2.1 copy-start.2
  6.3 2.1 copy-start.5
  6.3 2.8 copy-start
  6.3 3.7 %copy-start.8 = (f32[8]{0:T(128)S(1)}, f32[8]{0:T(128)}, u32[]{:S(2)}) copy-start(f32[8]{0:T(128)} %param.25) | copy-start | bytes 100
  6.3 3.7 %copy-start.6 = (f32[8]{0:T(128)S(1)}, f32[8]{0:T(128)}, u32[]{:S(2)}) copy-start(f32[8]{0:T(128)} %param.24) | copy-start | bytes 100
  6.3 3.7 %copy-start.7 = (f32[8]{0:T(128)S(1)}, f32[8]{0:T(128)}, u32[]{:S(2)}) copy-start(f32[8]{0:T(128)} %param.26) | copy-start | bytes 100
  6.3 3.8 %copy-start.1 = (f32[4,512]{1,0:T(4,128)S(1)}, f32[4,512]{1,0:T(4,128)}, u32[]{:S(2)}) copy-start(f32[4,512]{1,0:T(4,128)} %param.20) | copy-start | bytes 24580
  6.3 3.8 %copy-start.3 = (f32[512]{0:T(512)S(1)}, f32[512]{0:T(512)}, u32[]{:S(2)}) copy-start(f32[512]{0:T(512)} %param.21) | copy-start | bytes 6148
  6.4 3.8 %copy-start.4 = (f32[512]{0:T(512)S(1)}, f32[512]{0:T(512)}, u32[]{:S(2)}) copy-start(f32[512]{0:T(512)} %param.27) | copy-start | bytes 6148

commit v5 on v4

--- a/solution.py
+++ b/solution.py
@@ -721,6 +721,118 @@
         block_out(inner_total, stot_ref.at[last], yy, mine, parts, x_own, bo_ref.at[last])
 
 
+def tail_part(own, ncore, ny, ndp, nloc, given, outs, late_to, ready_to, room, machine):
+    gw_ref, gbcw_ref, small_ref, other_ref, shared_ref, dh_ref, gain_ref, x_ref, bo_ref = given
+    fw_ref, fb_ref, small_out, shared_out, last_ref = outs
+    dh_in, x_own, small_in, core_sems, y_sems, local = room
+    model = gw_ref.shape[0]
+    Ry = x_own.shape[0]
+    core, yy, twin, ys, peers = places(ncore, ny)
+    nbits = log2(ndp)
+    dp_peers, dp_bits = bit_peers("dp", 1, 0, nbits)
+    t_peers, t_bits = bit_peers("tensor", 1, 0, log2(ncore * ny))
+    links = list(zip(dp_peers, dp_bits))
+    swapped = [links[1], links[0]] + links[2:] if nbits > 1 else links
+    t_links = list(zip(t_peers, t_bits))
+    per = nbits + 2
+    a, b = machine[:per], machine[per : 2 * per]
+    per_bc = nbits + len(t_links) + 2
+    c = machine[2 * per : 2 * per + per_bc]
+    sm, sh = machine[2 * per + per_bc : 2 * per + per_bc + 3], machine[2 * per + per_bc + 3 :]
+    mid = model // 2
+    job_a = Halving(links, mid, gw_ref.at[0:mid], a[0], a[1:-1], fw_ref.at[0:mid], a[-1])
+    job_b = Halving(swapped, mid, gw_ref.at[mid:model], b[0], b[1:-1], fw_ref.at[mid:model], b[-1])
+    job_c = Halving(t_links + links, model, gbcw_ref, c[0], c[1:-1], fb_ref, c[-1])
+    job_sm = Doubling(dp_peers, *sm)
+    job_sh = Doubling(t_peers + dp_peers, *sh)
+
+    def dh_copies():
+        return [
+            remote(
+                dh_ref.at[pl.ds(pl.multiple_of(ys[d] * Ry, Ry), Ry)],
+                dh_in.at[d],
+                y_sems.at[0, d],
+                y_sems.at[1, d],
+                peers[d],
+            )
+            for d in range(ny - 1)
+        ]
+
+    place = (twin, peers, ncore)
+    late = Spread(last_ref, *late_to, place)
+    ready = [Spread(bo_ref.at[nloc - 1], *ready_to, place)]
+    x_copy = pltpu.make_async_copy(x_ref.at[core * nloc + nloc - 1, yy], x_own, local.at[1])
+    start(dh_copies())
+    x_copy.start()
+    yield
+
+    def turn(*pairs):
+        for job, j in pairs:
+            job.close(j)
+        for job, j in pairs:
+            job.begin(j)
+
+    job_sh.acc[0] = shared_ref[...]
+    turn((job_sh, 0), (job_c, 0), (job_a, 0), (job_b, 0))
+    if ncore == 2:
+        small_copy = remote(other_ref, small_in, core_sems.at[0], core_sems.at[1], twin)
+        small_copy.start()
+    turn((job_c, 1), (job_sh, 1))
+    for spread in ready:
+        start(spread.first())
+    if ncore == 2:
+        small_copy.wait()
+        job_sm.acc[0] = small_ref[...] + small_in[...]
+    else:
+        job_sm.acc[0] = small_ref[...]
+    turn((job_sm, 0))
+    steps = [
+        (job_c, iter(range(2, 2 * job_c.n + 1))),
+        (job_sm, iter(range(1, len(job_sm.peers) + 1))),
+        (job_sh, iter(range(2, len(job_sh.peers) + 1))),
+    ]
+
+    def smaller():
+        found = []
+        for job, left in steps:
+            j = next(left, None)
+            if j is not None:
+                found.append((job, j))
+        return found
+
+    turn(*smaller(), (job_a, 1), (job_b, 1))
+    for copy in dh_copies():
+        copy.wait()
+    x_copy.wait()
+
+    @pl.loop(0, Ry // 32)
+    def _(i):
+        rows = pl.ds(pl.multiple_of(i * 32, 32), 32)
+        mine = pl.ds(pl.multiple_of(yy * Ry + i * 32, 32), 32)
+        dh = dh_ref[mine, :].astype(f32)
+        for d in range(ny - 1):
+            dh = dh + dh_in[d, rows, :].astype(f32)
+        last_ref[rows, :] = correction(x_own[rows, :], dh, gain_ref[...]).astype(bf16)
+
+    turn(*smaller())
+    start(late.first())
+    for j in range(2, 2 * nbits + 1):
+        turn(*smaller())
+        turn(*smaller(), (job_a, j), (job_b, j))
+    for spread in ready:
+        wait(spread.first())
+        start(spread.second())
+    for _ in range(2 * job_c.n):
+        turn(*smaller())
+    small_out[...] = job_sm.acc[len(job_sm.peers)]
+    shared_out[...] = job_sh.acc[len(job_sh.peers)]
+    wait(late.first())
+    start(late.second())
+    for spread in ready + [late]:
+        wait(spread.second())
+    yield
+
+
 def scan_kernel(
     width,
     own,
@@ -752,13 +864,10 @@
     go_ref,
     bo_ref,
     x_ref,
-    dh_ref,
-    gw_ref,
-    gbcw_ref,
-    small_ref,
-    other_ref,
-    shared_ref,
     corr_ref,
+    small_out,
+    shared_out,
+    last_ref,
     fz_ref,
     fo_ref,
     boy_ref,
@@ -767,6 +876,14 @@
     cy_ref,
     ct_ref,
     cty_ref,
+    fw_ref,
+    fb_ref,
+    ly_ref,
+    lt_ref,
+    lty_ref,
+    zy_ref,
+    zt_ref,
+    zty_ref,
     d_scr,
     bcc_scr,
     bca_scr,
@@ -799,6 +916,18 @@
     bo_sems,
     c_sems,
     local,
+    gw_ref,
+    gbcw_ref,
+    small_ref,
+    other_ref,
+    shared_ref,
+    small_in,
+    end_in,
+    x_end,
+    core_sems,
+    end_sems,
+    l_sems,
+    z_sems,
     *machine,
 ):
     rows_all = dz_ref.shape[0]
@@ -813,8 +942,8 @@
     dp_peers, dp_bits = bit_peers("dp", 1, 0, nbits)
     links = list(zip(dp_peers, dp_bits))
     swapped = [links[1], links[0]] + links[2:] if nbits > 1 else links
-    half = len(machine) // 2
-    mz, mo = machine[:half], machine[half:]
+    per = nbits + 2
+    mz, mo, rest = machine[:per], machine[per : 2 * per], machine[2 * per :]
     jobs = [
         Halving(links, model, gz_ref, mz[0], mz[1:-1], fz_ref, mz[-1]),
         Halving(swapped, model, go_ref, mo[0], mo[1:-1], fo_ref, mo[-1]),
@@ -1047,14 +1176,25 @@
 
     @pl.when(step == last_step)
     def _():
-        tail = acc_scr[:, width + 256 : width + 384]
+        end = tail_part(
+            own,
+            ncore,
+            ny,
+            ndp,
+            nloc_static,
+            (gw_ref, gbcw_ref, small_ref, other_ref, shared_ref, dh_scr, gain_ref, x_ref, bo_ref),
+            (fw_ref, fb_ref, small_out, shared_out, last_ref),
+            (ly_ref, lt_ref, lty_ref, l_sems),
+            (zy_ref, zt_ref, zty_ref, z_sems),
+            (end_in, x_end, small_in, core_sems, end_sems, local),
+            rest,
+        )
+        next(end)
         if ncore == 2:
-            send_scr[:, 0:own] = acc_scr[:, own:width].astype(bf16)
-            send_scr[:, own : own + L] = tail.astype(bf16)
-        dh_ref[...] = dh_scr[...]
+            send_scr[...] = acc_scr[:, own:width].astype(bf16)
+            copy = remote(send_scr, recv_scr, core_send, core_recv, twin)
         gbcw_ref[...] = acc_scr[:, width : width + 256].astype(gbcw_ref.dtype)
         if ncore == 2:
-            copy = remote(send_scr, recv_scr, core_send, core_recv, twin)
             copy.start()
         rows = [jnp.sum(gx_ref[k], axis=0, keepdims=True) for k in range(6)]
         rows.append(jnp.sum(ggg_ref[...], axis=0, keepdims=True))
@@ -1065,6 +1205,12 @@
             small_ref[k : k + 1, :] = rows[k][:, 0:own]
             if ncore == 2:
                 other_ref[k : k + 1, :] = rows[k][:, own:width]
+        for d in range(model // L):
+            turned = acc_scr[d * L : d * L + L, width + 256 : width + 384].T
+            line, lanes = 16 + heads * (d * L // own), slice(d * L % own, d * L % own + L)
+            small_ref[line : line + heads, lanes] = turned[0:heads]
+            if ncore == 2:
+                other_ref[line : line + heads, lanes] = turned[heads : 2 * heads]
         for k in range(2):
             small_ref[7 + k : 8 + k, 0:L] = dts[k]
             if ncore == 2:
@@ -1074,166 +1220,27 @@
         shared_ref[0:1, :] = jnp.sum(gpre_ref[...], axis=0, keepdims=True) / gain_ref[...]
         for k in range(5):
             shared_ref[k + 1 : k + 2, 0:256] = jnp.sum(gbc_ref[k], axis=0, keepdims=True)
+        for job in jobs:
+            job.close(2 * nbits)
         if ncore == 2:
             copy.wait()
-            theirs = recv_scr[...].astype(f32)
-            gw_ref[:, 0:own] = (acc_scr[:, 0:own] + theirs[:, 0:own]).astype(bf16)
-            tail = tail + pltpu.roll(theirs[:, own : own + L], L - heads, axis=1)
-        else:
-            gw_ref[:, 0:own] = acc_scr[:, 0:own].astype(bf16)
-        gw_ref[:, own : own + L] = tail.astype(bf16)
+
+        @pl.loop(0, model // 64)
+        def _(i):
+            rows = pl.ds(pl.multiple_of(i * 64, 64), 64)
+            total = acc_scr[rows, 0:own]
+            if ncore == 2:
+                total = total + recv_scr[rows, :].astype(f32)
+            gw_ref[rows, :] = total.astype(bf16)
+
+        for _ in end:
+            pass
         final = corr_spread(nloc_static - 2)
         wait(final.first())
         start(final.second())
         wait(bo_spread.second())
         for i in range(nloc_static - 1):
             wait(corr_spread(i).second())
-        for job in jobs:
-            job.close(2 * nbits)
-
-
-def tail_kernel(
-    own,
-    ncore,
-    ny,
-    ndp,
-    nloc,
-    gw_ref,
-    gbcw_ref,
-    small_ref,
-    other_ref,
-    shared_ref,
-    dh_ref,
-    gain_ref,
-    x_ref,
-    bo_ref,
-    fw_ref,
-    fb_ref,
-    small_out,
-    shared_out,
-    last_ref,
-    ly_ref,
-    lt_ref,
-    lty_ref,
-    boy_ref,
-    bot_ref,
-    boty_ref,
-    dh_in,
-    x_own,
-    small_in,
-    core_sems,
-    y_sems,
-    l_sems,
-    bo_sems,
-    local,
-    *machine,
-):
-    model = gw_ref.shape[0]
-    Ry = x_own.shape[0]
-    core, yy, twin, ys, peers = places(ncore, ny)
-    nbits = log2(ndp)
-    dp_peers, dp_bits = bit_peers("dp", 1, 0, nbits)
-    t_peers, t_bits = bit_peers("tensor", 1, 0, log2(ncore * ny))
-    links = list(zip(dp_peers, dp_bits))
-    swapped = [links[1], links[0]] + links[2:] if nbits > 1 else links
-    t_links = list(zip(t_peers, t_bits))
-    per = nbits + 2
-    a, b = machine[:per], machine[per : 2 * per]
-    per_bc = nbits + len(t_links) + 2
-    c = machine[2 * per : 2 * per + per_bc]
-    sm, sh = machine[2 * per + per_bc : 2 * per + per_bc + 3], machine[2 * per + per_bc + 3 :]
-    mid = model // 2
-    job_a = Halving(links, mid, gw_ref.at[0:mid], a[0], a[1:-1], fw_ref.at[0:mid], a[-1])
-    job_b = Halving(swapped, mid, gw_ref.at[mid:model], b[0], b[1:-1], fw_ref.at[mid:model], b[-1])
-    job_c = Halving(t_links + links, model, gbcw_ref, c[0], c[1:-1], fb_ref, c[-1])
-    job_sm = Doubling(dp_peers, *sm)
-    job_sh = Doubling(t_peers + dp_peers, *sh)
-
-    def dh_copies():
-        return [
-            remote(
-                dh_ref.at[pl.ds(pl.multiple_of(ys[d] * Ry, Ry), Ry)],
-                dh_in.at[d],
-                y_sems.at[0, d],
-                y_sems.at[1, d],
-                peers[d],
-            )
-            for d in range(ny - 1)
-        ]
-
-    place = (twin, peers, ncore)
-    late = Spread(last_ref, ly_ref, lt_ref, lty_ref, l_sems, place)
-    ready = [Spread(bo_ref.at[nloc - 1], boy_ref, bot_ref, boty_ref, bo_sems, place)]
-    x_copy = pltpu.make_async_copy(x_ref.at[core * nloc + nloc - 1, yy], x_own, local.at[0])
-    others = peers + ([twin] if ncore == 2 else [])
-    greet(others + dp_peers)
-    x_copy.start()
-
-    def turn(*pairs):
-        for job, j in pairs:
-            job.close(j)
-        for job, j in pairs:
-            job.begin(j)
-
-    job_sh.acc[0] = shared_ref[...]
-    turn((job_sh, 0), (job_c, 0), (job_a, 0), (job_b, 0))
-    if ncore == 2:
-        small_copy = remote(other_ref, small_in, core_sems.at[0], core_sems.at[1], twin)
-        small_copy.start()
-    turn((job_c, 1), (job_sh, 1))
-    start(dh_copies())
-    for spread in ready:
-        start(spread.first())
-    if ncore == 2:
-        small_copy.wait()
-        job_sm.acc[0] = small_ref[...] + small_in[...]
-    else:
-        job_sm.acc[0] = small_ref[...]
-    turn((job_sm, 0))
-    steps = [
-        (job_c, iter(range(2, 2 * job_c.n + 1))),
-        (job_sm, iter(range(1, len(job_sm.peers) + 1))),
-        (job_sh, iter(range(2, len(job_sh.peers) + 1))),
-    ]
-
-    def smaller():
-        found = []
-        for job, left in steps:
-            j = next(left, None)
-            if j is not None:
-                found.append((job, j))
-        return found
-
-    turn(*smaller(), (job_a, 1), (job_b, 1))
-    for copy in dh_copies():
-        copy.wait()
-    x_copy.wait()
-
-    @pl.loop(0, Ry // 32)
-    def _(i):
-        rows = pl.ds(pl.multiple_of(i * 32, 32), 32)
-        mine = pl.ds(pl.multiple_of(yy * Ry + i * 32, 32), 32)
-        dh = dh_ref[mine, :].astype(f32)
-        for d in range(ny - 1):
-            dh = dh + dh_in[d, rows, :].astype(f32)
-        last_ref[rows, :] = correction(x_own[rows, :], dh, gain_ref[...]).astype(bf16)
-
-    turn(*smaller())
-    start(late.first())
-    for j in range(2, 2 * nbits + 1):
-        turn(*smaller())
-        turn(*smaller(), (job_a, j), (job_b, j))
-    for spread in ready:
-        wait(spread.first())
-        start(spread.second())
-    for _ in range(2 * job_c.n):
-        turn(*smaller())
-    small_out[...] = job_sm.acc[len(job_sm.peers)]
-    shared_out[...] = job_sh.acc[len(job_sh.peers)]
-    wait(late.first())
-    start(late.second())
-    for spread in ready + [late]:
-        wait(spread.second())
 
 
 def finish_kernel(pieces, nloc, _idx, g_ref, *refs):
@@ -1264,7 +1271,16 @@
     gcxw_ref, gcxb_ref, gd_ref, ggg_ref, gdtb_ref, galog_ref, gpre_ref, gcbw_ref, gcbb_ref = outs[4:]
     gzx_ref[:, 0, :] = gz_ref[...].astype(f32)
     gzx_ref[:, 1, :] = gw_ref[:, 0:own].astype(f32)
-    gwdt_ref[...] = gw_ref[:, own : own + L].astype(f32)[:, 0:heads]
+    for d in range(gpre_ref.shape[1] // L):
+
+        @pl.when(pl.program_id(0) == d)
+        def _(d=d):
+            line = 16 + heads * (d * L // own)
+            rows = small_ref[line : line + heads, d * L % own : d * L % own + L]
+            if heads < 8:
+                rows = jnp.concatenate([rows, jnp.zeros((8 - heads, L), f32)], axis=0)
+            gwdt_ref[...] = rows.T[:, 0:heads]
+
     gwbc_ref[...] = fb_ref[...].astype(f32)
     v = go_ref[...].astype(f32)
     for k in range(own // L):
@@ -1532,8 +1548,11 @@
         zeros = (0,) * len(shape)
         return pl.BlockSpec((None,) + shape, lambda i, b, s: (i,) + zeros)
 
+    tbits = log2(nt)
+    lines = 16 + heads * model // own
+    late_shape = sds(nother, Ry, model, dtype=bf16)
     bc_type = bf16 if (model // (nt * ndp)) % 16 == 0 else f32
-    dh, gw2, gbcw, small, other, shared, corr, fz, fo, boy, bot, boty, cy0, ct0, cty0 = call(
+    s_out = call(
         partial(scan_kernel, width, own, heads, ncore, ny, ndp, nloc),
         (nloc, spans),
         [
@@ -1561,23 +1580,17 @@
             any_spec,
         ],
         [
-            whole_spec(R, model),
-            whole_spec(model, own + L),
-            whole_spec(model, 256),
-            whole_spec(16, own),
-            whole_spec(16, own),
+            whole_spec(nloc - 1, Ry, model),
+            whole_spec(lines, own),
             whole_spec(8, model),
-            whole_spec(nloc - 1, Ry, model),
+            whole_spec(Ry, model),
         ]
-        + [any_spec] * 8,
+        + [any_spec] * 16,
         [
-            sds(R, model, dtype=bf16),
-            sds(model, own + L, dtype=bf16),
-            sds(model, 256, dtype=bc_type),
-            sds(16, own),
-            sds(16, own),
+            sds(nloc - 1, Ry, model, dtype=bf16),
+            sds(lines, own),
             sds(8, model),
-            sds(nloc - 1, Ry, model, dtype=bf16),
+            sds(Ry, model, dtype=bf16),
             sds(model, own, dtype=bf16),
             sds(model, own, dtype=bf16),
             sds(nother, nloc - 1, Ry, model, dtype=bf16),
@@ -1586,7 +1599,10 @@
             sds(nother, nloc - 1, Ry, model, dtype=bf16),
             sds(nloc - 1, Ry, model, dtype=bf16),
             sds(nother, nloc - 1, Ry, model, dtype=bf16),
-        ],
+            sds(model, own, dtype=bf16),
+            sds(model, 256, dtype=bc_type),
+        ]
+        + [late_shape, sds(Ry, model, dtype=bf16), late_shape] * 2,
         [
             pltpu.VMEM((R, width + 384), bf16),
             pltpu.VMEM((R, 256), f32),
@@ -1609,8 +1625,8 @@
             pltpu.VMEM((2, 8, L), f32),
             pltpu.VMEM((8, model), f32),
             pltpu.VMEM((model, width + 384), f32),
-            pltpu.VMEM((model, own + L), bf16),
-            pltpu.VMEM((model, own + L), bf16),
+            pltpu.VMEM((model, own), bf16),
+            pltpu.VMEM((model, own), bf16),
             pltpu.VMEM((R, model), bf16),
             pltpu.VMEM((nloc - 1, nother, Ry, model), bf16),
             pltpu.VMEM((Ry, model), bf16),
@@ -1619,50 +1635,35 @@
             dma((2, nloc - 1, nother)),
             dma((2, 2 * ny)),
             dma((2, nloc - 1, 2 * ny)),
-            dma((1,)),
+            dma((2,)),
+            pltpu.VMEM((model, own), bf16),
+            pltpu.VMEM((model, 256), bc_type),
+            pltpu.VMEM((lines, own), f32),
+            pltpu.VMEM((lines, own), f32),
+            pltpu.VMEM((8, model), f32),
+            pltpu.VMEM((lines, own), f32),
+            pltpu.VMEM((nother, Ry, model), bf16),
+            pltpu.VMEM((Ry, model), bf16),
+            dma((2,)),
+            dma((2, nother)),
+            dma((2, 2 * ny)),
+            dma((2, 2 * ny)),
         ]
         + Halving.scratch(model, own, nbits, bf16)
-        + Halving.scratch(model, own, nbits, bf16),
+        + Halving.scratch(model, own, nbits, bf16)
+        + Halving.scratch(model // 2, own, nbits, bf16)
+        + Halving.scratch(model // 2, own, nbits, bf16)
+        + Halving.scratch(model, 256, nbits + tbits, bc_type)
+        + Doubling.scratch(nbits, lines, own)
+        + Doubling.scratch(nbits + tbits, 8, model),
         "scan_back",
         2 * nloc * R * model * (2 * wtot),
         nloc * R * (4 * model + 12 * width),
         2,
     )(seq0, hid, dz, dy, xl, bcl, dtl, sin, wz, wzo, wx, wxo, w_bc, wdt, prm, bcp, hp, ggg, gain, gz, go, bo, x4)
 
-    vm = pl.BlockSpec(memory_space=pltpu.VMEM)
-    tbits = log2(nt)
-    late_shape = sds(nother, Ry, model, dtype=bf16)
-    fw, fb, small, shared, last, *late_got = pl.pallas_call(
-        partial(tail_kernel, own, ncore, ny, ndp, nloc),
-        in_specs=[vm] * 7 + [any_spec] * 2,
-        out_specs=[any_spec] * 2 + [vm] * 3 + [any_spec] * 6,
-        out_shape=[
-            sds(model, own + L, dtype=bf16),
-            sds(model, 256, dtype=bc_type),
-            sds(16, own),
-            sds(8, model),
-            sds(Ry, model, dtype=bf16),
-        ]
-        + [late_shape, sds(Ry, model, dtype=bf16), late_shape] * 2,
-        scratch_shapes=[
-            pltpu.VMEM((nother, Ry, model), bf16),
-            pltpu.VMEM((Ry, model), bf16),
-            pltpu.VMEM((16, own), f32),
-            dma((2,)),
-            dma((2, nother)),
-            dma((2, 2 * ny)),
-            dma((2, 2 * ny)),
-            dma((1,)),
-        ]
-        + Halving.scratch(model // 2, own + L, nbits, bf16)
-        + Halving.scratch(model // 2, own + L, nbits, bf16)
-        + Halving.scratch(model, 256, nbits + tbits, bc_type)
-        + Doubling.scratch(nbits, 16, own)
-        + Doubling.scratch(nbits + tbits, 8, model),
-        compiler_params=pltpu.CompilerParams(collective_id=3, has_side_effects=True),
-        name="tail",
-    )(gw2, gbcw, small, other, shared, dh, gain, x4, bo)
-
+    corr, small, shared, last, fz, fo, boy, bot, boty, cy0, ct0, cty0, fw, fb = s_out[:14]
+    late_got = s_out[14:]
     pieces = ncore * ny
     where = jnp.stack([core, yy]).astype(jnp.int32)
 
@@ -1729,8 +1730,8 @@
     outs = pl.pallas_call(
         partial(unpack_kernel, own, heads),
         grid=(model // L,),
-        in_specs=[row_block(own), row_block(own), row_block(own + L), row_block(256)]
-        + [whole_spec(16, own), whole_spec(8, model)],
+        in_specs=[row_block(own), row_block(own), row_block(own), row_block(256)]
+        + [whole_spec(lines, own), whole_spec(8, model)],
         out_specs=[
             pl.BlockSpec((L, 2, own), lambda d: (d, 0, 0)),
             pl.BlockSpec((own, L), lambda d: (0, d)),

time: 282 us -> 277 us (0.982)
  Pallas kernels: 268 us -> 262 us
    pallas_call x1 -> x0, Pallas kernels: 66.2 us -> none  [body(): pl.pallas_call(partial(tail_kernel, own, ncore, ny, ndp, nloc), in_specs=...]
    pallas_call x1, Pallas kernels: 89 us -> 149 us  [body(): call(partial(scan_kernel, width, own, heads, ncore, ny, ndp, nloc), (nloc...]
where the time goes in v5:
time: 277 us; the launch traced here: 276 us
  Pallas kernels  262 us (95%)
  local copies, waits for them, and re-layouts  11.8 us (4%)
    pallas_call x1, Pallas kernels, body(): call(partial(scan_kernel, width, own, heads, ncore, ny, ndp, nloc), (nloc...  149 us
    pallas_call x1, Pallas kernels, body(): call(partial(forward_kernel, own, heads, ncore, ny, inner_total, nloc), (...  60.5 us
    pallas_call x1, Pallas kernels, body(): call(partial(gate_kernel, width, own, inner_total, ncore, ny), (nloc,), [...  27.2 us
    pallas_call x1, Pallas kernels, body(): call(partial(finish_kernel, pieces, nloc), (pieces, nloc), [placed_spec]...  16.5 us
    pallas_call x1, Pallas kernels, body(): pl.pallas_call(partial(unpack_kernel, own, heads), grid=(model // L,), in...  9.05 us
    slice x1, local copies, waits for them, and re-layouts, body(): wz, wx = (w_zx[:, 0], w_zx[:, 1])  5.6 us

profile of v5, /device:TPU:0, one launch (start us, length us, event | category | flops | bytes accessed | tf_op | source)
XLA Modules:
  0.0 276.0 jit_solution(13026098178277959425)
XLA Ops:
  0.6 5.6 %fusion = (bf16[1024,1,512]{2,1,0:T(2,128)(2,1)S(1)}, bf16[1024,1,512]{2,1,0:T(2,128)(2,1)S(1)}) fusion(bf16[1024,2,512]{2,1,0:T(2,128)(2,1)} %param.17), kind=kLoop, calls=%fused_computation.8 | loop fusion | bytes 4194304 | tf_op jit(solution)/shard_map/slice | solution.py:1389
  6.3 0.0 copy-start.2
  6.3 0.0 copy-start.5
  6.3 0.0 copy-start
  6.3 0.0 copy-start.8
  6.3 0.0 copy-start.6
  6.3 0.0 copy-start.7
  6.3 0.0 copy-start.1
  6.3 0.0 copy-start.3
  6.4 0.0 copy-start.4
  6.4 1.9 copy_bitcast_fusion
  8.3 0.1 pad.12.clone
  8.4 0.0 copy-done.2
  8.4 0.0 copy-done.5
  8.4 0.7 maximum_maximum_fusion.bcp_ref
  9.0 0.0 copy-done
  9.0 0.2 copy.32
  9.2 0.8 pad.8.wdt_ref
  10.0 0.0 copy-done.8
  10.0 0.0 copy-done.6
  10.0 0.0 copy-done.7
  10.0 0.1 broadcast_in_dim.44
  10.1 0.1 broadcast_in_dim_reshape.3
  10.2 0.0 copy-done.1
  10.2 0.0 copy-done.3
  10.2 0.0 copy-done.4
  10.2 1.2 concatenate.6.sm_ref
  11.4 60.5 %forward.1 = (bf16[3,512,1024]{2,1,0:T(8,128)(2,1)}, bf16[3,512,1024]{2,1,0:T(8,128)(2,1)}, f32[3,520,1024]{2,1,0:T(8,128)}, f32[3,520,256]{2,1,0:T(8,128)}, f32...) custom-call(s32[1]{0:T(128)} %constant.34.clone.1._seq, ...), custom_call_target="tpu_custom_call" | custom-call | flops 14092861440 | bytes 40894464 | tf_op jit(solution)/shard_map/forward/pallas_call | solution.py:1409
  72.0 27.2 %gate.1 = (bf16[3,512,1024]{2,1,0:T(8,128)(2,1)}, bf16[3,512,1024]{2,1,0:T(8,128)(2,1)}, bf16[1024,512]{1,0:T(8,128)(2,1)}, bf16[1024,512]{1,0:T(8,128)(2,1)}, f...) custom-call(s32[1]{0:T(128)} %constant.34.clone.1._seq, f32[3,2,512]{2,1,0:T(2,128)} %get-tuple-element.74.st_ref, ...), custom_call_target="tpu_custom_call" | custom-call | flops 6442450944 | bytes 31457280 | tf_op jit(solution)/shard_map/gate/pallas_call | solution.py:1493
  99.2 148.6 %scan_back.1 = (bf16[2,256,1024]{2,1,0:T(8,128)(2,1)}, f32[32,512]{1,0:T(8,128)}, f32[8,1024]{1,0:T(8,128)}, bf16[256,1024]{1,0:T(8,128)(2,1)}, bf16[1024,512]{1...) custom-call(s32[1]{0:T(128)} %constant.34.clone.1._seq, ...), custom_call_target="tpu_custom_call" | custom-call | flops 15300820992 | bytes 25165824 | tf_op jit(solution)/shard_map/scan_back/pallas_call | solution.py:1555
  247.8 9.0 %unpack.1 = (f32[1024,2,512]{2,1,0:T(2,128)}, f32[512,1024]{1,0:T(8,128)}, f32[1024,8]{1,0:T(8,128)}, f32[1024,256]{1,0:T(8,128)}, f32[4,512]{1,0:T(4,128)}, /*i...) custom-call(bf16[1024,512]{1,0:T(8,128)(2,1)} %get-tuple-element.112, ...), custom_call_target="tpu_custom_call" | custom-call | tf_op jit(solution)/shard_map/unpack/pallas_call | solution.py:1730
  256.9 1.8 copy.33
  258.7 0.6 pad_add_fusion._idx
  259.3 16.5 %finish.1 = (f32[6,2,256,1024]{3,2,1,0:T(8,128)}, bf16[6,2,256,1024]{3,2,1,0:T(8,128)(2,1)}) custom-call(s32[2]{0:T(128)} %pad_add_fusion._idx, bf16[6,2,256,1024]{3,2,1,0:T(8,128)(2,1)} %bitcast.35, bf16[2,256,1024]{2,1,0:T(8,128)(2,1)} %get-tuple-element.96.refs_0_, bf16[1,2,256,1024]{3,2,1,0:T(8,128)(2,1)} %get-tuple-element.97.refs_1_, ...), custom_call_target="tpu_custom_call" | custom-call | bytes 37748736 | tf_op jit(solution)/shard_map/finish/pallas_call | solution.py:1715
  (4 shorter events, 0.0 us)
Async XLA Ops:
  6.3 2.1 copy-start.2
  6.3 2.1 copy-start.5
  6.3 2.8 %copy-start = (bf16[1024,8]{0,1:T(8,128)(2,1)S(1)}, bf16[1024,8]{0,1:T(8,128)(2,1)}, u32[]{:S(2)}) copy-start(bf16[1024,8]{0,1:T(8,128)(2,1)} %param.19) | copy-start | bytes 49156
  6.3 3.7 %copy-start.8 = (f32[8]{0:T(128)S(1)}, f32[8]{0:T(128)}, u32[]{:S(2)}) copy-start(f32[8]{0:T(128)} %param.25) | copy-start | bytes 100
  6.3 3.7 %copy-start.6 = (f32[8]{0:T(128)S(1)}, f32[8]{0:T(128)}, u32[]{:S(2)}) copy-start(f32[8]{0:T(128)} %param.24) | copy-start | bytes 100
  6.3 3.7 %copy-start.7 = (f32[8]{0:T(128)S(1)}, f32[8]{0:T(128)}, u32[]{:S(2)}) copy-start(f32[8]{0:T(128)} %param.26) | copy-start | bytes 100
  6.3 3.8 %copy-start.1 = (f32[4,512]{1,0:T(4,128)S(1)}, f32[4,512]{1,0:T(4,128)}, u32[]{:S(2)}) copy-start(f32[4,512]{1,0:T(4,128)} %param.20) | copy-start | bytes 24580
  6.3 3.8 %copy-start.3 = (f32[512]{0:T(512)S(1)}, f32[512]{0:T(512)}, u32[]{:S(2)}) copy-start(f32[512]{0:T(512)} %param.21) | copy-start | bytes 6148
  6.4 3.8 %copy-start.4 = (f32[512]{0:T(512)S(1)}, f32[512]{0:T(512)}, u32[]{:S(2)}) copy-start(f32[512]{0:T(512)} %param.27) | copy-start | bytes 6148

commit v6 on v5

--- a/solution.py
+++ b/solution.py
@@ -723,7 +723,7 @@
 
 def tail_part(own, ncore, ny, ndp, nloc, given, outs, late_to, ready_to, room, machine):
     gw_ref, gbcw_ref, small_ref, other_ref, shared_ref, dh_ref, gain_ref, x_ref, bo_ref = given
-    fw_ref, fb_ref, small_out, shared_out, last_ref = outs
+    fw_ref, fb_ref, fb_scr, small_full, small_src, small_out, shared_out, last_ref = outs
     dh_in, x_own, small_in, core_sems, y_sems, local = room
     model = gw_ref.shape[0]
     Ry = x_own.shape[0]
@@ -738,12 +738,12 @@
     a, b = machine[:per], machine[per : 2 * per]
     per_bc = nbits + len(t_links) + 2
     c = machine[2 * per : 2 * per + per_bc]
-    sm, sh = machine[2 * per + per_bc : 2 * per + per_bc + 3], machine[2 * per + per_bc + 3 :]
+    d, sh = machine[2 * per + per_bc : 3 * per + per_bc], machine[3 * per + per_bc :]
     mid = model // 2
     job_a = Halving(links, mid, gw_ref.at[0:mid], a[0], a[1:-1], fw_ref.at[0:mid], a[-1])
     job_b = Halving(swapped, mid, gw_ref.at[mid:model], b[0], b[1:-1], fw_ref.at[mid:model], b[-1])
-    job_c = Halving(t_links + links, model, gbcw_ref, c[0], c[1:-1], fb_ref, c[-1])
-    job_sm = Doubling(dp_peers, *sm)
+    job_c = Halving(t_links + links, model, gbcw_ref, c[0], c[1:-1], fb_scr, c[-1])
+    job_sm = Halving(links, small_src.shape[0], small_src, d[0], d[1:-1], small_full, d[-1])
     job_sh = Doubling(t_peers + dp_peers, *sh)
 
     def dh_copies():
@@ -762,9 +762,6 @@
     late = Spread(last_ref, *late_to, place)
     ready = [Spread(bo_ref.at[nloc - 1], *ready_to, place)]
     x_copy = pltpu.make_async_copy(x_ref.at[core * nloc + nloc - 1, yy], x_own, local.at[1])
-    start(dh_copies())
-    x_copy.start()
-    yield
 
     def turn(*pairs):
         for job, j in pairs:
@@ -773,22 +770,27 @@
             job.begin(j)
 
     job_sh.acc[0] = shared_ref[...]
-    turn((job_sh, 0), (job_c, 0), (job_a, 0), (job_b, 0))
+    turn((job_c, 0), (job_sh, 0))
+    yield
+    turn((job_c, 1), (job_sh, 1))
+    start(dh_copies())
+    x_copy.start()
+    for spread in ready:
+        start(spread.first())
     if ncore == 2:
         small_copy = remote(other_ref, small_in, core_sems.at[0], core_sems.at[1], twin)
         small_copy.start()
-    turn((job_c, 1), (job_sh, 1))
-    for spread in ready:
-        start(spread.first())
+    yield
+    turn((job_a, 0), (job_b, 0))
     if ncore == 2:
         small_copy.wait()
-        job_sm.acc[0] = small_ref[...] + small_in[...]
+        small_src[...] = small_ref[...] + small_in[...]
     else:
-        job_sm.acc[0] = small_ref[...]
+        small_src[...] = small_ref[...]
     turn((job_sm, 0))
     steps = [
         (job_c, iter(range(2, 2 * job_c.n + 1))),
-        (job_sm, iter(range(1, len(job_sm.peers) + 1))),
+        (job_sm, iter(range(1, 2 * nbits + 1))),
         (job_sh, iter(range(2, len(job_sh.peers) + 1))),
     ]
 
@@ -800,36 +802,36 @@
                 found.append((job, j))
         return found
 
-    turn(*smaller(), (job_a, 1), (job_b, 1))
-    for copy in dh_copies():
-        copy.wait()
-    x_copy.wait()
-
-    @pl.loop(0, Ry // 32)
-    def _(i):
-        rows = pl.ds(pl.multiple_of(i * 32, 32), 32)
-        mine = pl.ds(pl.multiple_of(yy * Ry + i * 32, 32), 32)
-        dh = dh_ref[mine, :].astype(f32)
-        for d in range(ny - 1):
-            dh = dh + dh_in[d, rows, :].astype(f32)
-        last_ref[rows, :] = correction(x_own[rows, :], dh, gain_ref[...]).astype(bf16)
-
-    turn(*smaller())
-    start(late.first())
-    for j in range(2, 2 * nbits + 1):
-        turn(*smaller())
+    for j in range(1, 2 * nbits + 1):
         turn(*smaller(), (job_a, j), (job_b, j))
+        if j == 2:
+            wait(dh_copies())
+            x_copy.wait()
+
+            @pl.loop(0, Ry // 32)
+            def _(i):
+                rows = pl.ds(pl.multiple_of(i * 32, 32), 32)
+                mine = pl.ds(pl.multiple_of(yy * Ry + i * 32, 32), 32)
+                dh = dh_ref[mine, :].astype(f32)
+                for d in range(ny - 1):
+                    dh = dh + dh_in[d, rows, :].astype(f32)
+                last_ref[rows, :] = correction(x_own[rows, :], dh, gain_ref[...]).astype(bf16)
+
+            start(late.first())
     for spread in ready:
         wait(spread.first())
         start(spread.second())
     for _ in range(2 * job_c.n):
         turn(*smaller())
-    small_out[...] = job_sm.acc[len(job_sm.peers)]
+    fb_copy = pltpu.make_async_copy(fb_scr, fb_ref, local.at[1])
+    fb_copy.start()
+    small_out[...] = small_full[...]
     shared_out[...] = job_sh.acc[len(job_sh.peers)]
     wait(late.first())
     start(late.second())
     for spread in ready + [late]:
         wait(spread.second())
+    fb_copy.wait()
     yield
 
 
@@ -922,6 +924,9 @@
     other_ref,
     shared_ref,
     small_in,
+    fb_scr,
+    small_full,
+    small_src,
     end_in,
     x_end,
     core_sems,
@@ -1183,43 +1188,52 @@
             ndp,
             nloc_static,
             (gw_ref, gbcw_ref, small_ref, other_ref, shared_ref, dh_scr, gain_ref, x_ref, bo_ref),
-            (fw_ref, fb_ref, small_out, shared_out, last_ref),
+            (fw_ref, fb_ref, fb_scr, small_full, small_src, small_out, shared_out, last_ref),
             (ly_ref, lt_ref, lty_ref, l_sems),
             (zy_ref, zt_ref, zty_ref, z_sems),
             (end_in, x_end, small_in, core_sems, end_sems, local),
             rest,
         )
+        gbcw_ref[...] = acc_scr[:, width : width + 256].astype(gbcw_ref.dtype)
+        shared_ref[...] = jnp.zeros_like(shared_ref)
+        gpre = jnp.sum(gpre_ref[...], axis=0, keepdims=True) / gain_ref[...]
+        for k in range(model // L):
+            shared_ref[k : k + 1, 0:L] = gpre[:, k * L : k * L + L]
+        for k in range(5):
+            shared_ref[k : k + 1, L : L + 256] = jnp.sum(gbc_ref[k], axis=0, keepdims=True)
         next(end)
         if ncore == 2:
             send_scr[...] = acc_scr[:, own:width].astype(bf16)
             copy = remote(send_scr, recv_scr, core_send, core_recv, twin)
-        gbcw_ref[...] = acc_scr[:, width : width + 256].astype(gbcw_ref.dtype)
-        if ncore == 2:
-            copy.start()
         rows = [jnp.sum(gx_ref[k], axis=0, keepdims=True) for k in range(6)]
         rows.append(jnp.sum(ggg_ref[...], axis=0, keepdims=True))
         dts = [jnp.sum(gdt_ref[k], axis=0, keepdims=True) for k in range(2)]
         small_ref[...] = jnp.zeros_like(small_ref)
         other_ref[...] = jnp.zeros_like(other_ref)
+        lines = 16 + heads * model // own
+
+        def put(ref, k, row):
+            for q in range(own // L):
+                ref[q * lines + k : q * lines + k + 1, :] = row[:, q * L : q * L + L]
+
         for k in range(7):
-            small_ref[k : k + 1, :] = rows[k][:, 0:own]
+            put(small_ref, k, rows[k][:, 0:own])
             if ncore == 2:
-                other_ref[k : k + 1, :] = rows[k][:, own:width]
+                put(other_ref, k, rows[k][:, own:width])
         for d in range(model // L):
             turned = acc_scr[d * L : d * L + L, width + 256 : width + 384].T
-            line, lanes = 16 + heads * (d * L // own), slice(d * L % own, d * L % own + L)
-            small_ref[line : line + heads, lanes] = turned[0:heads]
+            line = (d * L % own) // L * lines + 16 + heads * (d * L // own)
+            small_ref[line : line + heads, :] = turned[0:heads]
             if ncore == 2:
-                other_ref[line : line + heads, lanes] = turned[heads : 2 * heads]
+                other_ref[line : line + heads, :] = turned[heads : 2 * heads]
         for k in range(2):
-            small_ref[7 + k : 8 + k, 0:L] = dts[k]
+            small_ref[7 + k : 8 + k, :] = dts[k]
             if ncore == 2:
                 moved = pltpu.roll(jnp.broadcast_to(dts[k], (8, L)), L - heads, axis=1)
-                other_ref[7 + k : 8 + k, 0:L] = moved[0:1]
-        shared_ref[...] = jnp.zeros_like(shared_ref)
-        shared_ref[0:1, :] = jnp.sum(gpre_ref[...], axis=0, keepdims=True) / gain_ref[...]
-        for k in range(5):
-            shared_ref[k + 1 : k + 2, 0:256] = jnp.sum(gbc_ref[k], axis=0, keepdims=True)
+                other_ref[7 + k : 8 + k, :] = moved[0:1]
+        if ncore == 2:
+            copy.start()
+        next(end)
         for job in jobs:
             job.close(2 * nbits)
         if ncore == 2:
@@ -1266,8 +1280,9 @@
                 bo_ref[...] = src[...]
 
 
-def unpack_kernel(own, heads, gz_ref, go_ref, gw_ref, fb_ref, small_ref, shared_ref, *outs):
+def unpack_kernel(own, heads, gz_total, gz_ref, go_ref, gw_ref, fb_ref, small_ref, shared_ref, *outs):
     gzx_ref, gwo_ref, gwdt_ref, gwbc_ref = outs[:4]
+    lines = 16 + heads * gz_total // own
     gcxw_ref, gcxb_ref, gd_ref, ggg_ref, gdtb_ref, galog_ref, gpre_ref, gcbw_ref, gcbb_ref = outs[4:]
     gzx_ref[:, 0, :] = gz_ref[...].astype(f32)
     gzx_ref[:, 1, :] = gw_ref[:, 0:own].astype(f32)
@@ -1275,8 +1290,8 @@
 
         @pl.when(pl.program_id(0) == d)
         def _(d=d):
-            line = 16 + heads * (d * L // own)
-            rows = small_ref[line : line + heads, d * L % own : d * L % own + L]
+            line = (d * L % own) // L * lines + 16 + heads * (d * L // own)
+            rows = small_ref[line : line + heads, :]
             if heads < 8:
                 rows = jnp.concatenate([rows, jnp.zeros((8 - heads, L), f32)], axis=0)
             gwdt_ref[...] = rows.T[:, 0:heads]
@@ -1288,16 +1303,20 @@
 
     @pl.when(pl.program_id(0) == 0)
     def _():
-        gcxw_ref[...] = small_ref[0:4]
-        gcxb_ref[...] = small_ref[4:5]
-        ggg_ref[...] = small_ref[6:7]
+        pick = (row_iota((L, L)) // HEAD == lane_iota((L, L))).astype(f32)
+        for q in range(own // L):
+            part, cols = small_ref[q * lines : q * lines + 8, :], slice(q * L, q * L + L)
+            gcxw_ref[:, cols] = part[0:4]
+            gcxb_ref[:, cols] = part[4:5]
+            ggg_ref[:, cols] = part[6:7]
+            each = L // HEAD
+            gd_ref[:, q * each : q * each + each] = exact(part, pick)[5:6, 0:each]
         gdtb_ref[...] = small_ref[7:8, 0:heads]
         galog_ref[...] = small_ref[8:9, 0:heads]
-        pick = (row_iota((own, L)) // HEAD == lane_iota((own, L))).astype(f32)
-        gd_ref[...] = exact(small_ref[0:8], pick)[5:6, 0:heads]
-        gpre_ref[...] = shared_ref[0:1]
-        gcbw_ref[...] = shared_ref[1:5, 0:256]
-        gcbb_ref[...] = shared_ref[5:6, 0:256]
+        for k in range(gpre_ref.shape[1] // L):
+            gpre_ref[:, k * L : k * L + L] = shared_ref[k : k + 1, 0:L]
+        gcbw_ref[...] = shared_ref[0:4, L : L + 256]
+        gcbb_ref[...] = shared_ref[4:5, L : L + 256]
 
 
 def seq_spec(*shape):
@@ -1550,6 +1569,7 @@
 
     tbits = log2(nt)
     lines = 16 + heads * model // own
+    srows = max(own // L * lines, 8 * ndp, 128)
     late_shape = sds(nother, Ry, model, dtype=bf16)
     bc_type = bf16 if (model // (nt * ndp)) % 16 == 0 else f32
     s_out = call(
@@ -1581,15 +1601,15 @@
         ],
         [
             whole_spec(nloc - 1, Ry, model),
-            whole_spec(lines, own),
-            whole_spec(8, model),
+            whole_spec(srows, L),
+            whole_spec(model // L, L + 256),
             whole_spec(Ry, model),
         ]
         + [any_spec] * 16,
         [
             sds(nloc - 1, Ry, model, dtype=bf16),
-            sds(lines, own),
-            sds(8, model),
+            sds(srows, L),
+            sds(model // L, L + 256),
             sds(Ry, model, dtype=bf16),
             sds(model, own, dtype=bf16),
             sds(model, own, dtype=bf16),
@@ -1638,10 +1658,13 @@
             dma((2,)),
             pltpu.VMEM((model, own), bf16),
             pltpu.VMEM((model, 256), bc_type),
-            pltpu.VMEM((lines, own), f32),
-            pltpu.VMEM((lines, own), f32),
-            pltpu.VMEM((8, model), f32),
-            pltpu.VMEM((lines, own), f32),
+            pltpu.VMEM((srows, L), f32),
+            pltpu.VMEM((srows, L), f32),
+            pltpu.VMEM((model // L, L + 256), f32),
+            pltpu.VMEM((srows, L), f32),
+            pltpu.VMEM((model, 256), bc_type),
+            pltpu.VMEM((srows, L), f32),
+            pltpu.VMEM((srows, L), f32),
             pltpu.VMEM((nother, Ry, model), bf16),
             pltpu.VMEM((Ry, model), bf16),
             dma((2,)),
@@ -1654,8 +1677,8 @@
         + Halving.scratch(model // 2, own, nbits, bf16)
         + Halving.scratch(model // 2, own, nbits, bf16)
         + Halving.scratch(model, 256, nbits + tbits, bc_type)
-        + Doubling.scratch(nbits, lines, own)
-        + Doubling.scratch(nbits + tbits, 8, model),
+        + Halving.scratch(srows, L, nbits, f32)
+        + Doubling.scratch(nbits + tbits, model // L, L + 256),
         "scan_back",
         2 * nloc * R * model * (2 * wtot),
         nloc * R * (4 * model + 12 * width),
@@ -1728,10 +1751,10 @@
         return pl.BlockSpec((L, cols), lambda d: (d, 0))
 
     outs = pl.pallas_call(
-        partial(unpack_kernel, own, heads),
+        partial(unpack_kernel, own, heads, model),
         grid=(model // L,),
         in_specs=[row_block(own), row_block(own), row_block(own), row_block(256)]
-        + [whole_spec(lines, own), whole_spec(8, model)],
+        + [whole_spec(srows, L), whole_spec(model // L, L + 256)],
         out_specs=[
             pl.BlockSpec((L, 2, own), lambda d: (d, 0, 0)),
             pl.BlockSpec((own, L), lambda d: (0, d)),

time: 277 us -> 270 us (0.975)
  Pallas kernels: 262 us -> 255 us
    pallas_call x1, Pallas kernels: 149 us -> 142 us  [body(): call(partial(scan_kernel, width, own, heads, ncore, ny, ndp, nloc), (nloc...]
where the time goes in v6:
time: 270 us; the launch traced here: 269 us
  Pallas kernels  255 us (94%)
  local copies, waits for them, and re-layouts  11.8 us (4%)
    pallas_call x1, Pallas kernels, body(): call(partial(scan_kernel, width, own, heads, ncore, ny, ndp, nloc), (nloc...  142 us
    pallas_call x1, Pallas kernels, body(): call(partial(forward_kernel, own, heads, ncore, ny, inner_total, nloc), (...  60.5 us
    pallas_call x1, Pallas kernels, body(): call(partial(gate_kernel, width, own, inner_total, ncore, ny), (nloc,), [...  27.2 us
    pallas_call x1, Pallas kernels, body(): call(partial(finish_kernel, pieces, nloc), (pieces, nloc), [placed_spec]...  16.5 us
    pallas_call x1, Pallas kernels, body(): pl.pallas_call(partial(unpack_kernel, own, heads, model), grid=(model //...  8.94 us
    slice x1, local copies, waits for them, and re-layouts, body(): wz, wx = (w_zx[:, 0], w_zx[:, 1])  5.6 us

profile of v6, /device:TPU:0, one launch (start us, length us, event | category | flops | bytes accessed | tf_op | source)
XLA Modules:
  0.0 269.3 jit_solution(2447266146978060380)
XLA Ops:
  0.6 5.6 %fusion = (bf16[1024,1,512]{2,1,0:T(2,128)(2,1)S(1)}, bf16[1024,1,512]{2,1,0:T(2,128)(2,1)S(1)}) fusion(bf16[1024,2,512]{2,1,0:T(2,128)(2,1)} %param.17), kind=kLoop, calls=%fused_computation.8 | loop fusion | bytes 4194304 | tf_op jit(solution)/shard_map/slice | solution.py:1408
  6.3 0.0 copy-start.2
  6.3 0.0 copy-start.5
  6.3 0.0 copy-start
  6.3 0.0 copy-start.8
  6.3 0.0 copy-start.6
  6.3 0.0 copy-start.7
  6.3 0.0 copy-start.1
  6.3 0.0 copy-start.3
  6.4 0.0 copy-start.4
  6.4 1.9 copy_bitcast_fusion
  8.3 0.1 pad.12.clone
  8.4 0.0 copy-done.2
  8.4 0.0 copy-done.5
  8.4 0.7 maximum_maximum_fusion.bcp_ref
  9.0 0.0 copy-done
  9.0 0.2 copy.32
  9.2 0.8 pad.8.wdt_ref
  10.0 0.0 copy-done.8
  10.0 0.0 copy-done.6
  10.0 0.0 copy-done.7
  10.0 0.1 broadcast_in_dim.44
  10.1 0.1 broadcast_in_dim_reshape.3
  10.2 0.0 copy-done.1
  10.2 0.0 copy-done.3
  10.2 0.0 copy-done.4
  10.2 1.2 concatenate.6.sm_ref
  11.4 60.5 %forward.1 = (bf16[3,512,1024]{2,1,0:T(8,128)(2,1)}, bf16[3,512,1024]{2,1,0:T(8,128)(2,1)}, f32[3,520,1024]{2,1,0:T(8,128)}, f32[3,520,256]{2,1,0:T(8,128)}, f32...) custom-call(s32[1]{0:T(128)} %constant.34.clone.1._seq, ...), custom_call_target="tpu_custom_call" | custom-call | flops 14092861440 | bytes 40894464 | tf_op jit(solution)/shard_map/forward/pallas_call | solution.py:1428
  72.0 27.2 %gate.1 = (bf16[3,512,1024]{2,1,0:T(8,128)(2,1)}, bf16[3,512,1024]{2,1,0:T(8,128)(2,1)}, bf16[1024,512]{1,0:T(8,128)(2,1)}, bf16[1024,512]{1,0:T(8,128)(2,1)}, f...) custom-call(s32[1]{0:T(128)} %constant.34.clone.1._seq, f32[3,2,512]{2,1,0:T(2,128)} %get-tuple-element.74.st_ref, ...), custom_call_target="tpu_custom_call" | custom-call | flops 6442450944 | bytes 31457280 | tf_op jit(solution)/shard_map/gate/pallas_call | solution.py:1512
  99.2 142.1 %scan_back.1 = (bf16[2,256,1024]{2,1,0:T(8,128)(2,1)}, f32[128,128]{1,0:T(8,128)}, f32[8,384]{1,0:T(8,128)}, bf16[256,1024]{1,0:T(8,128)(2,1)}, bf16[1024,512]{1...) custom-call(s32[1]{0:T(128)} %constant.34.clone.1._seq, ...), custom_call_target="tpu_custom_call" | custom-call | flops 15300820992 | bytes 25165824 | tf_op jit(solution)/shard_map/scan_back/pallas_call | solution.py:1575
  241.3 8.9 %unpack.1 = (f32[1024,2,512]{2,1,0:T(2,128)}, f32[512,1024]{1,0:T(8,128)}, f32[1024,8]{1,0:T(8,128)}, f32[1024,256]{1,0:T(8,128)}, f32[4,512]{1,0:T(4,128)}, /*i...) custom-call(bf16[1024,512]{1,0:T(8,128)(2,1)} %get-tuple-element.112, ...), custom_call_target="tpu_custom_call" | custom-call | tf_op jit(solution)/shard_map/unpack/pallas_call | solution.py:1753
  250.2 1.8 copy.33
  252.0 0.6 pad_add_fusion._idx
  252.6 16.5 %finish.1 = (f32[6,2,256,1024]{3,2,1,0:T(8,128)}, bf16[6,2,256,1024]{3,2,1,0:T(8,128)(2,1)}) custom-call(s32[2]{0:T(128)} %pad_add_fusion._idx, bf16[6,2,256,1024]{3,2,1,0:T(8,128)(2,1)} %bitcast.35, bf16[2,256,1024]{2,1,0:T(8,128)(2,1)} %get-tuple-element.96.refs_0_, bf16[1,2,256,1024]{3,2,1,0:T(8,128)(2,1)} %get-tuple-element.97.refs_1_, ...), custom_call_target="tpu_custom_call" | custom-call | bytes 37748736 | tf_op jit(solution)/shard_map/finish/pallas_call | solution.py:1738
  (4 shorter events, 0.0 us)
Async XLA Ops:
  6.3 2.1 copy-start.2
  6.3 2.1 copy-start.5
  6.3 2.8 %copy-start = (bf16[1024,8]{0,1:T(8,128)(2,1)S(1)}, bf16[1024,8]{0,1:T(8,128)(2,1)}, u32[]{:S(2)}) copy-start(bf16[1024,8]{0,1:T(8,128)(2,1)} %param.19) | copy-start | bytes 49156
  6.3 3.7 %copy-start.8 = (f32[8]{0:T(128)S(1)}, f32[8]{0:T(128)}, u32[]{:S(2)}) copy-start(f32[8]{0:T(128)} %param.25) | copy-start | bytes 100
  6.3 3.7 %copy-start.6 = (f32[8]{0:T(128)S(1)}, f32[8]{0:T(128)}, u32[]{:S(2)}) copy-start(f32[8]{0:T(128)} %param.24) | copy-start | bytes 100
  6.3 3.7 %copy-start.7 = (f32[8]{0:T(128)S(1)}, f32[8]{0:T(128)}, u32[]{:S(2)}) copy-start(f32[8]{0:T(128)} %param.26) | copy-start | bytes 100
  6.3 3.8 %copy-start.1 = (f32[4,512]{1,0:T(4,128)S(1)}, f32[4,512]{1,0:T(4,128)}, u32[]{:S(2)}) copy-start(f32[4,512]{1,0:T(4,128)} %param.20) | copy-start | bytes 24580
  6.3 3.8 %copy-start.3 = (f32[512]{0:T(512)S(1)}, f32[512]{0:T(512)}, u32[]{:S(2)}) copy-start(f32[512]{0:T(512)} %param.21) | copy-start | bytes 6148
  6.4 3.8 %copy-start.4 = (f32[512]{0:T(512)S(1)}, f32[512]{0:T(512)}, u32[]{:S(2)}) copy-start(f32[512]{0:T(512)} %param.27) | copy-start | bytes 6148

commit v7 on v6

--- a/solution.py
+++ b/solution.py
@@ -598,6 +598,7 @@
     recv_scr,
     po_in,
     x_own,
+    hid_scr,
     st_sems,
     core_send,
     core_recv,
@@ -633,10 +634,13 @@
     def x_copy():
         return pltpu.make_async_copy(x_ref.at[core * nloc + last, yy], x_own, local.at[0])
 
+    def hid_copy():
+        return pltpu.make_async_copy(hid_ref, hid_scr, local.at[1])
+
     @pl.when(here == 0)
     def _():
         greet(peers + ([twin] if ncore == 2 else []))
-        start(row_copies() + po_copies() + [x_copy()])
+        start(row_copies() + po_copies() + [x_copy(), hid_copy()])
         stot_ref[...] = stin_ref[...]
         for i in range(last):
             bo_ref[i] = bo01_ref[i]
@@ -682,7 +686,8 @@
 
     @pl.when(here == last)
     def _():
-        hid = hid_ref.reshape(nloc * rows_all, model)
+        hid_copy().wait()
+        hid = hid_scr.reshape(nloc * rows_all, model)
         dz = dz_scr.reshape(nloc * rows_all, width)
         q = q_scr.reshape(nloc * rows_all, width)
         sc = sc_scr.reshape(nloc * rows_all, model)
@@ -851,10 +856,10 @@
     bcl_ref,
     dtl_ref,
     sin_ref,
-    wz_ref,
-    wzo_ref,
-    wx_ref,
-    wxo_ref,
+    wz_hbm,
+    wzo_hbm,
+    wx_hbm,
+    wxo_hbm,
     wbc_ref,
     wdt_ref,
     prm_ref,
@@ -886,6 +891,11 @@
     zy_ref,
     zt_ref,
     zty_ref,
+    wz_ref,
+    wzo_ref,
+    wx_ref,
+    wxo_ref,
+    w_sems,
     d_scr,
     bcc_scr,
     bca_scr,
@@ -979,8 +989,13 @@
     def x_copy():
         return pltpu.make_async_copy(x_ref.at[core * nloc_static + seq - 1, yy], x_own, local.at[0])
 
+    def weight_copies():
+        both = ((wz_hbm, wz_ref), (wzo_hbm, wzo_ref), (wx_hbm, wx_ref), (wxo_hbm, wxo_ref))
+        return [pltpu.make_async_copy(src, dst, w_sems.at[n]) for n, (src, dst) in enumerate(both)]
+
     @pl.when(step == 0)
     def _():
+        start(weight_copies())
         greet(peers + dp_peers + ([twin] if ncore == 2 else []))
         start(bo_spread.first())
         acc_scr[...] = jnp.zeros_like(acc_scr)
@@ -1164,6 +1179,10 @@
 
     one_chunk()
 
+    @pl.when(step == spans - 1)
+    def _():
+        wait(weight_copies())
+
     @pl.when(back == spans - 1)
     def _():
         @pl.loop(0, model // 256)
@@ -1516,7 +1535,7 @@
             whole_spec(nloc, 2, R),
             whole_spec(nloc, 2, R),
             moved_spec(ncore, nloc, R, model),
-            whole_spec(nloc, R, model),
+            any_spec,
             seq_spec(R, width),
             seq_spec(R, width),
             seq_spec(R, width),
@@ -1551,11 +1570,12 @@
             pltpu.VMEM((model, 2 * own), bf16),
             pltpu.VMEM((nother, Ry, model), bf16),
             pltpu.VMEM((Ry, model), bf16),
+            pltpu.VMEM((nloc, R, model), bf16),
             dma((2, nother)),
             dma,
             dma,
             dma((2, nother)),
-            dma((1,)),
+            dma((2,)),
         ],
         "gate",
         4 * nloc * R * model * width,
@@ -1583,10 +1603,10 @@
             chunk_spec(R + PAD, 256),
             chunk_spec(R, L),
             chunk_spec(spans, L, width),
-            whole_spec(model, own),
-            whole_spec(model, own),
-            whole_spec(model, own),
-            whole_spec(model, own),
+            any_spec,
+            any_spec,
+            any_spec,
+            any_spec,
             whole_spec(model, 256),
             whole_spec(model, L),
             whole_spec(8, width),
@@ -1624,6 +1644,11 @@
         ]
         + [late_shape, sds(Ry, model, dtype=bf16), late_shape] * 2,
         [
+            pltpu.VMEM((model, own), bf16),
+            pltpu.VMEM((model, own), bf16),
+            pltpu.VMEM((model, own), bf16),
+            pltpu.VMEM((model, own), bf16),
+            dma((4,)),
             pltpu.VMEM((R, width + 384), bf16),
             pltpu.VMEM((R, 256), f32),
             pltpu.VMEM((R, 256), bf16),

time: 270 us -> 267 us (0.989)
  no operation moved by 1% of the time
where the time goes in v7:
time: 267 us
  Pallas kernels  253 us (95%)
  local copies, waits for them, and re-layouts  11.8 us (4%)
    pallas_call x1, Pallas kernels, body(): call(partial(scan_kernel, width, own, heads, ncore, ny, ndp, nloc), (nloc...  140 us
    pallas_call x1, Pallas kernels, body(): call(partial(forward_kernel, own, heads, ncore, ny, inner_total, nloc), (...  60.5 us
    pallas_call x1, Pallas kernels, body(): call(partial(gate_kernel, width, own, inner_total, ncore, ny), (nloc,), [...  26.2 us
    pallas_call x1, Pallas kernels, body(): call(partial(finish_kernel, pieces, nloc), (pieces, nloc), [placed_spec]...  16.5 us
    pallas_call x1, Pallas kernels, body(): pl.pallas_call(partial(unpack_kernel, own, heads, model), grid=(model //...  8.94 us
    slice x1, local copies, waits for them, and re-layouts, body(): wz, wx = (w_zx[:, 0], w_zx[:, 1])  5.6 us

profile of v7, /device:TPU:0, one launch (start us, length us, event | category | flops | bytes accessed | tf_op | source)
XLA Modules:
  0.0 266.7 jit_solution(14675955422273978689)
XLA Ops:
  0.6 5.6 %fusion = (bf16[1024,1,512]{2,1,0:T(2,128)(2,1)S(1)}, bf16[1024,1,512]{2,1,0:T(2,128)(2,1)S(1)}) fusion(bf16[1024,2,512]{2,1,0:T(2,128)(2,1)} %param.17), kind=kLoop, calls=%fused_computation.8 | loop fusion | bytes 4194304 | tf_op jit(solution)/shard_map/slice | solution.py:1427
  6.3 0.0 copy-start.2
  6.3 0.0 copy-start.5
  6.3 0.0 copy-start
  6.3 0.0 copy-start.8
  6.3 0.0 copy-start.6
  6.3 0.0 copy-start.7
  6.3 0.0 copy-start.1
  6.3 0.0 copy-start.3
  6.4 0.0 copy-start.4
  6.4 1.9 copy_bitcast_fusion
  8.3 0.1 pad.12.clone
  8.4 0.0 copy-done.2
  8.4 0.0 copy-done.5
  8.4 0.7 maximum_maximum_fusion.bcp_ref
  9.0 0.0 copy-done
  9.0 0.2 copy.32
  9.2 0.8 pad.8.wdt_ref
  10.0 0.0 copy-done.8
  10.0 0.0 copy-done.6
  10.0 0.0 copy-done.7
  10.0 0.1 broadcast_in_dim.44
  10.1 0.1 broadcast_in_dim_reshape.3
  10.2 0.0 copy-done.1
  10.2 0.0 copy-done.3
  10.2 0.0 copy-done.4
  10.2 1.2 concatenate.6.sm_ref
  11.4 60.5 %forward.1 = (bf16[3,512,1024]{2,1,0:T(8,128)(2,1)}, bf16[3,512,1024]{2,1,0:T(8,128)(2,1)}, f32[3,520,1024]{2,1,0:T(8,128)}, f32[3,520,256]{2,1,0:T(8,128)}, f32...) custom-call(s32[1]{0:T(128)} %constant.34.clone.1._seq, ...), custom_call_target="tpu_custom_call" | custom-call | flops 14092861440 | bytes 40894464 | tf_op jit(solution)/shard_map/forward/pallas_call | solution.py:1447
  72.0 26.2 %gate.1 = (bf16[3,512,1024]{2,1,0:T(8,128)(2,1)}, bf16[3,512,1024]{2,1,0:T(8,128)(2,1)}, bf16[1024,512]{1,0:T(8,128)(2,1)}, bf16[1024,512]{1,0:T(8,128)(2,1)}, f...) custom-call(s32[1]{0:T(128)} %constant.34.clone.1._seq, f32[3,2,512]{2,1,0:T(2,128)} %get-tuple-element.74.st_ref, ...), custom_call_target="tpu_custom_call" | custom-call | flops 6442450944 | bytes 31457280 | tf_op jit(solution)/shard_map/gate/pallas_call | solution.py:1531
  98.2 140.5 %scan_back.1 = (bf16[2,256,1024]{2,1,0:T(8,128)(2,1)}, f32[128,128]{1,0:T(8,128)}, f32[8,384]{1,0:T(8,128)}, bf16[256,1024]{1,0:T(8,128)(2,1)}, bf16[1024,512]{1...) custom-call(s32[1]{0:T(128)} %constant.34.clone.1._seq, ...), custom_call_target="tpu_custom_call" | custom-call | flops 15300820992 | bytes 25165824 | tf_op jit(solution)/shard_map/scan_back/pallas_call | solution.py:1595
  238.7 8.9 %unpack.1 = (f32[1024,2,512]{2,1,0:T(2,128)}, f32[512,1024]{1,0:T(8,128)}, f32[1024,8]{1,0:T(8,128)}, f32[1024,256]{1,0:T(8,128)}, f32[4,512]{1,0:T(4,128)}, /*i...) custom-call(bf16[1024,512]{1,0:T(8,128)(2,1)} %get-tuple-element.112, ...), custom_call_target="tpu_custom_call" | custom-call | tf_op jit(solution)/shard_map/unpack/pallas_call | solution.py:1778
  247.6 1.8 copy.33
  249.5 0.6 pad_add_fusion._idx
  250.0 16.5 %finish.1 = (f32[6,2,256,1024]{3,2,1,0:T(8,128)}, bf16[6,2,256,1024]{3,2,1,0:T(8,128)(2,1)}) custom-call(s32[2]{0:T(128)} %pad_add_fusion._idx, bf16[6,2,256,1024]{3,2,1,0:T(8,128)(2,1)} %bitcast.35, bf16[2,256,1024]{2,1,0:T(8,128)(2,1)} %get-tuple-element.96.refs_0_, bf16[1,2,256,1024]{3,2,1,0:T(8,128)(2,1)} %get-tuple-element.97.refs_1_, ...), custom_call_target="tpu_custom_call" | custom-call | bytes 37748736 | tf_op jit(solution)/shard_map/finish/pallas_call | solution.py:1763
  (4 shorter events, 0.0 us)
Async XLA Ops:
  6.3 2.1 copy-start.2
  6.3 2.1 copy-start.5
  6.3 2.8 %copy-start = (bf16[1024,8]{0,1:T(8,128)(2,1)S(1)}, bf16[1024,8]{0,1:T(8,128)(2,1)}, u32[]{:S(2)}) copy-start(bf16[1024,8]{0,1:T(8,128)(2,1)} %param.19) | copy-start | bytes 49156
  6.3 3.7 %copy-start.8 = (f32[8]{0:T(128)S(1)}, f32[8]{0:T(128)}, u32[]{:S(2)}) copy-start(f32[8]{0:T(128)} %param.25) | copy-start | bytes 100
  6.3 3.7 %copy-start.6 = (f32[8]{0:T(128)S(1)}, f32[8]{0:T(128)}, u32[]{:S(2)}) copy-start(f32[8]{0:T(128)} %param.24) | copy-start | bytes 100
  6.3 3.7 %copy-start.7 = (f32[8]{0:T(128)S(1)}, f32[8]{0:T(128)}, u32[]{:S(2)}) copy-start(f32[8]{0:T(128)} %param.26) | copy-start | bytes 100
  6.3 3.8 %copy-start.1 = (f32[4,512]{1,0:T(4,128)S(1)}, f32[4,512]{1,0:T(4,128)}, u32[]{:S(2)}) copy-start(f32[4,512]{1,0:T(4,128)} %param.20) | copy-start | bytes 24580
  6.3 3.8 %copy-start.3 = (f32[512]{0:T(512)S(1)}, f32[512]{0:T(512)}, u32[]{:S(2)}) copy-start(f32[512]{0:T(512)} %param.21) | copy-start | bytes 6148
  6.4 3.8 %copy-start.4 = (f32[512]{0:T(512)S(1)}, f32[512]{0:T(512)}, u32[]{:S(2)}) copy-start(f32[512]{0:T(512)} %param.27) | copy-start | bytes 6148
